TPU v7x, 256 devices: a whole 4x4x8 slice. The times are simulated.
256 devices in a mesh: rep: 2 (over core), dp: 128 (over x, y, z).
Axes of the slice: x: 4, y: 4, z: 8, core: 2. Of those that a mesh axis runs over, the one named last changes fastest.
Arguments:
- x: bfloat16 [256, 2048, 896], P(('rep', 'dp')), parts along dimension 0
- dy: bfloat16 [256, 2048, 896], P(('rep', 'dp')), parts along dimension 0
- w_gate: bfloat16 [2, 896, 2560], replicated
- w_up: bfloat16 [2, 896, 2560], replicated
- w_down: bfloat16 [2, 2560, 896], replicated
- m_w_gate: float32 [2, 896, 2560], P(None, 'dp')
- m_w_up: float32 [2, 896, 2560], P(None, 'dp')
- m_w_down: float32 [2, 2560, 896], P(None, 'dp')
- v_w_gate: float32 [2, 896, 2560], P(None, 'dp')
- v_w_up: float32 [2, 896, 2560], P(None, 'dp')
- v_w_down: float32 [2, 2560, 896], P(None, 'dp')
Outputs:
- output 1: bfloat16 [4, 896, 2560], P('rep'), parts along dimension 0
- output 2: bfloat16 [4, 896, 2560], P('rep'), parts along dimension 0
- output 3: bfloat16 [4, 2560, 896], P('rep'), parts along dimension 0
- output 4: float32 [4, 896, 2560], P('rep', 'dp'), parts along dimension 0
- output 5: float32 [4, 896, 2560], P('rep', 'dp'), parts along dimension 0
- output 6: float32 [4, 2560, 896], P('rep', 'dp'), parts along dimension 0
- output 7: float32 [4, 896, 2560], P('rep', 'dp'), parts along dimension 0
- output 8: float32 [4, 896, 2560], P('rep', 'dp'), parts along dimension 0
- output 9: float32 [4, 2560, 896], P('rep', 'dp'), parts along dimension 0
There are 2 independent parts. A program takes and returns all parts, laid end to end along the dimension named above; an argument that names none is the same for every part.
All inputs are finite; a program needn't handle non-finite values.
Results may differ from a plain program's by a relative error of at most 0.022.
Values are sent between devices in bfloat16 or wider.
A program may use at most 768 MiB of HBM per device.

v0:
```python
import jax
import jax.numpy as jnp
from jax import lax

NAMES = ("w_gate", "w_up", "w_down")


def matmul(a, w):
    return jnp.dot(a, w, preferred_element_type=jnp.float32).astype(jnp.bfloat16)


def normed(h):
    wide = h.astype(jnp.float32)
    scale = lax.rsqrt(jnp.mean(wide**2, -1, keepdims=True) + 1e-6)
    return (wide * scale).astype(jnp.bfloat16)


def layer(h, w):
    a = normed(h)
    gate = jnp.dot(a, w["w_gate"], preferred_element_type=jnp.float32)
    up = jnp.dot(a, w["w_up"], preferred_element_type=jnp.float32)
    return h + matmul((jax.nn.silu(gate) * up).astype(jnp.bfloat16), w["w_down"])


def adamw(w, m, v, g):
    m = 0.9 * m + 0.1 * g
    v = 0.95 * v + 0.05 * g * g
    step = m * lax.rsqrt(v + 1e-8) + 0.1 * w
    return (w - 0.02 * step).astype(jnp.bfloat16), m, v


def clipped(gradients, sum_of_squares, count):
    factor = jnp.minimum(1.0, 0.5 * lax.rsqrt(sum_of_squares / count + 1e-30))
    return [g * factor for g in gradients]


def stack(weights, h):
    for number in range(weights["w_gate"].shape[0]):
        h = layer(h, {name: w[number] for name, w in weights.items()})
    return h


def solution(mesh):
    groups = mesh.shape["rep"]

    def step(x, dy, *arrays):
        weights, m, v = (arrays[i : i + 3] for i in (0, 3, 6))
        x, dy = (t.reshape(groups, -1, *t.shape[1:]) for t in (x, dy))

        def of_a_group(x, dy):
            _, back = jax.vjp(lambda w: stack(w, x), dict(zip(NAMES, weights, strict=True)))
            by_weights = back(dy)[0]
            gradients = [by_weights[name].astype(jnp.float32) for name in NAMES]
            gradients = clipped(gradients, sum(jnp.sum(g * g) for g in gradients), sum(g.size for g in gradients))
            new = [adamw(w.astype(jnp.float32), m, v, g) for w, m, v, g in zip(weights, m, v, gradients, strict=True)]
            return tuple(one[which] for which in range(3) for one in new)

        return tuple(t.reshape(-1, *t.shape[2:]) for t in jax.vmap(of_a_group)(x, dy))

    return step
```

profile of v0, /device:TPU:8, one launch (start us, length us, event | category | flops | bytes accessed | tf_op | source)
XLA Modules:
  0.0 2669.7 jit_solution(1145380381384999662)
XLA Ops:
  10.0 6.1 copy.15
  16.1 14.2 fusion.71
  30.3 22.5 fusion.69
  52.8 15.3 fusion.30
  68.1 15.1 fusion.43
  83.3 18.4 fusion.60
  101.7 17.7 fusion.63
  119.4 15.6 convolution_convert_fusion.1
  141.1 24.0 fusion.10
  165.1 15.3 fusion.58
  180.4 19.1 fusion.45
  206.8 15.8 convolution_convert_fusion
  222.6 19.2 fusion.55
  241.8 26.5 fusion.52
  268.4 15.6 convolution_bitcast_fusion.1
  284.0 19.7 fusion.49
  303.7 505.4 %fusion.147 = (f32[8,2560]{1,0:T(8,128)S(1)}, f32[8,2560]{1,0:T(8,128)S(1)}, f32[8,2560]{1,0:T(8,128)S(1)}, f32[8,2560]{1,0:T(8,128)S(1)}) fusion(f32[1,896,2560]{2,1,0:T(8,128)} %fusion.52, f32[1,896,2560]{2,1,0:T(8,128)} %convolution_bitcast_fusion.1, f32[1,896,2560]{2,1,0:T(8,128)} %fusion.55, f32[1,896,2560]{2,1,0:T(8,128)} %fusion.49), kind=kCustom, calls=%all-reduce-scatter.4 | all-reduce-scatter fusion | flops 10485761 | bytes 37028864
  820.2 28.2 %collective-permute-start.35 = (bf16[8,2560]{1,0:T(8,128)(2,1)S(1)}, bf16[8,2560]{1,0:T(8,128)(2,1)S(1)}, u32[]{:S(2)}, u32[]{:S(2)}) collective-permute-start(bf16[8,2560]{1,0:T(8,128)(2,1)S(1)} %convert.164), channel_id=1, source_target_pairs={{0,4},{1,5},{2,6},{3,7},{4,8},{5,9},{6,10},{7,11},{8,12},{9,13},{1... | collective-permute-start | bytes 122888
  859.5 21.7 collective-permute-start.41
  942.4 22.3 fusion.46
  979.5 17.1 convolution_bitcast_fusion
  1012.4 793.8 %all-reduce.24 = (bf16[1,2560,896]{2,1,0:T(8,128)(2,1)}, bf16[1,2560,896]{2,1,0:T(8,128)(2,1)}) all-reduce(f32[1,2560,896]{2,1,0:T(8,128)} %convolution_bitcast_fusion, f32[1,2560,896]{2,1,0:T(8,128)} %fusion.46), channel_id=21, replica_groups=[2,128]<=[256], use_global_device_ids=true, to_apply=%add.5.clone.clone | all-reduce | flops 4587520 | bytes 27525120
  1853.4 10.2 concatenate
  1863.6 15.6 collective-permute-start.26
  1879.2 35.1 %collective-permute-start.27 = (bf16[8,2560]{1,0:T(8,128)(2,1)}, bf16[8,2560]{1,0:T(8,128)(2,1)S(1)}, u32[]{:S(2)}, u32[]{:S(2)}) collective-permute-start(bf16[8,2560]{1,0:T(8,128)(2,1)} %convert.167), channel_id=1, source_target_pairs={{0,12},{1,13},{2,14},{3,15},{4,16},{5,17},{6,18},{7,19},{8,20},{9,... | collective-permute-start | bytes 122888
  1933.0 326.3 %all-reduce.10 = f32[1]{0:T(128)} all-reduce(f32[1]{0:T(128)} %bitcast.50), channel_id=3, replica_groups=mesh['rep'=2,'dp'=128] {'dp'}, use_global_device_ids=true, to_apply=%region_3.4.clone | all-reduce | flops 1 | bytes 8 | tf_op jit(solution)/vmap()/reduce_sum | solution.py:54
  2270.3 129.7 %all-gather.14.cloned.1.call-done = bf16[1,2,2560,896]{3,1,0,2:T(2,128)(2,1)} async-done(((bf16[1,2,20,896]{3,1,0,2:T(2,128)(2,1)}), bf16[1,2,2560,896]{3,1,0,2:T(2,128)(2,1)}) %all-gather.14.cloned.1.call-update) | async-done | bytes 9175056 | tf_op jit(solution)/reshape | solution.py:58
  2400.0 8.5 copy.27
  2408.4 118.6 %all-gather.12.cloned.1.call-done = bf16[1,2,896,2560]{3,1,0,2:T(2,128)(2,1)} async-done(((bf16[1,2,7,2560]{3,1,0,2:T(2,128)(2,1)}), bf16[1,2,896,2560]{3,1,0,2:T(2,128)(2,1)}) %all-gather.12.cloned.1.call-update) | async-done | bytes 9175056 | tf_op jit(solution)/reshape | solution.py:58
  2527.0 8.7 copy.26
  2535.7 118.4 %all-gather.10.cloned.1.call-done = bf16[1,2,896,2560]{3,1,0,2:T(2,128)(2,1)} async-done(((bf16[1,2,7,2560]{3,1,0,2:T(2,128)(2,1)}), bf16[1,2,896,2560]{3,1,0,2:T(2,128)(2,1)}) %all-gather.10.cloned.1.call-update) | async-done | bytes 9175056 | tf_op jit(solution)/reshape | solution.py:58
  2654.1 8.7 copy.25
  (221 shorter events, 201.3 us)
Async XLA Ops:
  7.2 2392.8 %all-gather.14.cloned.1.call-start = ((), (), s32[]{:S(2)}) async-start(), calls=%async_computation.2 | async-start | bytes 9246720 | tf_op jit(solution)/reshape | solution.py:58
  813.1 35.3 %collective-permute-start.31 = (bf16[7,2560]{1,0:T(8,128)(2,1)S(1)}, bf16[7,2560]{1,0:T(8,128)(2,1)S(1)}, u32[]{:S(2)}, u32[]{:S(2)}) collective-permute-start(bf16[7,2560]{1,0:T(8,128)(2,1)S(1)} %slice.25), channel_id=1, source_target_pairs={{0,16},{1,17},{2,18},{3,19},{4,20},{5,21},{6,22},{7,23},{8,24},{9,... | collective-permute-start | bytes 107528
  814.4 36.0 %collective-permute-start.32 = (bf16[8,2560]{1,0:T(8,128)(2,1)S(1)}, bf16[8,2560]{1,0:T(8,128)(2,1)S(1)}, u32[]{:S(2)}, u32[]{:S(2)}) collective-permute-start(bf16[8,2560]{1,0:T(8,128)(2,1)S(1)} %convert.164), channel_id=1, source_target_pairs={{0,1},{1,2},{2,3},{3,4},{4,5},{5,6},{6,7},{7,8},{8,9},{9,10},{10,1... | collective-permute-start | bytes 122888
  816.3 36.0 %collective-permute-start.33 = (bf16[8,2560]{1,0:T(8,128)(2,1)S(1)}, bf16[8,2560]{1,0:T(8,128)(2,1)S(1)}, u32[]{:S(2)}, u32[]{:S(2)}) collective-permute-start(bf16[8,2560]{1,0:T(8,128)(2,1)S(1)} %convert.164), channel_id=1, source_target_pairs={{0,2},{1,3},{2,4},{3,5},{4,6},{5,7},{6,8},{7,9},{8,10},{9,11},{10,... | collective-permute-start | bytes 122888
  818.2 36.0 %collective-permute-start.34 = (bf16[8,2560]{1,0:T(8,128)(2,1)S(1)}, bf16[8,2560]{1,0:T(8,128)(2,1)S(1)}, u32[]{:S(2)}, u32[]{:S(2)}) collective-permute-start(bf16[8,2560]{1,0:T(8,128)(2,1)S(1)} %convert.164), channel_id=1, source_target_pairs={{0,3},{1,4},{2,5},{3,6},{4,7},{5,8},{6,9},{7,10},{8,11},{9,12},{10... | collective-permute-start | bytes 122888
  820.2 36.0 %collective-permute-start.35 = (bf16[8,2560]{1,0:T(8,128)(2,1)S(1)}, bf16[8,2560]{1,0:T(8,128)(2,1)S(1)}, u32[]{:S(2)}, u32[]{:S(2)}) collective-permute-start(bf16[8,2560]{1,0:T(8,128)(2,1)S(1)} %convert.164), channel_id=1, source_target_pairs={{0,4},{1,5},{2,6},{3,7},{4,8},{5,9},{6,10},{7,11},{8,12},{9,13},{1... | collective-permute-start | bytes 122888
  850.3 30.9 %collective-permute-start.37 = (bf16[8,2560]{1,0:T(8,128)(2,1)S(1)}, bf16[8,2560]{1,0:T(8,128)(2,1)S(1)}, u32[]{:S(2)}, u32[]{:S(2)}) collective-permute-start(bf16[8,2560]{1,0:T(8,128)(2,1)S(1)} %convert.164), channel_id=1, source_target_pairs={{0,6},{1,7},{2,8},{3,9},{4,10},{5,11},{6,12},{7,13},{8,14},{9,15},... | collective-permute-start | bytes 122888
  852.3 31.5 %collective-permute-start.38 = (bf16[8,2560]{1,0:T(8,128)(2,1)S(1)}, bf16[8,2560]{1,0:T(8,128)(2,1)S(1)}, u32[]{:S(2)}, u32[]{:S(2)}) collective-permute-start(bf16[8,2560]{1,0:T(8,128)(2,1)S(1)} %convert.164), channel_id=1, source_target_pairs={{0,7},{1,8},{2,9},{3,10},{4,11},{5,12},{6,13},{7,14},{8,15},{9,16}... | collective-permute-start | bytes 122888
  854.2 34.8 %collective-permute-start.39 = (bf16[8,2560]{1,0:T(8,128)(2,1)S(1)}, bf16[8,2560]{1,0:T(8,128)(2,1)S(1)}, u32[]{:S(2)}, u32[]{:S(2)}) collective-permute-start(bf16[8,2560]{1,0:T(8,128)(2,1)S(1)} %convert.164), channel_id=1, source_target_pairs={{0,8},{1,9},{2,10},{3,11},{4,12},{5,13},{6,14},{7,15},{8,16},{9,17... | collective-permute-start | bytes 122888
  856.1 34.8 %collective-permute-start.40 = (bf16[8,2560]{1,0:T(8,128)(2,1)S(1)}, bf16[8,2560]{1,0:T(8,128)(2,1)S(1)}, u32[]{:S(2)}, u32[]{:S(2)}) collective-permute-start(bf16[8,2560]{1,0:T(8,128)(2,1)S(1)} %convert.164), channel_id=1, source_target_pairs={{0,9},{1,10},{2,11},{3,12},{4,13},{5,14},{6,15},{7,16},{8,17},{9,1... | collective-permute-start | bytes 122888
  859.5 37.0 %collective-permute-start.41 = (bf16[8,2560]{1,0:T(8,128)(2,1)S(1)}, bf16[8,2560]{1,0:T(8,128)(2,1)S(1)}, u32[]{:S(2)}, u32[]{:S(2)}) collective-permute-start(bf16[8,2560]{1,0:T(8,128)(2,1)S(1)} %convert.164), channel_id=1, source_target_pairs={{0,10},{1,11},{2,12},{3,13},{4,14},{5,15},{6,16},{7,17},{8,18},{9,... | collective-permute-start | bytes 122888
  929.1 36.2 %collective-permute-start.58 = (bf16[8,2560]{1,0:T(8,128)(2,1)S(1)}, bf16[8,2560]{1,0:T(8,128)(2,1)S(1)}, u32[]{:S(2)}, u32[]{:S(2)}) collective-permute-start(bf16[8,2560]{1,0:T(8,128)(2,1)S(1)} %convert.165), channel_id=1, source_target_pairs={{0,11},{1,12},{2,13},{3,14},{4,15},{5,16},{6,17},{7,18},{8,19},{9,... | collective-permute-start | bytes 122888
  932.4 35.7 %collective-permute-start.59 = (bf16[8,2560]{1,0:T(8,128)(2,1)S(1)}, bf16[8,2560]{1,0:T(8,128)(2,1)S(1)}, u32[]{:S(2)}, u32[]{:S(2)}) collective-permute-start(bf16[8,2560]{1,0:T(8,128)(2,1)S(1)} %convert.165), channel_id=1, source_target_pairs={{0,12},{1,13},{2,14},{3,15},{4,16},{5,17},{6,18},{7,19},{8,20},{9,... | collective-permute-start | bytes 122888
  937.2 34.0 %collective-permute-start.60 = (bf16[8,2560]{1,0:T(8,128)(2,1)S(1)}, bf16[8,2560]{1,0:T(8,128)(2,1)S(1)}, u32[]{:S(2)}, u32[]{:S(2)}) collective-permute-start(bf16[8,2560]{1,0:T(8,128)(2,1)S(1)} %convert.165), channel_id=1, source_target_pairs={{0,13},{1,14},{2,15},{3,16},{4,17},{5,18},{6,19},{7,20},{8,21},{9,... | collective-permute-start | bytes 122888
  938.5 36.1 %collective-permute-start.61 = (bf16[8,2560]{1,0:T(8,128)(2,1)S(1)}, bf16[8,2560]{1,0:T(8,128)(2,1)S(1)}, u32[]{:S(2)}, u32[]{:S(2)}) collective-permute-start(bf16[8,2560]{1,0:T(8,128)(2,1)S(1)} %convert.165), channel_id=1, source_target_pairs={{0,14},{1,15},{2,16},{3,17},{4,18},{5,19},{6,20},{7,21},{8,22},{9,... | collective-permute-start | bytes 122888
  941.1 37.0 %collective-permute-start.62 = (bf16[8,2560]{1,0:T(8,128)(2,1)S(1)}, bf16[8,2560]{1,0:T(8,128)(2,1)S(1)}, u32[]{:S(2)}, u32[]{:S(2)}) collective-permute-start(bf16[8,2560]{1,0:T(8,128)(2,1)S(1)} %convert.165), channel_id=1, source_target_pairs={{0,15},{1,16},{2,17},{3,18},{4,19},{5,20},{6,21},{7,22},{8,23},{9,... | collective-permute-start | bytes 122888
  965.3 31.4 %collective-permute-start = (bf16[8,2560]{1,0:T(8,128)(2,1)}, bf16[8,2560]{1,0:T(8,128)(2,1)S(1)}, u32[]{:S(2)}, u32[]{:S(2)}) collective-permute-start(bf16[8,2560]{1,0:T(8,128)(2,1)} %convert.166), channel_id=1, source_target_pairs={{0,1},{1,2},{2,3},{3,4},{4,5},{5,6},{6,7},{7,8},{8,9},{9,10},{10,1... | collective-permute-start | bytes 122888
  968.2 30.2 %collective-permute-start.1 = (bf16[8,2560]{1,0:T(8,128)(2,1)}, bf16[8,2560]{1,0:T(8,128)(2,1)S(1)}, u32[]{:S(2)}, u32[]{:S(2)}) collective-permute-start(bf16[8,2560]{1,0:T(8,128)(2,1)} %convert.166), channel_id=1, source_target_pairs={{0,2},{1,3},{2,4},{3,5},{4,6},{5,7},{6,8},{7,9},{8,10},{9,11},{10,... | collective-permute-start | bytes 122888
  978.1 31.0 %collective-permute-start.12 = (bf16[8,2560]{1,0:T(8,128)(2,1)}, bf16[8,2560]{1,0:T(8,128)(2,1)S(1)}, u32[]{:S(2)}, u32[]{:S(2)}) collective-permute-start(bf16[8,2560]{1,0:T(8,128)(2,1)} %convert.166), channel_id=1, source_target_pairs={{0,13},{1,14},{2,15},{3,16},{4,17},{5,18},{6,19},{7,20},{8,21},{9,... | collective-permute-start | bytes 122888
  996.7 810.8 %collective-permute-start.13 = (bf16[8,2560]{1,0:T(8,128)(2,1)}, bf16[8,2560]{1,0:T(8,128)(2,1)S(1)}, u32[]{:S(2)}, u32[]{:S(2)}) collective-permute-start(bf16[8,2560]{1,0:T(8,128)(2,1)} %convert.166), channel_id=1, source_target_pairs={{0,14},{1,15},{2,16},{3,17},{4,18},{5,19},{6,20},{7,21},{8,22},{9,... | collective-permute-start | bytes 122888
  998.4 811.0 %collective-permute-start.14 = (bf16[8,2560]{1,0:T(8,128)(2,1)}, bf16[8,2560]{1,0:T(8,128)(2,1)S(1)}, u32[]{:S(2)}, u32[]{:S(2)}) collective-permute-start(bf16[8,2560]{1,0:T(8,128)(2,1)} %convert.166), channel_id=1, source_target_pairs={{0,15},{1,16},{2,17},{3,18},{4,19},{5,20},{6,21},{7,22},{8,23},{9,... | collective-permute-start | bytes 122888
  999.8 811.6 %collective-permute-start.2 = (bf16[8,2560]{1,0:T(8,128)(2,1)}, bf16[8,2560]{1,0:T(8,128)(2,1)S(1)}, u32[]{:S(2)}, u32[]{:S(2)}) collective-permute-start(bf16[8,2560]{1,0:T(8,128)(2,1)} %convert.166), channel_id=1, source_target_pairs={{0,3},{1,4},{2,5},{3,6},{4,7},{5,8},{6,9},{7,10},{8,11},{9,12},{10... | collective-permute-start | bytes 122888
  1003.2 810.1 %collective-permute-start.3 = (bf16[8,2560]{1,0:T(8,128)(2,1)}, bf16[8,2560]{1,0:T(8,128)(2,1)S(1)}, u32[]{:S(2)}, u32[]{:S(2)}) collective-permute-start(bf16[8,2560]{1,0:T(8,128)(2,1)} %convert.166), channel_id=1, source_target_pairs={{0,4},{1,5},{2,6},{3,7},{4,8},{5,9},{6,10},{7,11},{8,12},{9,13},{1... | collective-permute-start | bytes 122888
  1009.1 806.2 %collective-permute-start.4 = (bf16[8,2560]{1,0:T(8,128)(2,1)}, bf16[8,2560]{1,0:T(8,128)(2,1)S(1)}, u32[]{:S(2)}, u32[]{:S(2)}) collective-permute-start(bf16[8,2560]{1,0:T(8,128)(2,1)} %convert.166), channel_id=1, source_target_pairs={{0,5},{1,6},{2,7},{3,8},{4,9},{5,10},{6,11},{7,12},{8,13},{9,14},{... | collective-permute-start | bytes 122888
  1846.8 32.4 %collective-permute-start.22 = (bf16[8,2560]{1,0:T(8,128)(2,1)}, bf16[8,2560]{1,0:T(8,128)(2,1)S(1)}, u32[]{:S(2)}, u32[]{:S(2)}) collective-permute-start(bf16[8,2560]{1,0:T(8,128)(2,1)} %convert.167), channel_id=1, source_target_pairs={{0,7},{1,8},{2,9},{3,10},{4,11},{5,12},{6,13},{7,14},{8,15},{9,16}... | collective-permute-start | bytes 122888
  1848.8 65.6 %collective-permute-start.23 = (bf16[8,2560]{1,0:T(8,128)(2,1)}, bf16[8,2560]{1,0:T(8,128)(2,1)S(1)}, u32[]{:S(2)}, u32[]{:S(2)}) collective-permute-start(bf16[8,2560]{1,0:T(8,128)(2,1)} %convert.167), channel_id=1, source_target_pairs={{0,8},{1,9},{2,10},{3,11},{4,12},{5,13},{6,14},{7,15},{8,16},{9,17... | collective-permute-start | bytes 122888
  1850.7 69.1 %collective-permute-start.24 = (bf16[8,2560]{1,0:T(8,128)(2,1)}, bf16[8,2560]{1,0:T(8,128)(2,1)S(1)}, u32[]{:S(2)}, u32[]{:S(2)}) collective-permute-start(bf16[8,2560]{1,0:T(8,128)(2,1)} %convert.167), channel_id=1, source_target_pairs={{0,9},{1,10},{2,11},{3,12},{4,13},{5,14},{6,15},{7,16},{8,17},{9,1... | collective-permute-start | bytes 122888
  1852.0 72.8 %collective-permute-start.25 = (bf16[8,2560]{1,0:T(8,128)(2,1)}, bf16[8,2560]{1,0:T(8,128)(2,1)S(1)}, u32[]{:S(2)}, u32[]{:S(2)}) collective-permute-start(bf16[8,2560]{1,0:T(8,128)(2,1)} %convert.167), channel_id=1, source_target_pairs={{0,10},{1,11},{2,12},{3,13},{4,14},{5,15},{6,16},{7,17},{8,18},{9,... | collective-permute-start | bytes 122888
  1863.6 62.6 %collective-permute-start.26 = (bf16[8,2560]{1,0:T(8,128)(2,1)}, bf16[8,2560]{1,0:T(8,128)(2,1)S(1)}, u32[]{:S(2)}, u32[]{:S(2)}) collective-permute-start(bf16[8,2560]{1,0:T(8,128)(2,1)} %convert.167), channel_id=1, source_target_pairs={{0,11},{1,12},{2,13},{3,14},{4,15},{5,16},{6,17},{7,18},{8,19},{9,... | collective-permute-start | bytes 122888
  1879.2 46.9 %collective-permute-start.27 = (bf16[8,2560]{1,0:T(8,128)(2,1)}, bf16[8,2560]{1,0:T(8,128)(2,1)S(1)}, u32[]{:S(2)}, u32[]{:S(2)}) collective-permute-start(bf16[8,2560]{1,0:T(8,128)(2,1)} %convert.167), channel_id=1, source_target_pairs={{0,12},{1,13},{2,14},{3,15},{4,16},{5,17},{6,18},{7,19},{8,20},{9,... | collective-permute-start | bytes 122888
  2261.8 265.2 %all-gather.12.cloned.1.call-start = ((), (), s32[]{:S(2)}) async-start(), calls=%async_computation.1 | async-start | bytes 9246720 | tf_op jit(solution)/reshape | solution.py:58
  2263.6 390.4 %all-gather.10.cloned.1.call-start = ((), (), s32[]{:S(2)}) async-start(), calls=%async_computation | async-start | bytes 9246720 | tf_op jit(solution)/reshape | solution.py:58
  (61 other events, 9282.1 us)
Sparse Core Ops, SparseCore 0:
  2261.9 138.0 all-gather.13
  2404.3 122.7 all-gather.11
  2531.3 122.7 all-gather.9
where the time goes:
time: 2680 us; the launch traced here: 2670 us
  blocking collectives  1630 us (61%)
  waiting for transfers between devices  379 us (14%)
  matrix products  274 us (10%)
  starting transfers between devices  251 us (9%)
  local copies, waits for them, and re-layouts  66.7 us (2%)
  other arithmetic  53.2 us (2%)
    unnamed x2, blocking collectives  1300 us
    reshape x3, waiting for transfers between devices, step(): t.reshape(-1, *t.shape[2:])  367 us
    reduce_sum x1, blocking collectives, of_a_group(): jnp.sum(g * g)  326 us
    unnamed x64, starting transfers between devices  250 us
    dot_general x5, matrix products, layer(): up = jnp.dot(a, w['w_up'], preferred_element_type=jnp.float32)  98.3 us
    dot_general x5, matrix products, layer(): gate = jnp.dot(a, w['w_gate'], preferred_element_type=jnp.float32)  90 us
    dot_general x5, matrix products, matmul(): jnp.dot(a, w, preferred_element_type=jnp.float32).astype(jnp.bfloat16)  86 us
    unnamed x71, local copies, waits for them, and re-layouts  63 us
  transfers between devices with their start and end apart: 67, of which 9 were waited for; matrix products, arithmetic and copies ran while one was open for 3% of the time, Pallas kernels for 0%

commit v1 on v0

v1 whole, which is shorter than its diff:
```python
import functools
import heapq
import jax
import jax.numpy as jnp
from jax import lax
from jax.experimental import pallas as pl
from jax.experimental.pallas import tpu as pltpu

F32, BF16 = jnp.float32, jnp.bfloat16
MESH = pl.DeviceIdType.MESH
RATE, LATENCY = 46.6e3, 2.3
TURN, ADD, HOP = 0.1, 2.0e6, 0.7
WAYS = (1, -1)
RING, CROSS, DIRECT = range(3)


class Torus:
    def __init__(self, nx, ny, nz):
        self.n = {"x": nx, "y": ny, "z": nz}
        self.size = nx * ny * nz

    def me(self):
        p = lax.axis_index("dp")
        ny, nz = self.n["y"], self.n["z"]
        return {"z": lax.rem(p, nz), "y": lax.rem(lax.div(p, nz), ny), "x": lax.div(p, ny * nz)}

    def peer(self, me, dim, delta):
        at = dict(me)
        at[dim] = lax.rem(me[dim] + delta + self.n[dim], self.n[dim])
        return {"dp": (at["x"] * self.n["y"] + at["y"]) * self.n["z"] + at["z"]}


ORDERS = ("zxy", "xyz", "yxz")


def hops(n, flip):
    far, near = n // 2, n - 1 - n // 2
    return {1: near, -1: far} if flip else {1: far, -1: near}


class Balance:
    def __init__(self):
        self.load = {}

    def flip(self, dim, n, size):
        plain = [self.load.get((dim, s), 0) + size * hops(n, False)[s] for s in WAYS]
        turned = [self.load.get((dim, s), 0) + size * hops(n, True)[s] for s in WAYS]
        flip = max(turned) < max(plain)
        self.load[dim, 1], self.load[dim, -1] = turned if flip else plain
        return flip


def wrap(value, n):
    return lax.rem(value + 2 * n, n)


def simulate(actions, copies):
    links, arrived, order = {}, {}, []
    waiting = {a: set(needs) for a, (needs, _, _, _) in actions.items()}
    by_need = {}
    for a, (needs, _, _, _) in actions.items():
        for c in needs:
            by_need.setdefault(c, []).append(a)
    ready = [(actions[a][3], i, a) for i, a in enumerate(actions) if not waiting[a]]
    rank = {a: i for i, a in enumerate(actions)}
    heapq.heapify(ready)
    now, done = 0.0, {}
    while ready:
        at, _, a = heapq.heappop(ready)
        now = max(now, at) + actions[a][2]
        order.append(a)
        done[a] = now
        for c in [("action", a)] + list(actions[a][1]):
            if c[0] == "action":
                end = now
            else:
                link, size, extra = copies[c]
                start = max(now, links.get(link, 0.0))
                links[link] = start + size / RATE
                end = links[link] + LATENCY + extra
            for b in by_need.get(c, ()):
                waiting[b].discard(c)
                arrived[b] = max(arrived.get(b, 0.0), end)
                if not waiting[b]:
                    heapq.heappush(ready, (max(arrived[b], actions[b][3]), rank[b], b))
    assert len(order) == len(actions), (len(order), len(actions))
    return order, now


def barrier(torus, me, peers):
    sem = pltpu.get_barrier_semaphore()
    for dim, delta in peers:
        pl.semaphore_signal(sem, inc=1, device_id=torus.peer(me, dim, delta), device_id_type=MESH)
    pl.semaphore_wait(sem, len(peers))


def both_ways(torus, dim):
    n = torus.n[dim]
    return [] if n == 1 else [(dim, 1)] if n == 2 else [(dim, 1), (dim, -1)]


def all_others(torus, dim):
    return [(dim, d) for d in range(1, torus.n[dim])]


class ReduceScatter:
    def __init__(self, torus, rows, units):
        self.t, self.rows, self.units = torus, rows, units
        self.dims = [tuple(order) for order in ORDERS]
        self.nslots = sum(torus.n.values()) - 3

    def sizes(self, c):
        return [self.t.n[d] for d in self.dims[c]]

    def here(self, c):
        return [self.me[d] for d in self.dims[c]]

    def peers(self):
        full = {dims[DIRECT] for dims in self.dims}
        out = []
        for dim in "xyz":
            out += all_others(self.t, dim) if dim in full else both_ways(self.t, dim)
        return out

    def credit_peers(self, c):
        a, b, d = self.dims[c]
        return both_ways(self.t, a) + both_ways(self.t, b) + all_others(self.t, d)

    def scratch(self):
        n = self.t.n
        t, r1, r2, r3, k2, k3 = [], [], [], [], [], []
        for dims in self.dims:
            n1, n2, n3 = (n[d] for d in dims)
            tail = (self.rows, 128)
            t.append(pltpu.VMEM((self.units, n1, n2 * n3) + tail, BF16))
            r1.append(pltpu.VMEM((self.units, max(n1 - 1, 1), n2 * n3) + tail, BF16))
            r2.append(pltpu.VMEM((self.units, max(n2 - 1, 1), n3) + tail, BF16))
            r3.append(pltpu.VMEM((self.units, max(n3 - 1, 1)) + tail, BF16))
            k2.append(pltpu.VMEM((self.units, n3) + tail, F32))
            k3.append(pltpu.VMEM((self.units,) + tail, F32))
        sems = [pltpu.SemaphoreType.DMA((self.units, 3, self.nslots)), pltpu.SemaphoreType.DMA((self.units, 3, self.nslots)), pltpu.SemaphoreType.REGULAR((self.units, 3))]
        return [t, r1, r2, r3, k2, k3] + sems

    def slots(self, c, phase, flip):
        n = self.t.n[self.dims[c][phase]]
        k = hops(n, flip[phase])
        out, s = {}, 0
        for sign in WAYS:
            for h in range(k[sign]):
                out[sign, h] = s
                s += 1
        return out

    def base(self, c, phase):
        return sum(self.t.n[d] - 1 for d in self.dims[c][:phase])

    def flips(self, balance, c):
        n1, n2, n3 = self.sizes(c)
        block, (a, b, _) = self.rows * 256, self.dims[c]
        return balance.flip(a, n1, block * n2 * n3), balance.flip(b, n2, block * n3)

    def plan(self, unit, c, flip):
        n = self.sizes(c)
        n1, n2, n3 = n
        block = self.rows * 256
        size = [block * n2 * n3, block * n3, block]
        actions, copies = {}, {}
        key = (unit, c)

        def send(phase, sign, h):
            cid = ("copy", key, phase, sign, h)
            copies[cid] = ((self.dims[c][phase], sign), size[phase], 0)
            return cid

        first, last = [], []
        for phase in (RING, CROSS):
            k = hops(n[phase], flip[phase])
            first.append([send(phase, s, k[s] - 1) for s in WAYS if k[s]])
            last.append([("copy", key, phase, s, 0) for s in WAYS if k[s]])
            for s in WAYS:
                for h in range(k[s] - 1, 0, -1):
                    actions[key, "step", phase, s, h] = ([("copy", key, phase, s, h)], [send(phase, s, h - 1)], size[phase] / ADD)
        direct = []
        for rel in range(1, n3):
            cid = ("copy", key, DIRECT, 0, rel)
            far = min(rel, n3 - rel)
            copies[cid] = ((self.dims[c][DIRECT], 1 if rel <= n3 // 2 else -1), size[DIRECT] * far, HOP * (far - 1))
            direct.append(cid)
        sends = first + [direct, []]
        actions[key, "start"] = ([], sends[RING], TURN)
        before = (key, "start")
        for phase, needs in enumerate(last + [direct]):
            a = (key, "end", phase)
            actions[a] = (needs + [("action", before)], sends[phase + 1], size[phase] / ADD + TURN)
            before = a
        return actions, copies

    def bind(self, me, refs):
        self.me, (self.T, self.R1, self.R2, self.R3, self.K2, self.K3, self.ssem, self.rsem, self.credit) = me, refs
        return self

    def remote(self, u, c, flip, phase, sign, h):
        n1, n2, n3 = self.sizes(c)
        m1, m2, m3 = self.here(c)
        mine = self.T[c].at[u]
        if phase == RING:
            slot = self.slots(c, phase, flip)[sign, h]
            src, dst = mine.at[wrap(m1 + sign * (h + 1), n1)], self.R1[c].at[u, slot]
        elif phase == CROSS:
            slot = self.slots(c, phase, flip)[sign, h]
            src, dst = mine.at[m1, pl.ds(wrap(m2 + sign * (h + 1), n2) * n3, n3)], self.R2[c].at[u, slot]
        else:
            slot, sign = h - 1, h
            src, dst = mine.at[m1, m2 * n3 + wrap(m3 + h, n3)], self.R3[c].at[u, slot]
        s = self.base(c, phase) + slot
        to = self.t.peer(self.me, self.dims[c][phase], sign)
        return pltpu.make_async_remote_copy(src_ref=src, dst_ref=dst, send_sem=self.ssem.at[u, c, s], recv_sem=self.rsem.at[u, c, s], device_id=to, device_id_type=MESH)

    def all_sends(self, c, flip):
        n = self.sizes(c)
        out = []
        for phase in (RING, CROSS):
            k = hops(n[phase], flip[phase])
            out += [(phase, s, h) for s in WAYS for h in range(k[s])]
        return out + [(DIRECT, 0, rel) for rel in range(1, n[DIRECT])]

    def run(self, u, c, flip, what, store):
        n = self.sizes(c)
        n1, n2, n3 = n
        m1, m2, m3 = self.here(c)
        T, R1, R2, R3 = (r[c].at[u] for r in (self.T, self.R1, self.R2, self.R3))
        K2, K3 = self.K2[c].at[u], self.K3[c].at[u]
        mine = T.at[m1]
        wide = lambda v: v.astype(F32)
        go = lambda *a: self.remote(u, c, flip, *a)

        def loop(count, body):
            def one(i, carry):
                body(i)
                return carry

            lax.fori_loop(0, count, one, 0, unroll=2 - count % 2)

        def sends(phase):
            k = hops(n[phase], flip[phase])
            for s in WAYS:
                if k[s]:
                    go(phase, s, k[s] - 1).start()

        def arrived(phase):
            slots = self.slots(c, phase, flip)
            ways = [s for s in WAYS if (s, 0) in slots]
            for s in ways:
                go(phase, s, 0).wait_recv()
            return [slots[s, 0] for s in ways]

        kind, *where = what
        if kind == "start":
            sends(RING)
        elif kind == "step":
            phase, s, h = where
            go(phase, s, h).wait_recv()
            slot = self.slots(c, phase, flip)[s, h]
            q = wrap(self.here(c)[phase] + s * h, n[phase])

            def ring(i):
                T[q, i] = (wide(T[q, i]) + wide(R1[slot, i])).astype(BF16)

            def cross(i):
                b = q * n3 + i
                mine[b] = (wide(mine[b]) + wide(R2[slot, i])).astype(BF16)

            loop(n2 * n3 if phase == RING else n3, cross if phase else ring)
            go(phase, s, h - 1).start()
        elif where == [RING]:
            got = arrived(RING)

            def total(b):
                return sum((wide(R1[g, b]) for g in got), wide(mine[b]))

            def own(i):
                K2[i] = total(m2 * n3 + i)

            def others(i):
                b = lax.rem((m2 + 1) * n3 + i, n2 * n3)
                mine[b] = total(b).astype(BF16)

            loop((n2 - 1) * n3, others)
            sends(CROSS)
            loop(n3, own)
        elif where == [CROSS]:
            got = arrived(CROSS)

            def total(q):
                return sum((wide(R2[g, q]) for g in got), K2[q])

            for rel in range(1, n3):
                q = wrap(m3 + rel, n3)
                mine[m2 * n3 + q] = total(q).astype(BF16)
            for rel in range(1, n3):
                go(DIRECT, 0, rel).start()
            K3[...] = total(m3)
        else:
            for rel in range(1, n3):
                go(DIRECT, 0, rel).wait_recv()
            store(sum((wide(R3[i]) for i in range(n3 - 1)), K3[...]).astype(BF16).astype(F32))

    def wait_sends(self, u, c, flip):
        for a in self.all_sends(c, flip):
            self.remote(u, c, flip, *a).wait_send()

    def give_credit(self, u, c):
        for dim, delta in self.credit_peers(c):
            pl.semaphore_signal(self.credit.at[u, c], inc=1, device_id=self.t.peer(self.me, dim, delta), device_id_type=MESH)

    def take_credit(self, u, c):
        pl.semaphore_wait(self.credit.at[u, c], len(self.credit_peers(c)))


def reduce_scatter(torus, terms, rows, collective_id):
    layers, units = len(terms), len(terms[0])
    rs = ReduceScatter(torus, rows, units)
    actions, copies, balance, flips = {}, {}, Balance(), {}
    for l in range(layers):
        for u in range(units):
            for c in range(3):
                flips[l, u, c] = rs.flips(balance, c)
                got, sent = rs.plan((l, u), c, flips[l, u, c])
                copies |= sent
                for a, (needs, sends, cost) in got.items():
                    if l and a[1] == "start":
                        actions[a[0], "load"] = ([("action", (((l - 1, u), c), "end", 2))], [], TURN, 0)
                        needs = needs + [("action", (a[0], "load"))]
                    actions[a] = (needs, sends, cost, 0)
    order, took = simulate(actions, copies)
    flat = [t for layer in terms for unit in layer for t in unit]

    def kernel(*refs):
        ins, out, scratch, lsem = refs[: len(flat)], refs[len(flat)], refs[len(flat) + 1 : -1], refs[-1]
        me = torus.me()
        it = rs.bind(me, scratch)
        barrier(torus, me, rs.peers())

        def load(l, u, c):
            return pltpu.make_async_copy(ins[(l * units + u) * 3 + c], it.T[c].at[u], lsem.at[u, c])

        for u in range(units):
            for c in range(3):
                load(0, u, c).start()
        for a in order:
            ((l, u), c), what = a[0], a[1:]
            flip = flips[l, u, c]
            if what[0] == "load":
                it.wait_sends(u, c, flips[l - 1, u, c])
                it.give_credit(u, c)
                load(l, u, c).start()
                continue
            if what[0] == "start":
                load(l, u, c).wait()
                if l:
                    it.take_credit(u, c)

            def store(value):
                out[l, u, c] = value

            it.run(u, c, flip, what, store)
        for u in range(units):
            for c in range(3):
                it.wait_sends(u, c, flips[layers - 1, u, c])

    return pl.pallas_call(
        kernel,
        out_shape=jax.ShapeDtypeStruct((layers, units, 3, rows, 128), F32),
        in_specs=[pl.BlockSpec(memory_space=pl.ANY)] * len(flat),
        out_specs=pl.BlockSpec(memory_space=pltpu.VMEM),
        scratch_shapes=rs.scratch() + [pltpu.SemaphoreType.DMA((units, 3))],
        compiler_params=pltpu.CompilerParams(collective_id=collective_id, has_side_effects=True, vmem_limit_bytes=56 * 2**20),
        name="reduce_scatter",
    )(*flat)


class AllGather:
    def __init__(self, torus, block_bytes, split=2):
        self.t, self.bytes, self.split = torus, block_bytes, split
        self.dims = [tuple(order) for order in ORDERS]
        self.copies, self.actions, self.index, self.flip = {}, {}, {}, {}
        self.balance = Balance()
        for c in range(3):
            self.plan(c)
        self.order, self.took = simulate({a: (*v, 0) for a, v in self.actions.items()}, self.copies)

    def peers(self):
        return [p for dim in "xyz" for p in both_ways(self.t, dim)]

    def pieces(self, c, j):
        n3 = self.t.n[self.dims[c][DIRECT]]
        return n3 if not j else self.split if n3 % self.split == 0 else 1

    def size(self, c, phase, j):
        line = self.bytes * self.t.n[self.dims[c][DIRECT]]
        return self.bytes if phase == DIRECT else line if phase == CROSS else line // self.pieces(c, j)

    def k(self, c, phase, j, i):
        dim = self.dims[c][phase]
        key = (c, phase, j, i)
        if key not in self.flip:
            self.flip[key] = self.balance.flip(dim, self.t.n[dim], self.size(c, phase, j))
        return hops(self.t.n[dim], self.flip[key])

    def plan(self, c):
        n1, n2, n3 = (self.t.n[d] for d in self.dims[c])

        def send(where, s, h):
            phase, j, _ = where
            cid = (c, where, s, h)
            self.copies[cid] = ((self.dims[c][phase], s), self.size(c, phase, j), 0)
            self.index[cid] = len(self.index)
            return cid

        def own(*where):
            k = self.k(c, *where)
            return [send(where, s, 1) for s in WAYS if k[s]]

        def line(j):
            return [x for i in range(self.pieces(c, j)) for x in own(RING, j, i)]

        def passing(*where):
            k = self.k(c, *where)
            for s in WAYS:
                for h in range(1, k[s] + 1):
                    yield s, h, (c, "pass", where, s, h), [(c, where, s, h)], [send(where, s, h + 1)] if h < k[s] else []

        def act(a, needs, sends):
            self.actions[a] = (needs, sends, TURN / 2)

        act((c, "start"), [], own(DIRECT, 0, 0) + own(RING, 0, 0))
        got = [("action", (c, "start"))]
        for s, h, a, needs, sends in passing(DIRECT, 0, 0):
            act(a, needs, sends + own(RING, 0, (-s * h) % n3))
            got.append(("action", a))
        act((c, "line"), got, own(CROSS, 0, 0))
        for s, h, a, needs, sends in passing(CROSS, 0, 0):
            act(a, needs, sends + line((-s * h) % n2))
        for j in range(n2):
            for i in range(self.pieces(c, j)):
                for _, _, a, needs, sends in passing(RING, j, i):
                    act(a, needs, sends)

    def bind(self, me, G, ssem, rsem):
        self.me, self.G, self.ssem, self.rsem = me, G, ssem, rsem
        return self

    def remote(self, cid, back):
        c, (phase, j, i), s, h = cid
        a, b, d = self.dims[c]
        n1, n2, n3 = (self.t.n[x] for x in (a, b, d))
        m1, m2, m3 = (self.me[x] for x in (a, b, d))
        off = s * (back - h)
        G = self.G[c]
        if phase == DIRECT:
            ref = G.at[m1, m2 * n3 + wrap(m3 + off, n3)]
        elif phase == CROSS:
            ref = G.at[m1, pl.ds(wrap(m2 + off, n2) * n3, n3)]
        elif j == 0:
            ref = G.at[wrap(m1 + off, n1), m2 * n3 + wrap(m3 + i, n3)]
        else:
            size = n3 // self.pieces(c, j)
            ref = G.at[wrap(m1 + off, n1), pl.ds(wrap(m2 + j, n2) * n3 + i * size, size)]
        x = self.index[cid]
        return pltpu.make_async_remote_copy(src_ref=ref, dst_ref=ref, send_sem=self.ssem.at[x], recv_sem=self.rsem.at[x], device_id=self.t.peer(self.me, self.dims[c][phase], s), device_id_type=MESH)

    def run(self, a):
        needs, sends, _ = self.actions[a]
        for cid in needs:
            if cid in self.index:
                self.remote(cid, 0).wait_recv()
        for cid in sends:
            self.remote(cid, 1).start()

    def wait_sends(self):
        for cid in self.copies:
            self.remote(cid, 1).wait_send()


MIB = 2**20
LAYERS, D, FF = 2, 896, 2560
LANES, ROWS, CHUNK = 128, 144, 48
HIGH = {0: 7, 1: 7, 2: 20}
WIDE = {0: FF, 1: FF, 2: D}


def tiles(u):
    high, wide = HIGH[u], WIDE[u] // LANES
    out = []
    for k in range(ROWS // 8):
        ct, row = divmod(8 * k, high)
        out.append((ct, row, min(8, high - row), ct + 1 < wide))
    return out


def owner_index(torus, c, i):
    ny, nz = torus.n["y"], torus.n["z"]
    at = {"z": lax.rem(i, nz), "y": lax.rem(lax.div(i, nz), ny), "x": lax.div(i, ny * nz)}
    n = torus.n
    a, b, d = ORDERS[c]
    return at[a], at[b] * n[d] + at[d]


def pack(torus, u, X, outs):
    high = HIGH[u]
    sub = lax.broadcasted_iota(jnp.int32, (8, LANES), 0)

    def piece(i, ct, row, count, more):
        start = high * i + row + 8
        a = X[ct, pl.ds(start, 8), :]
        if count == 8:
            return a
        b = X[ct + 1, pl.ds(start - row - count, 8), :] if more else jnp.zeros((8, LANES), F32)
        return jnp.where(sub < count, a, b)

    got = tiles(u)

    def body(i, carry):
        at = [owner_index(torus, c, i) for c in range(3)]
        for j in range(ROWS // 16):
            both = jnp.concatenate([piece(i, *got[2 * j]), piece(i, *got[2 * j + 1])], axis=0).astype(BF16)
            c, r = divmod(16 * j, CHUNK)
            outs[c][at[c][0], at[c][1], pl.ds(r, 16), :] = both
        return carry

    lax.fori_loop(0, torus.size, body, 0, unroll=4)


def pieces_shapes(torus, dtype, *mid):
    out = []
    for order in ORDERS:
        a, b, d = (torus.n[x] for x in order)
        out.append(jax.ShapeDtypeStruct((a, b * d) + mid + (CHUNK, LANES), dtype))
    return out


def weight_terms(torus, u, a, b):
    tokens = a.shape[0]
    rows, cols = a.shape[1], b.shape[1]
    step = 256
    by_rows = u == 2
    steps = (rows if by_rows else cols) // step

    def kernel(a_ref, b_ref, o0, o1, o2, X):
        s = pl.program_id(0)
        got = lax.dot_general(a_ref[...], b_ref[...], (((0,), (0,)), ((), ())), preferred_element_type=F32)
        if by_rows:
            for ct in range(cols // LANES):
                X[ct, pl.ds(pl.multiple_of(s * step, step) + 8, step), :] = got[:, ct * LANES : (ct + 1) * LANES]
        else:
            for k in range(step // LANES):
                X[s * (step // LANES) + k, pl.ds(8, rows), :] = got[:, k * LANES : (k + 1) * LANES]

        @pl.when(s == steps - 1)
        def _():
            pack(torus, u, X, (o0, o1, o2))

    a_spec = pl.BlockSpec((tokens, step), lambda s: (0, s)) if by_rows else pl.BlockSpec((tokens, rows), lambda s: (0, 0))
    b_spec = pl.BlockSpec((tokens, cols), lambda s: (0, 0)) if by_rows else pl.BlockSpec((tokens, step), lambda s: (0, s))
    shapes = pieces_shapes(torus, BF16)
    return pl.pallas_call(
        kernel,
        grid=(steps,),
        out_shape=shapes,
        in_specs=[a_spec, b_spec],
        out_specs=[pl.BlockSpec(s.shape, lambda i: (0, 0, 0, 0)) for s in shapes],
        scratch_shapes=[pltpu.VMEM((cols // LANES, rows + 24, LANES), F32)],
        compiler_params=pltpu.CompilerParams(vmem_limit_bytes=56 * MIB),
        cost_estimate=pl.CostEstimate(flops=2 * tokens * rows * cols, bytes_accessed=2 * (tokens * (rows + cols) + rows * cols), transcendentals=0),
        name=f"terms_{u}",
    )(a, b)


def step_and_gather(torus, g, w, m, v, count, collective_id):
    ag = AllGather(torus, LAYERS * 3 * CHUNK * 256)
    dims = "zxy"
    slots = {d: torus.n[d] - 1 for d in dims}

    def kernel(g_ref, *refs):
        w_in, m_in, v_in, G, m_out, v_out = (refs[i : i + 3] for i in range(0, 18, 3))
        flat, wflat, part, E, esend, erecv, ssem, rsem = refs[18:]
        me = torus.me()
        barrier(torus, me, [p for d in "xyz" for p in all_others(torus, d)])
        acc = jnp.zeros((8, LANES), F32)
        for l in range(LAYERS):
            for u in range(3):
                for c in range(3):
                    value = g_ref[l, u, c]
                    flat[l, u, pl.ds(c * CHUNK, CHUNK), :] = value
                    for r in range(0, CHUNK, 8):
                        acc = acc + value[r : r + 8] * value[r : r + 8]
        part[0] = acc
        base = 0
        for i, d in enumerate(dims):
            n = torus.n[d]
            copies = []
            for rel in range(1, n):
                s = base + rel - 1
                copies.append(pltpu.make_async_remote_copy(src_ref=part.at[i], dst_ref=E.at[s], send_sem=esend.at[s], recv_sem=erecv.at[s], device_id=torus.peer(me, d, rel), device_id_type=MESH))
            for copy in copies:
                copy.start()
            total = part[i]
            for rel in range(1, n):
                copies[rel - 1].wait_recv()
                total = total + E[base + rel - 1]
            part[i + 1] = total
            for copy in copies:
                copy.wait_send()
            base += n - 1
        mean = jnp.sum(part[3], keepdims=True) / count
        factor = jnp.minimum(1.0, 0.5 * lax.rsqrt(mean + 1e-30))
        for l in range(LAYERS):
            for u in range(3):
                high = HIGH[u]
                wflat[l, u, pl.ds(ROWS - 8, 8), :] = jnp.zeros((8, LANES), F32)
                for ct in range(WIDE[u] // LANES):
                    at = (l, slice(None), pl.ds(ct * LANES, LANES))
                    grad = flat[l, u, pl.ds(ct * high, high), :] * factor
                    new_m = 0.9 * m_in[u][at] + 0.1 * grad
                    new_v = 0.95 * v_in[u][at] + 0.05 * grad * grad
                    wide = w_in[u][at]
                    new_w = wide - 0.02 * (new_m * lax.rsqrt(new_v + 1e-8) + 0.1 * wide)
                    m_out[u][at] = new_m
                    v_out[u][at] = new_v
                    wflat[l, u, pl.ds(ct * high, high), :] = new_w
        it = ag.bind(me, G, ssem, rsem)
        for c in range(3):
            n = [torus.n[d] for d in ORDERS[c]]
            at = [me[d] for d in ORDERS[c]]
            for l in range(LAYERS):
                for u in range(3):
                    G[c][at[0], at[1] * n[2] + at[2], l, u] = wflat[l, u, pl.ds(c * CHUNK, CHUNK), :].astype(BF16)
        for a in ag.order:
            it.run(a)
        it.wait_sends()

    vmem = pl.BlockSpec(memory_space=pltpu.VMEM)
    nsum = sum(slots.values())
    shapes = pieces_shapes(torus, BF16, LAYERS, 3)
    f32 = [jax.ShapeDtypeStruct(t.shape, F32) for t in m]
    k = len(ag.copies)
    got = pl.pallas_call(
        kernel,
        out_shape=[pltpu.MemorySpace.VMEM(s.shape, s.dtype) for s in shapes] + f32 * 2,
        in_specs=[vmem] * 10,
        out_specs=[vmem] * 9,
        scratch_shapes=[
            pltpu.VMEM((LAYERS, 3, ROWS, LANES), F32),
            pltpu.VMEM((LAYERS, 3, ROWS, LANES), F32),
            pltpu.VMEM((4, 8, LANES), F32),
            pltpu.VMEM((nsum, 8, LANES), F32),
            pltpu.SemaphoreType.DMA((nsum,)),
            pltpu.SemaphoreType.DMA((nsum,)),
            pltpu.SemaphoreType.DMA((k,)),
            pltpu.SemaphoreType.DMA((k,)),
        ],
        compiler_params=pltpu.CompilerParams(collective_id=collective_id, has_side_effects=True, vmem_limit_bytes=10 * MIB),
        name="step_and_gather",
    )(g, *w, *m, *v)
    return got[:3], got[3:6], got[6:]


def unpack(torus, G):
    nx, ny, nz = (torus.n[d] for d in "xyz")
    pair = 2
    group = pair * nz
    groups = torus.size // group
    pairs = ny // pair

    def kernel(g0, g1, g2, *refs):
        outs, Z, Y = refs[:3], refs[3], refs[4]
        l, s = pl.program_id(0), pl.program_id(1)
        corner = {"x": lax.div(s, pairs), "y": lax.rem(s, pairs) * pair, "z": 0}
        for u in range(3):
            high, wide = HIGH[u], WIDE[u] // LANES
            for i in range(group):
                y, z = divmod(i, nz)
                at = corner | {"y": corner["y"] + y, "z": z}
                for c, ref in enumerate((g0, g1, g2)):
                    a, b, d = ORDERS[c]
                    Z[i, pl.ds(c * CHUNK, CHUNK), :] = ref[at[a], at[b] * torus.n[d] + at[d], l, u].astype(F32)
            for i in range(group):
                for ct in range(wide):
                    for r in range(0, high, 8):
                        Y[ct, pl.ds(high * i + r, 8), :] = Z[i, pl.ds(high * ct + r, 8), :]
            rows = high * group
            for ct in range(wide):
                outs[u][0, :, pl.ds(ct * LANES, LANES)] = Y[ct, pl.ds(0, rows), :].astype(BF16)

    shapes = [(LAYERS, HIGH[u] * torus.size, WIDE[u]) for u in range(3)]
    return pl.pallas_call(
        kernel,
        grid=(LAYERS, groups),
        out_shape=[jax.ShapeDtypeStruct(s, BF16) for s in shapes],
        in_specs=[pl.BlockSpec(memory_space=pltpu.VMEM)] * 3,
        out_specs=[pl.BlockSpec((1, HIGH[u] * group, WIDE[u]), lambda l, s: (l, s, 0)) for u in range(3)],
        scratch_shapes=[pltpu.VMEM((group, ROWS + 8, LANES), F32), pltpu.VMEM((FF // LANES, HIGH[2] * group + 8, LANES), F32)],
        compiler_params=pltpu.CompilerParams(vmem_limit_bytes=16 * MIB),
        name="unpack",
    )(*G)


def dot(a, b, dims):
    return lax.dot_general(a, b, (dims, ((), ())), preferred_element_type=F32)


def normed(h):
    wide = h.astype(F32)
    scale = lax.rsqrt(jnp.mean(wide**2, -1, keepdims=True) + 1e-6)
    return (wide * scale).astype(BF16), wide, scale


def hidden(a, gate_w, up_w):
    gate, up = dot(a, gate_w, ((1,), (0,))), dot(a, up_w, ((1,), (0,)))
    s = jax.nn.sigmoid(gate)
    act = gate * s
    return (act * up).astype(BF16), act, up, s * (1.0 + gate * (1.0 - s))


def hidden_back(d, act, up, slope):
    return (d * up * slope).astype(BF16), (d * act).astype(BF16)


def solution(mesh):
    torus = Torus(4, 4, 8)
    count = float(LAYERS * 3 * D * FF)

    def step(x, dy, wg, wu, wd, mg, mu, md, vg, vu, vd):
        x, dy = x[0], dy[0]
        a0, _, _ = normed(x)
        mid0, act0, up0, slope0 = hidden(a0, wg[0], wu[0])
        h1 = x + dot(mid0, wd[0], ((1,), (0,))).astype(BF16)
        a1, wide1, scale1 = normed(h1)
        mid1, act1, up1, slope1 = hidden(a1, wg[1], wu[1])
        dmid1 = dot(dy, wd[1], ((1,), (1,))).astype(BF16).astype(F32)
        dgate1, dup1 = hidden_back(dmid1, act1, up1, slope1)
        t1 = [weight_terms(torus, 0, a1, dgate1), weight_terms(torus, 1, a1, dup1), weight_terms(torus, 2, mid1, dy)]
        da = (dot(dgate1, wg[1], ((1,), (1,))) + dot(dup1, wu[1], ((1,), (1,)))).astype(BF16).astype(F32)
        inner = jnp.mean(da * wide1, -1, keepdims=True)
        dh = dy + (scale1 * da - wide1 * (scale1 * scale1 * scale1 * inner)).astype(BF16)
        dmid0 = dot(dh, wd[0], ((1,), (1,))).astype(BF16).astype(F32)
        dgate0, dup0 = hidden_back(dmid0, act0, up0, slope0)
        t0 = [weight_terms(torus, 0, a0, dgate0), weight_terms(torus, 1, a0, dup0), weight_terms(torus, 2, mid0, dh)]
        g = reduce_scatter(torus, [t1, t0], CHUNK, 1)[::-1]
        p = lax.axis_index("dp")
        mine = [lax.dynamic_slice_in_dim(w, p * HIGH[u], HIGH[u], 1).astype(F32) for u, w in enumerate((wg, wu, wd))]
        G, m, v = step_and_gather(torus, g, mine, (mg, mu, md), (vg, vu, vd), count, 2)
        return (*unpack(torus, G), *m, *v)

    P = jax.sharding.PartitionSpec
    return jax.shard_map(
        step,
        mesh=mesh,
        in_specs=(P(("rep", "dp")),) * 2 + (P(),) * 3 + (P(None, "dp"),) * 6,
        out_specs=(P("rep"),) * 3 + (P("rep", "dp"),) * 6,
        check_vma=False,
    )
```

time: 2680 us -> 619 us (0.23)
  blocking collectives: 1630 us -> 0 us
  Pallas kernels: 0 us -> 402 us
  waiting for transfers between devices: 379 us -> 0 us
  starting transfers between devices: 251 us -> 0 us
  matrix products: 274 us -> 186 us
  local copies, waits for them, and re-layouts: 66.7 us -> 7.65 us
  other arithmetic: 53.2 us -> 11.4 us
    unnamed x2 -> x0, blocking collectives: 1300 us -> none
    pallas_call x0 -> x9, Pallas kernels: none -> 402 us  [the longest x1 145 us: reduce_scatter(): pl.pallas_call(kernel, out_shape=jax.ShapeDtypeStruct((layers, units, 3,...]
    reshape x3 -> x0, waiting for transfers between devices: 367 us -> none  [step(): t.reshape(-1, *t.shape[2:])]
    reduce_sum x1 -> x0, blocking collectives: 326 us -> none  [of_a_group(): jnp.sum(g * g)]
    unnamed x64 -> x0, starting transfers between devices: 250 us -> none
    dot_general x15 -> x9, matrix products: 274 us -> 186 us  [dot(): return lax.dot_general(a, b, (dims, ((), ())), preferred_element_type=F32)]
    unnamed x71 -> x44, local copies, waits for them, and re-layouts: 63 us -> 6.6 us
    unnamed x8 -> x0, other arithmetic: 45.2 us -> none
  transfers between devices with their start and end apart: 67 -> 0, of which waited for: 9 -> 0; matrix products, arithmetic and copies ran while one was open for 3% -> 0% of each run, Pallas kernels for 0% -> 0%
where the time goes in v1:
time: 619 us; the launch traced here: 609 us
  Pallas kernels  402 us (65%)
  matrix products  186 us (30%)
  other arithmetic  11.4 us (2%)
  local copies, waits for them, and re-layouts  7.65 us (1%)
    dot_general x9, matrix products, dot(): return lax.dot_general(a, b, (dims, ((), ())), preferred_element_type=F32)  186 us
    pallas_call x1, Pallas kernels, reduce_scatter(): pl.pallas_call(kernel, out_shape=jax.ShapeDtypeStruct((layers, units, 3,...  145 us
    pallas_call x1, Pallas kernels, step_and_gather(): pl.pallas_call(kernel, out_shape=[pltpu.MemorySpace.VMEM(s.shape, s.dtype...  133 us
    pallas_call x6, Pallas kernels, weight_terms(): pl.pallas_call(kernel, grid=(steps,), out_shape=shapes, in_specs=[a_spec,...  111 us
    pallas_call x1, Pallas kernels, unpack(): pl.pallas_call(kernel, grid=(LAYERS, groups), out_shape=[jax.ShapeDtypeSt...  14.2 us

profile of v1, /device:TPU:8, one launch (start us, length us, event | category | flops | bytes accessed | tf_op | source)
XLA Modules:
  0.0 608.8 jit_solution(2668363732816668317)
XLA Ops:
  0.6 2.8 fusion.8
  3.5 18.2 %fusion.29 = f32[2048,2560]{1,0:T(8,128)} fusion(bf16[2,896,2560]{2,1,0:T(8,128)(2,1)} %param.13, bf16[1,2048,896]{2,1,0:T(8,128)(2,1)} %param.11, f32[2048]{0:T(1024)S(1)} %add_rsqrt_fusion.1), kind=kOutput, calls=%fused_computation.48 | convolution fusion | flops 9400745984 | bytes 29237248 | tf_op jit(solution)/shard_map/dot_general | solution.py:709
  21.7 24.4 %multiply_convert_fusion.1 = (bf16[2048,2560]{1,0:T(8,128)(2,1)}, f32[2048,2560]{1,0:T(8,128)}) fusion(f32[2048,2560]{1,0:T(8,128)} %fusion.29, bf16[2,896,2560]{2,1,0:T(8,128)(2,1)} %param.14, bf16[1,2048,896]{2,1,0:T(8,128)(2,1)S(1)} %copy-done, f32[2048]{0:T(1024)S(1)} %add_rsqrt_fusion.1), kind=kOutput, calls=%fused_computation.13 | convolution fusion | flops 9432203264 | bytes 60694528 | tf_op jit(solution)/shard_map/dot_general | solution.py:709
  46.1 15.8 %fusion.12 = (f32[2048]{0:T(1024)S(1)}, bf16[2048,896]{1,0:T(8,128)(2,1)S(1)}) fusion(bf16[2048,2560]{1,0:T(8,128)(2,1)} %get-tuple-element.83.a_ref, bf16[2,2560,896]{2,1,0:T(8,128)(2,1)} %param.15, bf16[1,2048,896]{2,1,0:T(8,128)(2,1)S(1)} %copy-done), kind=kOutput, calls=%fused_computation.29 | convolution fusion | flops 9404413952 | bytes 22421504 | tf_op jit(solution)/shard_map/dot_general | solution.py:709
  61.9 1.8 copy-done.2
  63.7 0.7 fusion.13.a_ref
  64.5 18.5 %fusion.17 = f32[2048,2560]{1,0:T(8,128)} fusion(bf16[2048,896]{1,0:T(8,128)(2,1)S(1)} %fusion.13.a_ref, bf16[2,896,2560]{2,1,0:T(8,128)(2,1)} %param.13), kind=kOutput, calls=%fused_computation.36 | convolution fusion | flops 9395240960 | bytes 29229056 | tf_op jit(solution)/shard_map/dot_general | solution.py:709
  83.0 15.7 %convolution_convert_fusion.1 = bf16[2048,2560]{1,0:T(8,128)(2,1)} fusion(bf16[2,2560,896]{2,1,0:T(8,128)(2,1)} %param.15, bf16[1,2048,896]{2,1,0:T(8,128)(2,1)S(1)} %copy-done.4), kind=kOutput, calls=%fused_computation.21 | convolution fusion | flops 9400483840 | bytes 18743296 | tf_op jit(solution)/shard_map/dot_general | solution.py:709
  98.6 32.2 %multiply_convert_fusion = (bf16[2048,2560]{1,0:T(8,128)(2,1)}, bf16[2048,2560]{1,0:T(8,128)(2,1)}, bf16[2048,2560]{1,0:T(8,128)(2,1)}) fusion(f32[2048,2560]{1,0:T(8,128)} %fusion.17, bf16[2048,2560]{1,0:T(8,128)(2,1)} %convolution_convert_fusion.1, bf16[2048,896]{1,0:T(8,128)(2,1)} %copy-done.6, bf16[2,896,2560]{2,1,0:T(8,128)(2,1)} %param.14), kind=kOutput, calls=%fused_computation.10 | convolution fusion | flops 9479127040 | bytes 71172096 | tf_op jit(solution)/shard_map/dot_general | solution.py:709
  130.8 16.4 %fusion.15 = f32[2048,896]{1,0:T(8,128)} fusion(bf16[2048,2560]{1,0:T(8,128)(2,1)} %get-tuple-element.79.b_ref, bf16[2,896,2560]{2,1,0:T(8,128)(2,1)} %param.13), kind=kOutput, calls=%fused_computation.34 | convolution fusion | flops 9395240960 | bytes 22413312 | tf_op jit(solution)/shard_map/dot_general | solution.py:709
  147.2 16.6 %fusion.14 = (f32[2048]{0:T(1024)S(1)}, bf16[2048,896]{1,0:T(8,128)(2,1)S(1)}) fusion(bf16[2048,896]{1,0:T(8,128)(2,1)S(1)} %copy-done.3, f32[2048,896]{1,0:T(8,128)} %fusion.15, bf16[2048,2560]{1,0:T(8,128)(2,1)} %get-tuple-element.80.b_ref, bf16[2,896,2560]{2,1,0:T(8,128)(2,1)} %param.14), kind=kOutput, calls=%fused_computation.31 | convolution fusion | flops 9406248960 | bytes 29761536 | tf_op jit(solution)/shard_map/dot_general | solution.py:709
  163.8 3.4 fusion.41.b_ref
  167.2 19.2 %terms_2.3 = (bf16[8,16,48,128]{3,2,1,0:T(8,128)(2,1)}, bf16[4,32,48,128]{3,2,1,0:T(8,128)(2,1)}, bf16[4,32,48,128]{3,2,1,0:T(8,128)(2,1)}) custom-call(bf16[2048,2560]{1,0:T(8,128)(2,1)} %get-tuple-element.83.a_ref, bf16[2048,896]{1,0:T(8,128)(2,1)} %fusion.41.b_ref), custom_call_target="tpu_custom_call" | custom-call | flops 9395240960 | bytes 18743296 | tf_op jit(solution)/shard_map/terms_2/pallas_call | solution.py:566
  186.4 28.2 %fusion.5 = (bf16[2048,2560]{1,0:T(8,128)(2,1)}, bf16[2048,2560]{1,0:T(8,128)(2,1)}) fusion(f32[2048,2560]{1,0:T(8,128)} %fusion.29, f32[2048,2560]{1,0:T(8,128)} %get-tuple-element.84, bf16[2048,896]{1,0:T(8,128)(2,1)S(1)} %copy-done.7, bf16[2,2560,896]{2,1,0:T(8,128)(2,1)} %param.15), kind=kOutput, calls=%fused_computation.9 | convolution fusion | flops 9473884160 | bytes 71172096 | tf_op jit(solution)/shard_map/dot_general | solution.py:709
  214.7 2.5 fusion.9.a_ref
  217.2 18.0 %terms_1.3 = (bf16[8,16,48,128]{3,2,1,0:T(8,128)(2,1)}, bf16[4,32,48,128]{3,2,1,0:T(8,128)(2,1)}, bf16[4,32,48,128]{3,2,1,0:T(8,128)(2,1)}) custom-call(bf16[2048,896]{1,0:T(8,128)(2,1)} %fusion.9.a_ref, bf16[2048,2560]{1,0:T(8,128)(2,1)} %get-tuple-element.81.b_ref), custom_call_target="tpu_custom_call" | custom-call | flops 9395240960 | bytes 18743296 | tf_op jit(solution)/shard_map/terms_1/pallas_call | solution.py:566
  235.2 18.0 %terms_0.3 = (bf16[8,16,48,128]{3,2,1,0:T(8,128)(2,1)}, bf16[4,32,48,128]{3,2,1,0:T(8,128)(2,1)}, bf16[4,32,48,128]{3,2,1,0:T(8,128)(2,1)}) custom-call(bf16[2048,896]{1,0:T(8,128)(2,1)} %fusion.9.a_ref, bf16[2048,2560]{1,0:T(8,128)(2,1)} %get-tuple-element.82.b_ref), custom_call_target="tpu_custom_call" | custom-call | flops 9395240960 | bytes 18743296 | tf_op jit(solution)/shard_map/terms_0/pallas_call | solution.py:566
  253.2 18.0 %terms_1.2 = (bf16[8,16,48,128]{3,2,1,0:T(8,128)(2,1)}, bf16[4,32,48,128]{3,2,1,0:T(8,128)(2,1)}, bf16[4,32,48,128]{3,2,1,0:T(8,128)(2,1)}) custom-call(bf16[2048,896]{1,0:T(8,128)(2,1)} %copy-done.6, bf16[2048,2560]{1,0:T(8,128)(2,1)} %get-tuple-element.80.b_ref), custom_call_target="tpu_custom_call" | custom-call | flops 9395240960 | bytes 18743296 | tf_op jit(solution)/shard_map/terms_1/pallas_call | solution.py:566
  271.2 18.0 %terms_0.2 = (bf16[8,16,48,128]{3,2,1,0:T(8,128)(2,1)}, bf16[4,32,48,128]{3,2,1,0:T(8,128)(2,1)}, bf16[4,32,48,128]{3,2,1,0:T(8,128)(2,1)}) custom-call(bf16[2048,896]{1,0:T(8,128)(2,1)} %copy-done.6, bf16[2048,2560]{1,0:T(8,128)(2,1)} %get-tuple-element.79.b_ref), custom_call_target="tpu_custom_call" | custom-call | flops 9395240960 | bytes 18743296 | tf_op jit(solution)/shard_map/terms_0/pallas_call | solution.py:566
  289.2 19.4 %terms_2.2 = (bf16[8,16,48,128]{3,2,1,0:T(8,128)(2,1)}, bf16[4,32,48,128]{3,2,1,0:T(8,128)(2,1)}, bf16[4,32,48,128]{3,2,1,0:T(8,128)(2,1)}) custom-call(bf16[2048,2560]{1,0:T(8,128)(2,1)} %get-tuple-element.78.a_ref, bf16[2048,896]{1,0:T(8,128)(2,1)} %bitcast.58), custom_call_target="tpu_custom_call" | custom-call | flops 9395240960 | bytes 18743296 | tf_op jit(solution)/shard_map/terms_2/pallas_call | solution.py:566
  308.6 144.6 %reduce_scatter.1 = f32[2,3,3,48,128]{4,3,2,1,0:T(8,128)} custom-call(bf16[8,16,48,128]{3,2,1,0:T(8,128)(2,1)} %get-tuple-element.39.refs_0_, bf16[4,32,48,128]{3,2,1,0:T(8,128)(2,1)} %get-tuple-element.40.refs_1_, bf16[4,32,48,128]{3,2,1,0:T(8,128)(2,1)} %get-tuple-element.41.refs_2_, bf16[8,16,48,128]{3,2,1,0:T(8,128)(2,1)} %get-tuple-element.42.refs_3_, ...), custom_call_target="tpu_custom_call" | custom-call | tf_op jit(solution)/shard_map/reduce_scatter/pallas_call | solution.py:371
  453.3 1.0 rev.3.g_ref
  454.3 1.1 dynamic-slice_convert_fusion.1
  455.4 0.9 dynamic-slice_convert_fusion.refs_2_
  456.6 133.0 %step_and_gather.1 = (bf16[8,16,2,3,48,128]{5,4,3,2,1,0:T(8,128)(2,1)S(1)}, bf16[4,32,2,3,48,128]{5,4,3,2,1,0:T(8,128)(2,1)S(1)}, bf16[4,32,2,3,48,128]{5,4,3,2,...) custom-call(f32[2,3,3,48,128]{4,3,2,1,0:T(8,128)S(1)} %rev.3.g_ref, ...), custom_call_target="tpu_custom_call" | custom-call | tf_op jit(solution)/shard_map/step_and_gather/pallas_call | solution.py:647
  589.6 14.2 %unpack.1 = (bf16[2,896,2560]{2,1,0:T(8,128)(2,1)}, bf16[2,896,2560]{2,1,0:T(8,128)(2,1)}, bf16[2,2560,896]{2,1,0:T(8,128)(2,1)}) custom-call(bf16[8,16,2,3,48,128]{5,4,3,2,1,0:T(8,128)(2,1)S(1)} %get-tuple-element.57.g0, bf16[4,32,2,3,48,128]{5,4,3,2,1,0:T(8,128)(2,1)S(1)} %get-tuple-element.58.g1, bf16[4,32,2,3,48,128]{5,4,3,2,1,0:T(8,128)(2,1)S(1)} %get-tuple-element.59.g2), custom_call_target="tpu_custom_call" | custom-call | tf_op jit(solution)/shard_map/unpack/pallas_call | solution.py:696
  603.8 0.8 copy.29
  604.6 0.8 copy.30
  605.4 0.7 copy.31
  606.1 0.8 copy.32
  606.9 0.8 copy.33
  607.6 0.7 copy.34
  (40 shorter events, 0.3 us)
Async XLA Ops:
  3.5 18.2 %copy-start.14 = (f32[2048]{0:T(1024)}, f32[2048]{0:T(1024)S(1)}, u32[]{:S(2)}) copy-start(f32[2048]{0:T(1024)S(1)} %add_rsqrt_fusion.1) | copy-start | bytes 24580
  3.5 18.2 %copy-start = (bf16[1,2048,896]{2,1,0:T(8,128)(2,1)S(1)}, bf16[1,2048,896]{2,1,0:T(8,128)(2,1)}, u32[]{:S(2)}) copy-start(bf16[1,2048,896]{2,1,0:T(8,128)(2,1)} %param.11) | copy-start | bytes 11010052
  61.9 1.8 copy-start.2
  64.4 18.5 %copy-start.6 = (bf16[2048,896]{1,0:T(8,128)(2,1)}, bf16[2048,896]{1,0:T(8,128)(2,1)S(1)}, u32[]{:S(2)}) copy-start(bf16[2048,896]{1,0:T(8,128)(2,1)S(1)} %fusion.13.a_ref) | copy-start | bytes 11010052
  64.4 18.5 %copy-start.4 = (bf16[1,2048,896]{2,1,0:T(8,128)(2,1)S(1)}, bf16[1,2048,896]{2,1,0:T(8,128)(2,1)}, u32[]{:S(2)}) copy-start(bf16[1,2048,896]{2,1,0:T(8,128)(2,1)} %param.12) | copy-start | bytes 11010052
  130.8 16.4 %copy-start.3 = (bf16[2048,896]{1,0:T(8,128)(2,1)S(1)}, bf16[2048,896]{1,0:T(8,128)(2,1)}, u32[]{:S(2)}) copy-start(bf16[2048,896]{1,0:T(8,128)(2,1)} %copy-done.2) | copy-start | bytes 11010052
  147.2 16.6 %copy-start.5 = (bf16[1,2048,896]{2,1,0:T(8,128)(2,1)S(1)}, bf16[1,2048,896]{2,1,0:T(8,128)(2,1)}, u32[]{:S(2)}) copy-start(bf16[1,2048,896]{2,1,0:T(8,128)(2,1)} %param.12) | copy-start | bytes 11010052
  167.2 19.2 %copy-start.7 = (bf16[2048,896]{1,0:T(8,128)(2,1)S(1)}, bf16[2048,896]{1,0:T(8,128)(2,1)}, u32[]{:S(2)}) copy-start(bf16[2048,896]{1,0:T(8,128)(2,1)} %fusion.41.b_ref) | copy-start | bytes 11010052
  186.4 28.2 %copy-start.1 = (bf16[1,2048,896]{2,1,0:T(8,128)(2,1)S(1)}, bf16[1,2048,896]{2,1,0:T(8,128)(2,1)}, u32[]{:S(2)}) copy-start(bf16[1,2048,896]{2,1,0:T(8,128)(2,1)} %param.11) | copy-start | bytes 11010052
  186.4 28.2 %copy-start.15 = (f32[2048]{0:T(1024)S(1)}, f32[2048]{0:T(1024)}, u32[]{:S(2)}) copy-start(f32[2048]{0:T(1024)} %copy-done.14) | copy-start | bytes 24580
  308.6 147.7 %copy-start.8 = (f32[2,20,896]{2,0,1:T(2,128)S(1)}, f32[2,20,896]{2,0,1:T(2,128)}, u32[]{:S(2)}) copy-start(f32[2,20,896]{2,0,1:T(2,128)} %param.18) | copy-start | bytes 430084
  308.6 147.8 %copy-start.9 = (f32[2,20,896]{2,0,1:T(2,128)S(1)}, f32[2,20,896]{2,0,1:T(2,128)}, u32[]{:S(2)}) copy-start(f32[2,20,896]{2,0,1:T(2,128)} %param.21) | copy-start | bytes 430084
  308.6 147.8 %copy-start.10 = (f32[2,7,2560]{2,0,1:T(2,128)S(1)}, f32[2,7,2560]{2,0,1:T(2,128)}, u32[]{:S(2)}) copy-start(f32[2,7,2560]{2,0,1:T(2,128)} %param.16) | copy-start | bytes 430084
  308.6 147.8 %copy-start.11 = (f32[2,7,2560]{2,0,1:T(2,128)S(1)}, f32[2,7,2560]{2,0,1:T(2,128)}, u32[]{:S(2)}) copy-start(f32[2,7,2560]{2,0,1:T(2,128)} %param.17) | copy-start | bytes 430084
  308.6 147.9 %copy-start.12 = (f32[2,7,2560]{2,0,1:T(2,128)S(1)}, f32[2,7,2560]{2,0,1:T(2,128)}, u32[]{:S(2)}) copy-start(f32[2,7,2560]{2,0,1:T(2,128)} %param.19) | copy-start | bytes 430084
  308.6 147.9 %copy-start.13 = (f32[2,7,2560]{2,0,1:T(2,128)S(1)}, f32[2,7,2560]{2,0,1:T(2,128)}, u32[]{:S(2)}) copy-start(f32[2,7,2560]{2,0,1:T(2,128)} %param.20) | copy-start | bytes 430084

commit v2 on v1

--- a/solution.py
+++ b/solution.py
@@ -1,4 +1,3 @@
-import functools
 import heapq
 import jax
 import jax.numpy as jnp
@@ -12,6 +11,7 @@
 TURN, ADD, HOP = 0.1, 2.0e6, 0.7
 WAYS = (1, -1)
 RING, CROSS, DIRECT = range(3)
+PACKING, MARGIN = 2.5, 1.0
 
 
 class Torus:
@@ -87,6 +87,61 @@
     return order, now
 
 
+def place(actions, copies, stages):
+    links, known, done = {}, {}, set()
+    now, left = 0.0, dict(actions)
+    slots = {}
+
+    def ready(a, at):
+        needs, _, _ = actions[a]
+        return all(c in known and known[c] <= at for c in needs)
+
+    def do(a, where):
+        nonlocal now
+        _, sends, cost = actions[a]
+        now += cost
+        known["action", a] = now
+        for c in sends:
+            link, size, extra = copies[c]
+            links[link] = max(now, links.get(link, 0.0)) + size / RATE
+            known[c] = links[link] + LATENCY + extra + MARGIN
+        del left[a]
+        slots.setdefault(where, []).append(a)
+
+    def drain(where, allowed, wait):
+        nonlocal now
+        while True:
+            able = [a for a in left if allowed(a)]
+            best = min((max([known.get(c, 1e9) for c in actions[a][0]], default=0.0) for a in able), default=1e9)
+            if best > (1e8 if wait else now):
+                return
+            now = max(now, best)
+            for a in able:
+                if ready(a, now):
+                    do(a, where)
+                    break
+
+    packed = set()
+    usual = lambda a: a[1] != "start" or a[0][0] in packed
+    for number, cost, count, unit in stages:
+        for t in range(count):
+            now += cost
+            slots[number, t] = []
+            drain((number, t), usual, False)
+        slots[number, "before"], slots[number, "after"] = [], []
+        if unit:
+            other = [a for a in left if a[0][0][1] == unit[1] and a[0][0][0] > unit[0]]
+            if other:
+                drain((number, "before"), lambda a: a in other, True)
+            now += PACKING
+            packed.add(unit)
+            drain((number, "after"), usual, False)
+    drain((stages[-1][0], "after"), lambda a: True, True)
+    assert not left, left
+    place.took = now
+    return slots
+
+
 def barrier(torus, me, peers):
     sem = pltpu.get_barrier_semaphore()
     for dim, delta in peers:
@@ -317,68 +372,6 @@
         pl.semaphore_wait(self.credit.at[u, c], len(self.credit_peers(c)))
 
 
-def reduce_scatter(torus, terms, rows, collective_id):
-    layers, units = len(terms), len(terms[0])
-    rs = ReduceScatter(torus, rows, units)
-    actions, copies, balance, flips = {}, {}, Balance(), {}
-    for l in range(layers):
-        for u in range(units):
-            for c in range(3):
-                flips[l, u, c] = rs.flips(balance, c)
-                got, sent = rs.plan((l, u), c, flips[l, u, c])
-                copies |= sent
-                for a, (needs, sends, cost) in got.items():
-                    if l and a[1] == "start":
-                        actions[a[0], "load"] = ([("action", (((l - 1, u), c), "end", 2))], [], TURN, 0)
-                        needs = needs + [("action", (a[0], "load"))]
-                    actions[a] = (needs, sends, cost, 0)
-    order, took = simulate(actions, copies)
-    flat = [t for layer in terms for unit in layer for t in unit]
-
-    def kernel(*refs):
-        ins, out, scratch, lsem = refs[: len(flat)], refs[len(flat)], refs[len(flat) + 1 : -1], refs[-1]
-        me = torus.me()
-        it = rs.bind(me, scratch)
-        barrier(torus, me, rs.peers())
-
-        def load(l, u, c):
-            return pltpu.make_async_copy(ins[(l * units + u) * 3 + c], it.T[c].at[u], lsem.at[u, c])
-
-        for u in range(units):
-            for c in range(3):
-                load(0, u, c).start()
-        for a in order:
-            ((l, u), c), what = a[0], a[1:]
-            flip = flips[l, u, c]
-            if what[0] == "load":
-                it.wait_sends(u, c, flips[l - 1, u, c])
-                it.give_credit(u, c)
-                load(l, u, c).start()
-                continue
-            if what[0] == "start":
-                load(l, u, c).wait()
-                if l:
-                    it.take_credit(u, c)
-
-            def store(value):
-                out[l, u, c] = value
-
-            it.run(u, c, flip, what, store)
-        for u in range(units):
-            for c in range(3):
-                it.wait_sends(u, c, flips[layers - 1, u, c])
-
-    return pl.pallas_call(
-        kernel,
-        out_shape=jax.ShapeDtypeStruct((layers, units, 3, rows, 128), F32),
-        in_specs=[pl.BlockSpec(memory_space=pl.ANY)] * len(flat),
-        out_specs=pl.BlockSpec(memory_space=pltpu.VMEM),
-        scratch_shapes=rs.scratch() + [pltpu.SemaphoreType.DMA((units, 3))],
-        compiler_params=pltpu.CompilerParams(collective_id=collective_id, has_side_effects=True, vmem_limit_bytes=56 * 2**20),
-        name="reduce_scatter",
-    )(*flat)
-
-
 class AllGather:
     def __init__(self, torus, block_bytes, split=2):
         self.t, self.bytes, self.split = torus, block_bytes, split
@@ -483,6 +476,7 @@
 
 
 MIB = 2**20
+VMEM_ALL = 67043328
 LAYERS, D, FF = 2, 896, 2560
 LANES, ROWS, CHUNK = 128, 144, 48
 HIGH = {0: 7, 1: 7, 2: 20}
@@ -506,16 +500,16 @@
     return at[a], at[b] * n[d] + at[d]
 
 
-def pack(torus, u, X, outs):
+def pack(torus, u, X, stride, outs):
     high = HIGH[u]
     sub = lax.broadcasted_iota(jnp.int32, (8, LANES), 0)
 
     def piece(i, ct, row, count, more):
-        start = high * i + row + 8
-        a = X[ct, pl.ds(start, 8), :]
+        start = high * i + 8 + ct * stride
+        a = X[pl.ds(start + row, 8), :]
         if count == 8:
             return a
-        b = X[ct + 1, pl.ds(start - row - count, 8), :] if more else jnp.zeros((8, LANES), F32)
+        b = X[pl.ds(start + stride - count, 8), :] if more else jnp.zeros((8, LANES), F32)
         return jnp.where(sub < count, a, b)
 
     got = tiles(u)
@@ -537,43 +531,6 @@
         a, b, d = (torus.n[x] for x in order)
         out.append(jax.ShapeDtypeStruct((a, b * d) + mid + (CHUNK, LANES), dtype))
     return out
-
-
-def weight_terms(torus, u, a, b):
-    tokens = a.shape[0]
-    rows, cols = a.shape[1], b.shape[1]
-    step = 256
-    by_rows = u == 2
-    steps = (rows if by_rows else cols) // step
-
-    def kernel(a_ref, b_ref, o0, o1, o2, X):
-        s = pl.program_id(0)
-        got = lax.dot_general(a_ref[...], b_ref[...], (((0,), (0,)), ((), ())), preferred_element_type=F32)
-        if by_rows:
-            for ct in range(cols // LANES):
-                X[ct, pl.ds(pl.multiple_of(s * step, step) + 8, step), :] = got[:, ct * LANES : (ct + 1) * LANES]
-        else:
-            for k in range(step // LANES):
-                X[s * (step // LANES) + k, pl.ds(8, rows), :] = got[:, k * LANES : (k + 1) * LANES]
-
-        @pl.when(s == steps - 1)
-        def _():
-            pack(torus, u, X, (o0, o1, o2))
-
-    a_spec = pl.BlockSpec((tokens, step), lambda s: (0, s)) if by_rows else pl.BlockSpec((tokens, rows), lambda s: (0, 0))
-    b_spec = pl.BlockSpec((tokens, cols), lambda s: (0, 0)) if by_rows else pl.BlockSpec((tokens, step), lambda s: (0, s))
-    shapes = pieces_shapes(torus, BF16)
-    return pl.pallas_call(
-        kernel,
-        grid=(steps,),
-        out_shape=shapes,
-        in_specs=[a_spec, b_spec],
-        out_specs=[pl.BlockSpec(s.shape, lambda i: (0, 0, 0, 0)) for s in shapes],
-        scratch_shapes=[pltpu.VMEM((cols // LANES, rows + 24, LANES), F32)],
-        compiler_params=pltpu.CompilerParams(vmem_limit_bytes=56 * MIB),
-        cost_estimate=pl.CostEstimate(flops=2 * tokens * rows * cols, bytes_accessed=2 * (tokens * (rows + cols) + rows * cols), transcendentals=0),
-        name=f"terms_{u}",
-    )(a, b)
 
 
 def step_and_gather(torus, g, w, m, v, count, collective_id):
@@ -705,25 +662,312 @@
     )(*G)
 
 
-def dot(a, b, dims):
+TOKENS, TILE, PART = 2048, 256, 512
+LT = TILE // LANES
+NN, NT, TN = ((1,), (0,)), ((1,), (1,)), ((0,), (0,))
+
+
+def dot(a, b, dims=NN):
     return lax.dot_general(a, b, (dims, ((), ())), preferred_element_type=F32)
 
 
-def normed(h):
-    wide = h.astype(F32)
-    scale = lax.rsqrt(jnp.mean(wide**2, -1, keepdims=True) + 1e-6)
-    return (wide * scale).astype(BF16), wide, scale
-
-
-def hidden(a, gate_w, up_w):
-    gate, up = dot(a, gate_w, ((1,), (0,))), dot(a, up_w, ((1,), (0,)))
+def scale_of(wide):
+    return lax.rsqrt(jnp.mean(wide * wide, -1, keepdims=True) + 1e-6)
+
+
+def normed_into(h_ref, a_ref, t_ref):
+    for r in range(0, TOKENS, TILE):
+        wide = h_ref[pl.ds(r, TILE), :].astype(F32)
+        a = (wide * scale_of(wide)).astype(BF16)
+        a_ref[pl.ds(r, TILE), :] = a
+        t_ref[:, pl.ds(r, TILE)] = a.T
+
+
+def forward(x, wg, wu, wd):
+    steps = FF // TILE
+
+    def kernel(x_ref, wg_ref, wu_ref, wd_ref, gate_ref, up_ref, h_ref, a_ref, at_ref, xt_ref, xa, acc):
+        t = pl.program_id(0)
+
+        @pl.when(t == 0)
+        def _():
+            normed_into(x_ref, xa, xt_ref)
+            acc[...] = jnp.zeros_like(acc)
+
+        for r in range(0, TOKENS, PART):
+            rows = pl.ds(r, PART)
+            a = xa[rows, :]
+            gate, up = dot(a, wg_ref[...]), dot(a, wu_ref[...])
+            for k in range(LT):
+                lanes = slice(k * LANES, (k + 1) * LANES)
+                gate_ref[k, rows, :] = gate[:, lanes]
+                up_ref[k, rows, :] = up[:, lanes]
+            mid = (jax.nn.silu(gate) * up).astype(BF16)
+            acc[rows, :] += dot(mid, wd_ref[...])
+
+        @pl.when(t == steps - 1)
+        def _():
+            for r in range(0, TOKENS, TILE):
+                rows = pl.ds(r, TILE)
+                h_ref[rows, :] = x_ref[rows, :] + acc[rows, :].astype(BF16)
+            normed_into(h_ref, a_ref, at_ref)
+
+    whole = pl.BlockSpec(memory_space=pltpu.VMEM)
+    cols = pl.BlockSpec((D, TILE), lambda t: (0, t))
+    saved = pl.BlockSpec((LT, TOKENS, LANES), lambda t: (t, 0, 0))
+    return pl.pallas_call(
+        kernel,
+        grid=(steps,),
+        out_shape=[jax.ShapeDtypeStruct((FF // LANES, TOKENS, LANES), F32)] * 2 + [jax.ShapeDtypeStruct((TOKENS, D), BF16)] * 2 + [jax.ShapeDtypeStruct((D, TOKENS), BF16)] * 2,
+        in_specs=[whole, cols, cols, pl.BlockSpec((TILE, D), lambda t: (t, 0))],
+        out_specs=[saved] * 2 + [whole] * 4,
+        scratch_shapes=[pltpu.VMEM((TOKENS, D), BF16), pltpu.VMEM((TOKENS, D), F32)],
+        compiler_params=pltpu.CompilerParams(vmem_limit_bytes=60 * MIB),
+        cost_estimate=pl.CostEstimate(flops=6 * TOKENS * D * FF, bytes_accessed=10 * TOKENS * FF, transcendentals=0),
+        name="forward",
+    )(x, wg, wu, wd)
+
+
+def hidden_back(gate, up, d):
     s = jax.nn.sigmoid(gate)
     act = gate * s
-    return (act * up).astype(BF16), act, up, s * (1.0 + gate * (1.0 - s))
-
-
-def hidden_back(d, act, up, slope):
-    return (d * up * slope).astype(BF16), (d * act).astype(BF16)
+    return (act * up).astype(BF16), (d * up * (s + act * (1.0 - s))).astype(BF16), (d * act).astype(BF16)
+
+
+def last_layer(a, dy, wg, wu, wd):
+    steps = FF // TILE
+
+    def kernel(a_ref, dy_ref, wg_ref, wu_ref, wd_ref, mid_ref, dgate_ref, dup_ref):
+        for r in range(0, TOKENS, PART):
+            rows = pl.ds(r, PART)
+            part = a_ref[rows, :]
+            gate, up = dot(part, wg_ref[...]), dot(part, wu_ref[...])
+            d = dot(dy_ref[rows, :], wd_ref[...], NT).astype(BF16).astype(F32)
+            mid, dgate_ref[0, rows, :], dup_ref[0, rows, :] = hidden_back(gate, up, d)
+            mid_ref[:, rows] = mid.T
+
+    whole = pl.BlockSpec(memory_space=pltpu.VMEM)
+    cols = pl.BlockSpec((D, TILE), lambda t: (0, t))
+    rows = pl.BlockSpec((TILE, D), lambda t: (t, 0))
+    saved = pl.BlockSpec((1, TOKENS, TILE), lambda t: (t, 0, 0))
+    return pl.pallas_call(
+        kernel,
+        grid=(steps,),
+        out_shape=[jax.ShapeDtypeStruct((FF, TOKENS), BF16)] + [jax.ShapeDtypeStruct((steps, TOKENS, TILE), BF16)] * 2,
+        in_specs=[whole, whole, cols, cols, rows],
+        out_specs=[pl.BlockSpec((TILE, TOKENS), lambda t: (t, 0))] + [saved] * 2,
+        compiler_params=pltpu.CompilerParams(vmem_limit_bytes=60 * MIB),
+        cost_estimate=pl.CostEstimate(flops=6 * TOKENS * D * FF, bytes_accessed=6 * TOKENS * FF, transcendentals=0),
+        name="last_layer",
+    )(a, dy, wg, wu, wd)
+
+
+STEPS = FF // TILE
+GAP = 24
+STRIDE = {u: HIGH[u] * 128 + GAP for u in range(3)}
+COST = {"down": 1.2, "side": 1.05, "da": 2.4, "norm": 0.5, "hidden": 1.45}
+
+
+def backward(torus, mid1, dgate1, dup1, h1, dy, at1, at0, wg1, wu1, wd0, gate0, up0, collective_id):
+    rs = ReduceScatter(torus, CHUNK, 3)
+    DOWN = 2
+    stages = [("down", (1, DOWN)), ("side", (1, 0)), ("side", (1, 1)), ("da", None), ("norm", None), ("hidden", None), ("down", (0, DOWN)), ("side", (0, 0)), ("side", (0, 1))]
+    length = {kind: STEPS for kind in COST} | {"norm": TOKENS // TILE}
+    actions, copies, balance, flips = {}, {}, Balance(), {}
+    for kind, unit in stages:
+        if unit is None:
+            continue
+        l, u = unit
+        for c in range(3):
+            flips[l, u, c] = rs.flips(balance, c)
+            got, sent = rs.plan(unit, c, flips[l, u, c])
+            copies |= sent
+            actions |= {a: v for a, v in got.items()}
+            if l:
+                actions[(unit, c), "free"] = ([("action", ((unit, c), "end", DIRECT))], [], TURN)
+    slots = place(actions, copies, [(i, COST[kind], length[kind], unit) for i, (kind, unit) in enumerate(stages)])
+
+    def kernel(mid1_ref, dg1_ref, du1_ref, h1_ref, dy_ref, at1_ref, at0_ref, wg_ref, wu_ref, wd_ref, g0_ref, u0_ref, out, mid0_ref, dg0_ref, du0_ref, dyv, at, X, Mb, Db, Wb, Vb, one, pair, rsc):
+        me = torus.me()
+        it = rs.bind(me, rsc)
+        copy = pltpu.make_async_copy
+        sem_dy, sem_at = one.at[0], one.at[1]
+        load_dy, load_at = copy(dy_ref, dyv, sem_dy), copy(at1_ref, at, sem_at)
+        load_dy.start()
+        load_at.start()
+
+        def part(i):
+            return pl.ds(i * TILE, TILE)
+
+        def fetches(stage):
+            kind, unit = stages[stage]
+            layer = unit[0] if unit else 0
+            src = {"mid": (mid0_ref, mid1_ref)[layer], 0: (dg0_ref, dg1_ref)[layer], 1: (du0_ref, du1_ref)[layer]}
+
+            def of(t, s):
+                if kind == "down":
+                    return [copy(src["mid"].at[part(t)], Mb.at[s], pair.at[0, s])]
+                if kind == "side":
+                    return [copy(src[unit[1]].at[t], Db.at[s, :, part(0)], pair.at[1, s])]
+                if kind == "da":
+                    return [
+                        copy(dg1_ref.at[t], Db.at[s, :, part(0)], pair.at[1, s]),
+                        copy(du1_ref.at[t], Db.at[s, :, part(1)], pair.at[2, s]),
+                        copy(wg_ref.at[:, part(t)], Wb.at[s, :, part(0)], pair.at[3, s]),
+                        copy(wu_ref.at[:, part(t)], Wb.at[s, :, part(1)], pair.at[4, s]),
+                    ]
+                if kind == "norm":
+                    return [copy(h1_ref.at[part(t)], Vb.at[s], pair.at[5, s])]
+                out = [copy(wd_ref.at[part(t)], Vb.at[s], pair.at[5, s])]
+                for k, ref in enumerate((g0_ref, u0_ref)):
+                    out.append(copy(ref.at[pl.ds(t * LT * TOKENS, LT * TOKENS)], X.at[pl.ds((s * 2 + k) * LT * TOKENS, LT * TOKENS)], pair.at[6 + k, s]))
+                return out
+
+            return of
+
+        def saves(t, s):
+            return [copy(Mb.at[s], mid0_ref.at[part(t)], pair.at[0, s]), copy(Db.at[s, :, part(0)], dg0_ref.at[t], pair.at[1, s]), copy(Db.at[s, :, part(1)], du0_ref.at[t], pair.at[2, s])]
+
+        def tile(stage, t, s):
+            kind, unit = stages[stage]
+            if kind == "down":
+                got = dot(Mb[s], dyv[...])
+                for ct in range(D // LANES):
+                    X[pl.ds(ct * STRIDE[DOWN] + 8 + t * TILE, TILE), :] = got[:, ct * LANES : (ct + 1) * LANES]
+            elif kind == "side":
+                got = dot(at[...], Db[s, :, part(0)])
+                for k in range(LT):
+                    X[pl.ds((t * LT + k) * STRIDE[0] + 8, D), :] = got[:, k * LANES : (k + 1) * LANES]
+            elif kind == "da":
+                for r in range(0, TOKENS, PART):
+                    got = dot(Db[s, pl.ds(r, PART), :], Wb[s], NT)
+                    for ct in range(D // LANES):
+                        rows = pl.ds(ct * TOKENS + r, PART)
+                        X[rows, :] = jnp.where(t == 0, 0.0, X[rows, :]) + got[:, ct * LANES : (ct + 1) * LANES]
+            elif kind == "norm":
+                da = jnp.concatenate([X[pl.ds(ct * TOKENS + t * TILE, TILE), :] for ct in range(D // LANES)], axis=1).astype(BF16).astype(F32)
+                wide = Vb[s].astype(F32)
+                scale = scale_of(wide)
+                inner = jnp.mean(da * wide, -1, keepdims=True)
+                dyv[part(t), :] = dyv[part(t), :] + (scale * da - wide * (scale * scale * scale * inner)).astype(BF16)
+            else:
+                for r in range(0, TOKENS, PART):
+                    rows = pl.ds(r, PART)
+                    d = dot(dyv[rows, :], Vb[s], NT).astype(BF16).astype(F32)
+                    gate, up = (jnp.concatenate([X[pl.ds(((s * 2 + k) * LT + j) * TOKENS + r, PART), :] for j in range(LT)], axis=1) for k in range(2))
+                    mid, Db[s, rows, part(0)], Db[s, rows, part(1)] = hidden_back(gate, up, d)
+                    Mb[s, :, rows] = mid.T
+
+        def act(a):
+            ((l, u), c), what = a[0], a[1:]
+            flip = flips[l, u, c]
+            if what[0] == "free":
+                it.wait_sends(u, c, flip)
+                it.give_credit(u, c)
+                return
+            if what[0] == "start" and l == 0:
+                it.take_credit(u, c)
+
+            def store(value):
+                out[l, u, c] = value
+
+            it.run(u, c, flip, what, store)
+
+        def begin(stage):
+            for f in fetches(stage)(0, 0):
+                f.start()
+
+        begin(0)
+        barrier(torus, me, rs.peers())
+        load_dy.wait()
+        load_at.wait()
+        for stage, (kind, unit) in enumerate(stages):
+            count = length[kind]
+            ahead = stage + 1 < len(stages) and stages[stage + 1][0] != "hidden" and kind != "hidden"
+            of = fetches(stage)
+            if kind == "da":
+                copy(at0_ref, at, sem_at).start()
+            if unit == (0, 0):
+                copy(at0_ref, at, sem_at).wait()
+
+            def body(t, carry, stage=stage, kind=kind, of=of, count=count, ahead=ahead):
+                s = lax.rem(t, 2)
+                for f in of(t, s):
+                    f.wait()
+
+                @pl.when(t + 1 < count)
+                def _():
+                    for f in of(t + 1, 1 - s):
+                        f.start()
+
+                if ahead:
+
+                    @pl.when(t == count - 1)
+                    def _():
+                        begin(stage + 1)
+
+                if kind == "hidden":
+
+                    @pl.when(t > 1)
+                    def _():
+                        for f in saves(t - 2, s):
+                            f.wait()
+
+                tile(stage, t, s)
+                if kind == "hidden":
+                    for f in saves(t, s):
+                        f.start()
+                for k in range(count):
+                    if slots[stage, k]:
+
+                        @pl.when(t == k)
+                        def _(k=k):
+                            for a in slots[stage, k]:
+                                act(a)
+
+                return carry
+
+            lax.fori_loop(0, count, body, 0)
+            if kind == "hidden":
+                for t in (count - 2, count - 1):
+                    for f in saves(t, t % 2):
+                        f.wait()
+            if kind == "hidden" or stages[min(stage + 1, len(stages) - 1)][0] == "hidden":
+                begin(stage + 1)
+            if unit:
+                for a in slots[stage, "before"]:
+                    act(a)
+                u = unit[1]
+                pack(torus, u, X, STRIDE[u], [T.at[u] for T in it.T])
+            for a in slots[stage, "after"]:
+                act(a)
+        for u in range(3):
+            for c in range(3):
+                it.wait_sends(u, c, flips[0, u, c])
+
+    any_space = pl.BlockSpec(memory_space=pl.ANY)
+    flops = 2 * TOKENS * D * FF * 9
+    return pl.pallas_call(
+        kernel,
+        out_shape=[jax.ShapeDtypeStruct((LAYERS, 3, 3, CHUNK, LANES), F32), jax.ShapeDtypeStruct(mid1.shape, BF16), jax.ShapeDtypeStruct(dgate1.shape, BF16), jax.ShapeDtypeStruct(dup1.shape, BF16)],
+        in_specs=[any_space] * 12,
+        out_specs=[pl.BlockSpec(memory_space=pltpu.VMEM)] + [any_space] * 3,
+        scratch_shapes=[
+            pltpu.VMEM((TOKENS, D), BF16),
+            pltpu.VMEM((D, TOKENS), BF16),
+            pltpu.VMEM((FF // LANES * STRIDE[0], LANES), F32),
+            pltpu.VMEM((2, TILE, TOKENS), BF16),
+            pltpu.VMEM((2, TOKENS, 2 * TILE), BF16),
+            pltpu.VMEM((2, D, 2 * TILE), BF16),
+            pltpu.VMEM((2, TILE, D), BF16),
+            pltpu.SemaphoreType.DMA((2,)),
+            pltpu.SemaphoreType.DMA((8, 2)),
+            rs.scratch(),
+        ],
+        compiler_params=pltpu.CompilerParams(collective_id=collective_id, has_side_effects=True, vmem_limit_bytes=VMEM_ALL),
+        cost_estimate=pl.CostEstimate(flops=flops, bytes_accessed=TOKENS * FF * 20, transcendentals=0),
+        name="backward",
+    )(mid1, dgate1, dup1, h1, dy, at1, at0, wg1, wu1, wd0, gate0.reshape(-1, LANES), up0.reshape(-1, LANES))[0]
 
 
 def solution(mesh):
@@ -732,21 +976,9 @@
 
     def step(x, dy, wg, wu, wd, mg, mu, md, vg, vu, vd):
         x, dy = x[0], dy[0]
-        a0, _, _ = normed(x)
-        mid0, act0, up0, slope0 = hidden(a0, wg[0], wu[0])
-        h1 = x + dot(mid0, wd[0], ((1,), (0,))).astype(BF16)
-        a1, wide1, scale1 = normed(h1)
-        mid1, act1, up1, slope1 = hidden(a1, wg[1], wu[1])
-        dmid1 = dot(dy, wd[1], ((1,), (1,))).astype(BF16).astype(F32)
-        dgate1, dup1 = hidden_back(dmid1, act1, up1, slope1)
-        t1 = [weight_terms(torus, 0, a1, dgate1), weight_terms(torus, 1, a1, dup1), weight_terms(torus, 2, mid1, dy)]
-        da = (dot(dgate1, wg[1], ((1,), (1,))) + dot(dup1, wu[1], ((1,), (1,)))).astype(BF16).astype(F32)
-        inner = jnp.mean(da * wide1, -1, keepdims=True)
-        dh = dy + (scale1 * da - wide1 * (scale1 * scale1 * scale1 * inner)).astype(BF16)
-        dmid0 = dot(dh, wd[0], ((1,), (1,))).astype(BF16).astype(F32)
-        dgate0, dup0 = hidden_back(dmid0, act0, up0, slope0)
-        t0 = [weight_terms(torus, 0, a0, dgate0), weight_terms(torus, 1, a0, dup0), weight_terms(torus, 2, mid0, dh)]
-        g = reduce_scatter(torus, [t1, t0], CHUNK, 1)[::-1]
+        gate0, up0, h1, a1, at1, at0 = forward(x, wg[0], wu[0], wd[0])
+        mid1, dgate1, dup1 = last_layer(a1, dy, wg[1], wu[1], wd[1])
+        g = backward(torus, mid1, dgate1, dup1, h1, dy, at1, at0, wg[1], wu[1], wd[0], gate0, up0, 1)
         p = lax.axis_index("dp")
         mine = [lax.dynamic_slice_in_dim(w, p * HIGH[u], HIGH[u], 1).astype(F32) for u, w in enumerate((wg, wu, wd))]
         G, m, v = step_and_gather(torus, g, mine, (mg, mu, md), (vg, vu, vd), count, 2)

time: 619 us -> 492 us (0.79); the launches traced: 609 us -> 490 us
  matrix products: 186 us -> 0 us
  Pallas kernels: 402 us -> 457 us
  local copies, waits for them, and re-layouts: 7.65 us -> 30.6 us
  other arithmetic: 11.4 us -> 1.99 us
    dot_general x9 -> x0, matrix products: 186 us -> none  [dot(): return lax.dot_general(a, b, (dims, ((), ())), preferred_element_type=F32)]
    pallas_call x7 -> x3, Pallas kernels: 255 us -> 299 us  [the longest x1 208 us: backward(): pl.pallas_call(kernel, out_shape=[jax.ShapeDtypeStruct((LAYERS, 3, 3, CHU...]
    squeeze x0 -> x2, local copies, waits for them, and re-layouts: none -> 18.5 us  [step(): mid1, dgate1, dup1 = last_layer(a1, dy, wg[1], wu[1], wd[1])]
    pallas_call x1, Pallas kernels: 133 us -> 144 us  [step_and_gather(): pl.pallas_call(kernel, out_shape=[pltpu.MemorySpace.VMEM(s.shape, s.dtype...]
where the time goes in v2:
time: 492 us; the launch traced here: 490 us
  Pallas kernels  457 us (93%)
  local copies, waits for them, and re-layouts  30.6 us (6%)
    pallas_call x1, Pallas kernels, backward(): pl.pallas_call(kernel, out_shape=[jax.ShapeDtypeStruct((LAYERS, 3, 3, CHU...  208 us
    pallas_call x1, Pallas kernels, step_and_gather(): pl.pallas_call(kernel, out_shape=[pltpu.MemorySpace.VMEM(s.shape, s.dtype...  144 us
    pallas_call x1, Pallas kernels, forward(): pl.pallas_call(kernel, grid=(steps,), out_shape=[jax.ShapeDtypeStruct((FF...  49.4 us
    pallas_call x1, Pallas kernels, last_layer(): pl.pallas_call(kernel, grid=(steps,), out_shape=[jax.ShapeDtypeStruct((FF...  41.3 us
    squeeze x2, local copies, waits for them, and re-layouts, step(): mid1, dgate1, dup1 = last_layer(a1, dy, wg[1], wu[1], wd[1])  18.5 us
    pallas_call x1, Pallas kernels, unpack(): pl.pallas_call(kernel, grid=(LAYERS, groups), out_shape=[jax.ShapeDtypeSt...  14.2 us
    unnamed x16, local copies, waits for them, and re-layouts  12.2 us

profile of v2, /device:TPU:8, one launch (start us, length us, event | category | flops | bytes accessed | tf_op | source)
XLA Modules:
  0.0 490.4 jit_solution(7256695093320106011)
XLA Ops:
  0.6 0.0 copy-start.1
  0.7 14.3 %slice_bitcast_fusion.1 = (bf16[896,2560]{1,0:T(8,128)(2,1)}, bf16[896,2560]{1,0:T(8,128)(2,1)}, bf16[896,2560]{1,0:T(8,128)(2,1)}, bf16[896,2560]{1,0:T(8,128)(2,1)}) fusion(bf16[2,896,2560]{2,1,0:T(8,128)(2,1)} %param.14, bf16[2,896,2560]{2,1,0:T(8,128)(2,1)} %param.13), kind=kLoop, calls=%fused_computation.1 | loop fusion | bytes 36700160 | tf_op jit(solution)/shard_map/squeeze | solution.py:980
  14.9 1.0 copy-done.1
  15.9 4.2 slice_bitcast_fusion
  20.1 49.4 %forward.1 = (f32[20,2048,128]{2,1,0:T(8,128)}, f32[20,2048,128]{2,1,0:T(8,128)}, bf16[2048,896]{1,0:T(8,128)(2,1)}, bf16[2048,896]{1,0:T(8,128)(2,1)}, bf16[896...) custom-call(bf16[2048,896]{1,0:T(8,128)(2,1)} %bitcast.16, bf16[896,2560]{1,0:T(8,128)(2,1)} %get-tuple-element.68.wg_ref, ...), custom_call_target="tpu_custom_call" | custom-call | flops 28185722880 | bytes 52428800 | tf_op jit(solution)/shard_map/forward/pallas_call | solution.py:718
  69.5 41.3 %last_layer.1 = (bf16[2560,2048]{1,0:T(8,128)(2,1)}, bf16[10,2048,256]{2,1,0:T(8,128)(2,1)}, bf16[10,2048,256]{2,1,0:T(8,128)(2,1)}) custom-call(bf16[2048,896]{1,0:T(8,128)(2,1)} %get-tuple-element.31.a_ref, bf16[2048,896]{1,0:T(8,128)(2,1)} %bitcast.17, bf16[896,2560]{1,0:T(8,128)(2,1)} %get-tuple-element.69.wg_ref, ...), custom_call_target="tpu_custom_call" | custom-call | flops 28185722880 | bytes 31457280 | tf_op jit(solution)/shard_map/last_layer/pallas_call | solution.py:753
  110.8 208.4 %backward.1 = (f32[2,3,3,48,128]{4,3,2,1,0:T(8,128)}, bf16[2560,2048]{1,0:T(8,128)(2,1)}, bf16[10,2048,256]{2,1,0:T(8,128)(2,1)}, bf16[10,2048,256]{2,1,0:T(8,128)(2,1)}) custom-call(bf16[2560,2048]{1,0:T(8,128)(2,1)} %get-tuple-element.32.mid1_ref, bf16[10,2048,256]{2,1,0:T(8,128)(2,1)} %get-tuple-element.33.dg1_ref, ...), custom_call_target="tpu_custom_call" | custom-call | flops 84557168640 | bytes 104857600 | tf_op jit(solution)/shard_map/backward/pallas_call | solution.py:950
  319.2 1.1 dynamic-slice_convert_fusion.1
  320.2 0.9 dynamic-slice_convert_fusion.refs_2_
  321.2 0.9 copy.22.refs_5_
  322.1 0.9 copy.25.refs_8_
  323.0 0.9 copy.20.refs_3_
  324.0 0.9 copy.21.refs_4_
  324.9 0.9 copy.23.refs_6_
  325.9 0.9 copy.24.refs_7_
  326.8 0.0 copy-start
  326.8 1.0 copy-done
  327.8 143.8 %step_and_gather.1 = (bf16[8,16,2,3,48,128]{5,4,3,2,1,0:T(8,128)(2,1)S(1)}, bf16[4,32,2,3,48,128]{5,4,3,2,1,0:T(8,128)(2,1)S(1)}, bf16[4,32,2,3,48,128]{5,4,3,2,...) custom-call(f32[2,3,3,48,128]{4,3,2,1,0:T(8,128)S(1)} %copy-done, ...), custom_call_target="tpu_custom_call" | custom-call | tf_op jit(solution)/shard_map/step_and_gather/pallas_call | solution.py:604
  471.6 14.2 %unpack.1 = (bf16[2,896,2560]{2,1,0:T(8,128)(2,1)}, bf16[2,896,2560]{2,1,0:T(8,128)(2,1)}, bf16[2,2560,896]{2,1,0:T(8,128)(2,1)}) custom-call(bf16[8,16,2,3,48,128]{5,4,3,2,1,0:T(8,128)(2,1)S(1)} %get-tuple-element.41.g0, bf16[4,32,2,3,48,128]{5,4,3,2,1,0:T(8,128)(2,1)S(1)} %get-tuple-element.42.g1, bf16[4,32,2,3,48,128]{5,4,3,2,1,0:T(8,128)(2,1)S(1)} %get-tuple-element.43.g2), custom_call_target="tpu_custom_call" | custom-call | tf_op jit(solution)/shard_map/unpack/pallas_call | solution.py:653
  485.8 0.8 copy.26
  486.6 0.8 copy.27
  487.4 0.7 copy.28
  488.1 0.8 copy.29
  488.9 0.8 copy.30
  489.7 0.7 copy.31
Async XLA Ops:
  0.6 15.3 %copy-start.1 = (bf16[2,2560,896]{2,1,0:T(8,128)(2,1)S(1)}, bf16[2,2560,896]{2,1,0:T(8,128)(2,1)}, u32[]{:S(2)}) copy-start(bf16[2,2560,896]{2,1,0:T(8,128)(2,1)} %param.15) | copy-start | bytes 27525124
  326.8 1.0 copy-start

commit v3 on v2

v3 whole, which is shorter than its diff:
```python
import heapq
import jax
import jax.numpy as jnp
from jax import lax
from jax.experimental import pallas as pl
from jax.experimental.pallas import tpu as pltpu

F32, BF16 = jnp.float32, jnp.bfloat16
MESH = pl.DeviceIdType.MESH
RATE, LATENCY = 46.6e3, 2.3
TURN, ADD, HOP = 0.1, 2.0e6, 0.7
WAYS = (1, -1)
RING, CROSS, DIRECT = range(3)
NEVER, MARGIN, SWEEPS = 1e9, 0.5, 2


class Torus:
    def __init__(self, nx, ny, nz):
        self.n = {"x": nx, "y": ny, "z": nz}
        self.size = nx * ny * nz

    def here(self):
        return Here(self)


class Here:
    def __init__(self, torus):
        p, n = lax.axis_index("dp"), torus.n
        ny, nz = n["y"], n["z"]
        mine = {"z": lax.rem(p, nz), "y": lax.rem(lax.div(p, nz), ny), "x": lax.div(p, ny * nz)}
        step = {"z": 1, "y": nz, "x": ny * nz}
        self.at = {d: [mine[d]] + [lax.rem(mine[d] + i, n[d]) for i in range(1, n[d])] for d in n}
        self.to = {d: [p + (self.at[d][i] - mine[d]) * step[d] for i in range(n[d])] for d in n}

    def peer(self, dim, delta):
        return {"dp": self.to[dim][delta % len(self.to[dim])]}

    def up(self, dim, delta):
        return self.at[dim][delta % len(self.at[dim])]


ORDERS = ("zxy", "xyz", "yxz")


def hops(n, flip):
    far, near = n // 2, n - 1 - n // 2
    return {1: near, -1: far} if flip else {1: far, -1: near}


class Balance:
    def __init__(self):
        self.load = {}

    def flip(self, dim, n, size):
        plain = [self.load.get((dim, s), 0) + size * hops(n, False)[s] for s in WAYS]
        turned = [self.load.get((dim, s), 0) + size * hops(n, True)[s] for s in WAYS]
        flip = max(turned) < max(plain)
        self.load[dim, 1], self.load[dim, -1] = turned if flip else plain
        return flip


def simulate(actions, copies):
    links, arrived, order = {}, {}, []
    waiting = {a: set(needs) for a, (needs, _, _, _) in actions.items()}
    by_need = {}
    for a, (needs, _, _, _) in actions.items():
        for c in needs:
            by_need.setdefault(c, []).append(a)
    ready = [(actions[a][3], i, a) for i, a in enumerate(actions) if not waiting[a]]
    rank = {a: i for i, a in enumerate(actions)}
    heapq.heapify(ready)
    now, done = 0.0, {}
    while ready:
        at, _, a = heapq.heappop(ready)
        now = max(now, at) + actions[a][2]
        order.append(a)
        done[a] = now
        for c in [("action", a)] + list(actions[a][1]):
            if c[0] == "action":
                end = now
            else:
                link, size, extra = copies[c]
                start = max(now, links.get(link, 0.0))
                links[link] = start + size / RATE
                end = links[link] + LATENCY + extra
            for b in by_need.get(c, ()):
                waiting[b].discard(c)
                arrived[b] = max(arrived.get(b, 0.0), end)
                if not waiting[b]:
                    heapq.heappush(ready, (max(arrived[b], actions[b][3]), rank[b], b))
    assert len(order) == len(actions), (len(order), len(actions))
    return order, now


def place(actions, copies, segments):
    links, known, left, slots, open_keys = {}, {}, dict(actions), {}, set()
    now = 0.0

    def do(a, where):
        nonlocal now
        _, sends, cost = left.pop(a)
        now += cost
        known["action", a] = now
        for c in sends:
            link, size, extra = copies[c]
            links[link] = max(now, links.get(link, 0.0)) + size / RATE
            known[c] = links[link] + LATENCY + extra
        where.append(a)

    def drain(where, allowed, wait):
        nonlocal now
        while True:
            able = [(max([known.get(c, NEVER) for c in actions[a][0]], default=0.0), i, a) for i, a in enumerate(left) if allowed(a)]
            best, _, a = min(able, default=(NEVER, 0, None))
            if best >= NEVER or not wait and best + MARGIN > now:
                return
            now = max(now, best)
            do(a, where)

    for key, cost, writes, whole in segments:
        now += cost
        slots[key] = ([], [])
        others = {(l, u, c) for (l, u), c in writes}
        drain(slots[key][0], lambda a: any(a[0][0][1] == u and a[0][1] == c and a[0][0][0] > l for l, u, c in others), True)
        open_keys |= set(whole)
        drain(slots[key][1], lambda a: a[1] != "start" or a[0] in open_keys, False)
    drain(slots[segments[-1][0]][1], lambda a: True, True)
    assert not left
    place.took = now
    return slots


def barrier(me, peers):
    sem = pltpu.get_barrier_semaphore()
    for dim, delta in peers:
        pl.semaphore_signal(sem, inc=1, device_id=me.peer(dim, delta), device_id_type=MESH)
    pl.semaphore_wait(sem, len(peers))


def both_ways(torus, dim):
    n = torus.n[dim]
    return [] if n == 1 else [(dim, 1)] if n == 2 else [(dim, 1), (dim, -1)]


def all_others(torus, dim):
    return [(dim, d) for d in range(1, torus.n[dim])]


class ReduceScatter:
    LANES = (2, 1, 1)

    def __init__(self, torus, rows, units):
        self.t, self.rows, self.units = torus, rows, units
        self.dims = [tuple(order) for order in ORDERS]
        self.nslots = max(self.base(c, DIRECT, 0) + self.sizes(c)[DIRECT] - 1 for c in range(3))

    def sizes(self, c):
        return [self.t.n[d] for d in self.dims[c]]

    def here(self, c):
        return [self.me.up(d, 0) for d in self.dims[c]]

    def base(self, c, phase, lane):
        n = self.sizes(c)
        return sum((n[i] - 1) * self.LANES[i] for i in range(phase)) + lane * (n[phase] - 1)

    def peers(self):
        full = {dims[DIRECT] for dims in self.dims}
        out = []
        for dim in "xyz":
            out += all_others(self.t, dim) if dim in full else both_ways(self.t, dim)
        return out

    def credit_peers(self, c):
        a, b, d = self.dims[c]
        return both_ways(self.t, a) + both_ways(self.t, b) + all_others(self.t, d)

    def scratch(self):
        n = self.t.n
        t, r1, r2, r3, k2, k3 = [], [], [], [], [], []
        for dims in self.dims:
            n1, n2, n3 = (n[d] for d in dims)
            tail = (self.rows, 128)
            t.append(pltpu.VMEM((self.units, n1, n2 * n3) + tail, BF16))
            r1.append(pltpu.VMEM((self.units, max(n1 - 1, 1), n2 * n3) + tail, BF16))
            r2.append(pltpu.VMEM((self.units, max(n2 - 1, 1), n3) + tail, BF16))
            r3.append(pltpu.VMEM((self.units, max(n3 - 1, 1)) + tail, BF16))
            k2.append(pltpu.VMEM((self.units, n3) + tail, F32))
            k3.append(pltpu.VMEM((self.units,) + tail, F32))
        sems = [pltpu.SemaphoreType.DMA((self.units, 3, self.nslots)), pltpu.SemaphoreType.DMA((self.units, 3, self.nslots)), pltpu.SemaphoreType.REGULAR((self.units, 3))]
        return [t, r1, r2, r3, k2, k3] + sems

    def slot(self, c, phase, sign, h):
        return h if sign > 0 else self.sizes(c)[phase] - 2 - h

    def flips(self, balance, c):
        n1, n2, n3 = self.sizes(c)
        block, (a, b, d) = self.rows * 256, self.dims[c]
        for rel in range(1, n3):
            link = d, 1 if rel <= n3 // 2 else -1
            balance.load[link] = balance.load.get(link, 0) + block * min(rel, n3 - rel)
        ring = [balance.flip(a, n1, block * n2 * n3 // self.LANES[RING]) for _ in range(self.LANES[RING])]
        return ring, [balance.flip(b, n2, block * n3)]

    def plan(self, unit, c, flip):
        n = self.sizes(c)
        n1, n2, n3 = n
        block = self.rows * 256
        size = [block * n2 * n3 // self.LANES[RING], block * n3, block]
        actions, copies = {}, {}
        key = (unit, c)

        def send(phase, lane, sign, h):
            cid = ("copy", key, phase, lane, sign, h)
            copies[cid] = ((self.dims[c][phase], sign), size[phase], 0)
            return cid

        first, last = [[], []], [[], []]
        for phase in (RING, CROSS):
            for lane, turned in enumerate(flip[phase]):
                k = hops(n[phase], turned)
                ways = [s for s in WAYS if k[s]]
                first[phase] += [send(phase, lane, s, k[s] - 1) for s in ways]
                last[phase] += [("copy", key, phase, lane, s, 0) for s in ways]
                for s in ways:
                    for h in range(k[s] - 1, 0, -1):
                        actions[key, "step", phase, lane, s, h] = ([("copy", key, phase, lane, s, h)], [send(phase, lane, s, h - 1)], size[phase] / ADD)
        direct = []
        for rel in range(1, n3):
            cid = ("copy", key, DIRECT, 0, 0, rel)
            far = min(rel, n3 - rel)
            copies[cid] = ((self.dims[c][DIRECT], 1 if rel <= n3 // 2 else -1), size[DIRECT] * far, HOP * (far - 1))
            direct.append(cid)
        sends = first + [direct, []]
        actions[key, "start"] = ([], sends[RING], TURN)
        before = (key, "start")
        for phase, needs in enumerate(last + [direct]):
            a = (key, "end", phase)
            actions[a] = (needs + [("action", before)], sends[phase + 1], size[phase] * self.LANES[phase] / ADD + TURN)
            before = a
        return actions, copies

    def bind(self, me, refs):
        self.me, (self.T, self.R1, self.R2, self.R3, self.K2, self.K3, self.ssem, self.rsem, self.credit) = me, refs
        return self

    def remote(self, u, c, phase, lane, sign, h):
        n1, n2, n3 = self.sizes(c)
        d1, d2, d3 = self.dims[c]
        up = self.me.up
        mine = self.T[c].at[u]
        slot = h - 1 if phase == DIRECT else self.slot(c, phase, sign, h)
        if phase == RING:
            part = n2 * n3 // self.LANES[RING]
            blocks = pl.ds(lane * part, part)
            src, dst = mine.at[up(d1, sign * (h + 1)), blocks], self.R1[c].at[u, slot, blocks]
        elif phase == CROSS:
            src, dst = mine.at[up(d1, 0), pl.ds(up(d2, sign * (h + 1)) * n3, n3)], self.R2[c].at[u, slot]
        else:
            sign = h
            src, dst = mine.at[up(d1, 0), up(d2, 0) * n3 + up(d3, h)], self.R3[c].at[u, slot]
        s = self.base(c, phase, lane) + slot
        to = self.me.peer(self.dims[c][phase], sign)
        return pltpu.make_async_remote_copy(src_ref=src, dst_ref=dst, send_sem=self.ssem.at[u, c, s], recv_sem=self.rsem.at[u, c, s], device_id=to, device_id_type=MESH)

    def all_sends(self, c, flip):
        n = self.sizes(c)
        out = []
        for phase in (RING, CROSS):
            for lane, turned in enumerate(flip[phase]):
                k = hops(n[phase], turned)
                out += [(phase, lane, s, h) for s in WAYS for h in range(k[s])]
        return out + [(DIRECT, 0, 0, rel) for rel in range(1, n[DIRECT])]

    def run(self, u, c, flip, what, store):
        n = self.sizes(c)
        n1, n2, n3 = n
        m1, m2, m3 = self.here(c)
        T, R1, R2, R3 = (r[c].at[u] for r in (self.T, self.R1, self.R2, self.R3))
        K2, K3 = self.K2[c].at[u], self.K3[c].at[u]
        mine = T.at[m1]
        wide = lambda v: v.astype(F32)
        go = lambda *a: self.remote(u, c, *a)

        def loop(count, body):
            def one(i, carry):
                body(i)
                return carry

            lax.fori_loop(0, count, one, 0, unroll=2 - count % 2)

        def ways(phase):
            for lane, turned in enumerate(flip[phase]):
                k = hops(n[phase], turned)
                for s in WAYS:
                    if k[s]:
                        yield lane, s, k[s]

        def sends(phase):
            for lane, s, k in ways(phase):
                go(phase, lane, s, k - 1).start()

        def arrived(phase):
            got = set()
            for lane, s, _ in ways(phase):
                go(phase, lane, s, 0).wait_recv()
                got.add(self.slot(c, phase, s, 0))
            return sorted(got)

        kind, *where = what
        if kind == "start":
            sends(RING)
        elif kind == "step":
            phase, lane, s, h = where
            go(*where).wait_recv()
            slot = self.slot(c, phase, s, h)
            q = self.me.up(self.dims[c][phase], s * h)
            part = n2 * n3 // self.LANES[RING]

            def ring(i):
                b = lane * part + i
                T[q, b] = (wide(T[q, b]) + wide(R1[slot, b])).astype(BF16)

            def cross(i):
                b = q * n3 + i
                mine[b] = (wide(mine[b]) + wide(R2[slot, i])).astype(BF16)

            loop(part if phase == RING else n3, cross if phase else ring)
            go(phase, lane, s, h - 1).start()
        elif where == [RING]:
            got = arrived(RING)

            def total(b):
                return sum((wide(R1[g, b]) for g in got), wide(mine[b]))

            def own(i):
                K2[i] = total(m2 * n3 + i)

            def others(i):
                b = lax.rem((m2 + 1) * n3 + i, n2 * n3)
                mine[b] = total(b).astype(BF16)

            loop((n2 - 1) * n3, others)
            sends(CROSS)
            loop(n3, own)
        elif where == [CROSS]:
            got = arrived(CROSS)

            def total(q):
                return sum((wide(R2[g, q]) for g in got), K2[q])

            for rel in range(1, n3):
                q = self.me.up(self.dims[c][DIRECT], rel)
                mine[m2 * n3 + q] = total(q).astype(BF16)
            for rel in range(1, n3):
                go(DIRECT, 0, 0, rel).start()
            K3[...] = total(m3)
        else:
            for rel in range(1, n3):
                go(DIRECT, 0, 0, rel).wait_recv()
            store(sum((wide(R3[i]) for i in range(n3 - 1)), K3[...]).astype(BF16).astype(F32))

    def wait_sends(self, u, c, flip):
        for a in self.all_sends(c, flip):
            self.remote(u, c, *a).wait_send()

    def give_credit(self, u, c):
        for dim, delta in self.credit_peers(c):
            pl.semaphore_signal(self.credit.at[u, c], inc=1, device_id=self.me.peer(dim, delta), device_id_type=MESH)

    def take_credit(self, u, c):
        pl.semaphore_wait(self.credit.at[u, c], len(self.credit_peers(c)))


class AllGather:
    def __init__(self, torus, block_bytes, split=2):
        self.t, self.bytes, self.split = torus, block_bytes, split
        self.dims = [tuple(order) for order in ORDERS]
        self.flip, self.balance = {}, Balance()
        self.build()
        for key in list(self.flip) * SWEEPS:
            took = self.took
            self.flip[key] = not self.flip[key]
            self.build()
            if self.took >= took:
                self.flip[key] = not self.flip[key]
        self.build()

    def build(self):
        self.copies, self.actions, self.index = {}, {}, {}
        for c in range(3):
            self.plan(c)
        self.order, self.took = simulate({a: (*v, 0) for a, v in self.actions.items()}, self.copies)

    def peers(self):
        return [p for dim in "xyz" for p in both_ways(self.t, dim)]

    def pieces(self, c, j):
        n3 = self.t.n[self.dims[c][DIRECT]]
        return n3 if not j else self.split if n3 % self.split == 0 else 1

    def size(self, c, phase, j):
        line = self.bytes * self.t.n[self.dims[c][DIRECT]]
        return self.bytes if phase == DIRECT else line // self.pieces(c, 1 if phase == CROSS else j)

    def k(self, c, phase, j, i):
        dim = self.dims[c][phase]
        key = (c, phase, j, i)
        if key not in self.flip:
            self.flip[key] = self.balance.flip(dim, self.t.n[dim], self.size(c, phase, j))
        return hops(self.t.n[dim], self.flip[key])

    def plan(self, c):
        n1, n2, n3 = (self.t.n[d] for d in self.dims[c])

        def send(where, s, h):
            phase, j, _ = where
            cid = (c, where, s, h)
            self.copies[cid] = ((self.dims[c][phase], s), self.size(c, phase, j), 0)
            self.index[cid] = len(self.index)
            return cid

        def own(*where):
            k = self.k(c, *where)
            return [send(where, s, 1) for s in WAYS if k[s]]

        def passing(*where):
            k = self.k(c, *where)
            for s in WAYS:
                for h in range(1, k[s] + 1):
                    yield s, h, (c, "pass", where, s, h), [(c, where, s, h)], [send(where, s, h + 1)] if h < k[s] else []

        def act(a, needs, sends):
            self.actions[a] = (needs, sends, TURN / 2)

        act((c, "start"), [], own(DIRECT, 0, 0) + own(RING, 0, 0))
        got = [("action", (c, "start"))]
        for s, h, a, needs, sends in passing(DIRECT, 0, 0):
            act(a, needs, sends + own(RING, 0, (-s * h) % n3))
            got.append(("action", a))
        parts = range(self.pieces(c, 1))
        act((c, "line"), got, [x for i in parts for x in own(CROSS, 0, i)])
        for i in parts:
            for s, h, a, needs, sends in passing(CROSS, 0, i):
                after = (-s * h) % n2, i
                if c:
                    act(a, needs, sends + own(RING, *after))
                else:
                    act(a, needs, sends)
                    act((c, "later", *after), [("action", x) for x in (a, (1, "line"), (2, "line"))], own(RING, *after))
        for j in range(n2):
            for i in range(self.pieces(c, j)):
                for _, _, a, needs, sends in passing(RING, j, i):
                    act(a, needs, sends)

    def bind(self, me, G, ssem, rsem):
        self.me, self.G, self.ssem, self.rsem = me, G, ssem, rsem
        return self

    def remote(self, cid, back):
        c, (phase, j, i), s, h = cid
        d1, d2, d3 = self.dims[c]
        n3, up = self.t.n[d3], self.me.up
        off = s * (back - h)
        G = self.G[c]
        if phase == DIRECT:
            ref = G.at[up(d1, 0), up(d2, 0) * n3 + up(d3, off)]
        elif phase == CROSS:
            size = n3 // self.pieces(c, 1)
            ref = G.at[up(d1, 0), pl.ds(up(d2, off) * n3 + i * size, size)]
        elif j == 0:
            ref = G.at[up(d1, off), up(d2, 0) * n3 + up(d3, i)]
        else:
            size = n3 // self.pieces(c, j)
            ref = G.at[up(d1, off), pl.ds(up(d2, j) * n3 + i * size, size)]
        x = self.index[cid]
        return pltpu.make_async_remote_copy(src_ref=ref, dst_ref=ref, send_sem=self.ssem.at[x], recv_sem=self.rsem.at[x], device_id=self.me.peer(self.dims[c][phase], s), device_id_type=MESH)

    def run(self, a):
        needs, sends, _ = self.actions[a]
        for cid in needs:
            if cid in self.index:
                self.remote(cid, 0).wait_recv()
        for cid in sends:
            self.remote(cid, 1).start()

    def wait_sends(self):
        for cid in self.copies:
            self.remote(cid, 1).wait_send()


MIB = 2**20
VMEM_ALL = 67043328
LAYERS, D, FF = 2, 896, 2560
LANES, ROWS, CHUNK = 128, 144, 48
HIGH = {0: 7, 1: 7, 2: 20}
WIDE = {0: FF, 1: FF, 2: D}
WINDOW = (16, 16, 24)


HALVES, RING_TILES = 2, 8
TOKENS, TILE, PART = 2048, 256, 512
LT, STEPS = TILE // LANES, FF // TILE
HALF = STEPS // HALVES


def home(u, ct):
    if u == HALVES:
        return u, ct
    t, k = divmod(ct, 2 * LT)
    m, j = divmod(k, LT)
    return m, (u * HALF + t) * LT + j


def tiles(u):
    high, wide = HIGH[u], WIDE[u] // LANES
    out = []
    for k in range(ROWS // 8):
        ct, row = divmod(8 * k, high)
        out.append((ct, row, min(8, high - row), ct + 1 < wide))
    return out


def owner_index(torus, c, i):
    ny, nz = torus.n["y"], torus.n["z"]
    at = {"z": lax.rem(i, nz), "y": lax.rem(lax.div(i, nz), ny), "x": lax.div(i, ny * nz)}
    n = torus.n
    a, b, d = ORDERS[c]
    return at[a], at[b] * n[d] + at[d]


def pack(torus, u, X, base, parts, first, count, outs):
    high = HIGH[u]
    sub = lax.broadcasted_iota(jnp.int32, (8, LANES), 0)

    def piece(i, ct, row, whole, more):
        a = X[pl.ds(base(ct) + high * i + row, 8), :]
        if whole == 8:
            return a
        b = X[pl.ds(base(ct + 1) + high * i - whole, 8), :] if more else jnp.zeros((8, LANES), F32)
        return jnp.where(sub < whole, a, b)

    got = tiles(u)

    def body(i, carry):
        at = [owner_index(torus, c, first + i) for c in range(3)]
        for j in parts:
            both = jnp.concatenate([piece(i, *got[2 * j]), piece(i, *got[2 * j + 1])], axis=0).astype(BF16)
            c, r = divmod(16 * j, CHUNK)
            outs[c][at[c][0], at[c][1], pl.ds(r, 16), :] = both
        return carry

    lax.fori_loop(0, count, body, 0, unroll=4)


def pieces_shapes(torus, dtype, *mid):
    out = []
    for order in ORDERS:
        a, b, d = (torus.n[x] for x in order)
        out.append(jax.ShapeDtypeStruct((a, b * d) + mid + (CHUNK, LANES), dtype))
    return out


def step_and_gather(torus, g, w, m, v, count, collective_id):
    ag = AllGather(torus, LAYERS * 3 * CHUNK * 256)
    dims = "zxy"
    slots = {d: torus.n[d] - 1 for d in dims}

    def window(p, x):
        rows = WINDOW[x]
        first = lax.div(p * HIGH[x], 8) * 8
        return pl.multiple_of(jnp.minimum(first, HIGH[x] * torus.size - rows), 8), rows

    def kernel(g_ref, *refs):
        w_in, m_in, v_in, G, m_out, v_out = (refs[i : i + 3] for i in range(0, 18, 3))
        flat, wflat, part, E, esend, erecv, ssem, rsem, win, wide_win, wsem = refs[18:]
        me = torus.here()
        p = lax.axis_index("dp")
        loads = []
        for x in range(3):
            first, rows = window(p, x)
            loads.append(pltpu.make_async_copy(w_in[x].at[:, pl.ds(first, rows)], win[x], wsem.at[x]))
            loads[x].start()
        barrier(me, [p for d in "xyz" for p in all_others(torus, d)])
        for x in range(3):
            loads[x].wait()
            for lt in range(WIDE[x] // LANES):
                wide_win[x][:, lt] = win[x][:, :, pl.ds(lt * LANES, LANES)].astype(F32)
        acc = jnp.zeros((8, LANES), F32)
        for l in range(LAYERS):
            for u in range(3):
                for c in range(3):
                    value = g_ref[l, u, c]
                    flat[l, u, pl.ds(c * CHUNK, CHUNK), :] = value
                    for r in range(0, CHUNK, 8):
                        acc = acc + value[r : r + 8] * value[r : r + 8]
        part[0] = acc
        base = 0
        for i, d in enumerate(dims):
            n = torus.n[d]
            copies = []
            for rel in range(1, n):
                s = base + rel - 1
                copies.append(pltpu.make_async_remote_copy(src_ref=part.at[i], dst_ref=E.at[s], send_sem=esend.at[s], recv_sem=erecv.at[s], device_id=me.peer(d, rel), device_id_type=MESH))
            for copy in copies:
                copy.start()
            total = part[i]
            for rel in range(1, n):
                copies[rel - 1].wait_recv()
                total = total + E[base + rel - 1]
            part[i + 1] = total
            for copy in copies:
                copy.wait_send()
            base += n - 1
        mean = jnp.sum(part[3], keepdims=True) / count
        factor = jnp.minimum(1.0, 0.5 * lax.rsqrt(mean + 1e-30))
        for l in range(LAYERS):
            for u in range(3):
                high = HIGH[u]
                wflat[l, u, pl.ds(ROWS - 8, 8), :] = jnp.zeros((8, LANES), F32)
                for ct in range(WIDE[u] // LANES):
                    x, lt = home(u, ct)
                    at = (slice(None), l, pl.ds(lt * LANES, LANES))
                    grad = flat[l, u, pl.ds(ct * high, high), :] * factor
                    new_m = 0.9 * m_in[x][at] + 0.1 * grad
                    new_v = 0.95 * v_in[x][at] + 0.05 * grad * grad
                    wide = wide_win[x][l, lt, pl.ds(p * high - window(p, x)[0], high), :]
                    new_w = wide - 0.02 * (new_m * lax.rsqrt(new_v + 1e-8) + 0.1 * wide)
                    m_out[x][at] = new_m
                    v_out[x][at] = new_v
                    wflat[l, u, pl.ds(ct * high, high), :] = new_w
        it = ag.bind(me, G, ssem, rsem)
        for c in range(3):
            n = [torus.n[d] for d in ORDERS[c]]
            at = [me.up(d, 0) for d in ORDERS[c]]
            for l in range(LAYERS):
                for u in range(3):
                    G[c][at[0], at[1] * n[2] + at[2], l, u] = wflat[l, u, pl.ds(c * CHUNK, CHUNK), :].astype(BF16)
        for a in ag.order:
            it.run(a)
        it.wait_sends()

    vmem = pl.BlockSpec(memory_space=pltpu.VMEM)
    nsum = sum(slots.values())
    shapes = pieces_shapes(torus, BF16, LAYERS, 3)
    turn = lambda ts: [jnp.transpose(t, (1, 0, 2)) for t in ts]
    m, v = turn(m), turn(v)
    f32 = [jax.ShapeDtypeStruct(t.shape, F32) for t in m]
    k = len(ag.copies)
    got = pl.pallas_call(
        kernel,
        out_shape=[pltpu.MemorySpace.VMEM(s.shape, s.dtype) for s in shapes] + f32 * 2,
        in_specs=[vmem] + [pl.BlockSpec(memory_space=pl.ANY)] * 3 + [vmem] * 6,
        out_specs=[vmem] * 9,
        scratch_shapes=[
            pltpu.VMEM((LAYERS, 3, ROWS, LANES), F32),
            pltpu.VMEM((LAYERS, 3, ROWS, LANES), F32),
            pltpu.VMEM((4, 8, LANES), F32),
            pltpu.VMEM((nsum, 8, LANES), F32),
            pltpu.SemaphoreType.DMA((nsum,)),
            pltpu.SemaphoreType.DMA((nsum,)),
            pltpu.SemaphoreType.DMA((k,)),
            pltpu.SemaphoreType.DMA((k,)),
            [pltpu.VMEM((LAYERS, WINDOW[x], WIDE[x]), BF16) for x in range(3)],
            [pltpu.VMEM((LAYERS, WIDE[x] // LANES, WINDOW[x], LANES), F32) for x in range(3)],
            pltpu.SemaphoreType.DMA((3,)),
        ],
        compiler_params=pltpu.CompilerParams(collective_id=collective_id, has_side_effects=True, vmem_limit_bytes=26 * MIB),
        name="step_and_gather",
    )(g, *w, *m, *v)
    return got[:3], turn(got[3:6]), turn(got[6:])


def unpack(torus, G):
    nx, ny, nz = (torus.n[d] for d in "xyz")
    pair = 2
    group = pair * nz
    groups = torus.size // group
    pairs = ny // pair

    def kernel(g0, g1, g2, *refs):
        outs, Z, Y = refs[:3], refs[3], refs[4]
        l, s = pl.program_id(0), pl.program_id(1)
        corner = {"x": lax.div(s, pairs), "y": lax.rem(s, pairs) * pair, "z": 0}
        for u in range(3):
            high, wide = HIGH[u], WIDE[u] // LANES
            for i in range(group):
                y, z = divmod(i, nz)
                at = corner | {"y": corner["y"] + y, "z": z}
                for c, ref in enumerate((g0, g1, g2)):
                    a, b, d = ORDERS[c]
                    Z[i, pl.ds(c * CHUNK, CHUNK), :] = ref[at[a], at[b] * torus.n[d] + at[d], l, u].astype(F32)
            for i in range(group):
                for ct in range(wide):
                    for r in range(0, high, 8):
                        Y[ct, pl.ds(high * i + r, 8), :] = Z[i, pl.ds(high * ct + r, 8), :]
            rows = high * group
            for ct in range(wide):
                x, lt = home(u, ct)
                outs[x][0, :, pl.ds(lt * LANES, LANES)] = Y[ct, pl.ds(0, rows), :].astype(BF16)

    shapes = [(LAYERS, HIGH[u] * torus.size, WIDE[u]) for u in range(3)]
    return pl.pallas_call(
        kernel,
        grid=(LAYERS, groups),
        out_shape=[jax.ShapeDtypeStruct(s, BF16) for s in shapes],
        in_specs=[pl.BlockSpec(memory_space=pltpu.VMEM)] * 3,
        out_specs=[pl.BlockSpec((1, HIGH[u] * group, WIDE[u]), lambda l, s: (l, s, 0)) for u in range(3)],
        scratch_shapes=[pltpu.VMEM((group, ROWS + 8, LANES), F32), pltpu.VMEM((FF // LANES, HIGH[2] * group + 8, LANES), F32)],
        compiler_params=pltpu.CompilerParams(vmem_limit_bytes=26 * MIB),
        name="unpack",
    )(*G)


NN, NT, TN = ((1,), (0,)), ((1,), (1,)), ((0,), (0,))


def dot(a, b, dims=NN):
    return lax.dot_general(a, b, (dims, ((), ())), preferred_element_type=F32)


def scale_of(wide):
    return lax.rsqrt(jnp.mean(wide * wide, -1, keepdims=True) + 1e-6)


def normed_into(h_ref, a_ref, t_ref):
    for r in range(0, TOKENS, TILE):
        wide = h_ref[pl.ds(r, TILE), :].astype(F32)
        a = (wide * scale_of(wide)).astype(BF16)
        a_ref[pl.ds(r, TILE), :] = a
        t_ref[:, pl.ds(r, TILE)] = a.T


def forward(x, wg, wu, wd):
    steps = STEPS

    def kernel(x_ref, wg_ref, wu_ref, wd_ref, gate_ref, up_ref, h_ref, a_ref, at_ref, xt_ref, xa, acc):
        t = pl.program_id(0)

        @pl.when(t == 0)
        def _():
            normed_into(x_ref, xa, xt_ref)
            acc[...] = jnp.zeros_like(acc)

        for r in range(0, TOKENS, PART):
            rows = pl.ds(r, PART)
            a = xa[rows, :]
            both = dot(a, jnp.concatenate([wg_ref[0], wu_ref[0]], axis=1))
            gate, up = both[:, :TILE], both[:, TILE:]
            for k in range(LT):
                lanes = slice(k * LANES, (k + 1) * LANES)
                gate_ref[k, rows, :] = gate[:, lanes]
                up_ref[k, rows, :] = up[:, lanes]
            mid = (jax.nn.silu(gate) * up).astype(BF16)
            acc[rows, :] += dot(mid, wd_ref[0])

        @pl.when(t == steps - 1)
        def _():
            for r in range(0, TOKENS, TILE):
                rows = pl.ds(r, TILE)
                h_ref[rows, :] = x_ref[rows, :] + acc[rows, :].astype(BF16)
            normed_into(h_ref, a_ref, at_ref)

    whole = pl.BlockSpec(memory_space=pltpu.VMEM)
    cols = pl.BlockSpec((1, D, TILE), lambda t: (0, 0, t))
    saved = pl.BlockSpec((LT, TOKENS, LANES), lambda t: (t, 0, 0))
    return pl.pallas_call(
        kernel,
        grid=(steps,),
        out_shape=[jax.ShapeDtypeStruct((FF // LANES, TOKENS, LANES), F32)] * 2 + [jax.ShapeDtypeStruct((TOKENS, D), BF16)] * 2 + [jax.ShapeDtypeStruct((D, TOKENS), BF16)] * 2,
        in_specs=[whole, cols, cols, pl.BlockSpec((1, TILE, D), lambda t: (0, t, 0))],
        out_specs=[saved] * 2 + [whole] * 4,
        scratch_shapes=[pltpu.VMEM((TOKENS, D), BF16), pltpu.VMEM((TOKENS, D), F32)],
        compiler_params=pltpu.CompilerParams(vmem_limit_bytes=60 * MIB),
        cost_estimate=pl.CostEstimate(flops=6 * TOKENS * D * FF, bytes_accessed=10 * TOKENS * FF, transcendentals=0),
        name="forward",
    )(x, wg, wu, wd)


def hidden_back(gate, up, d):
    s = jax.nn.sigmoid(gate)
    act = gate * s
    return (act * up).astype(BF16), (d * up * (s + act * (1.0 - s))).astype(BF16), (d * act).astype(BF16)


GAP = 24
SIDE_STRIDE, DOWN_STRIDE = D + GAP, FF // HALVES + GAP
DOWN_BASE = RING_TILES * SIDE_STRIDE
X_ROWS = DOWN_BASE + D // LANES * DOWN_STRIDE
COST = {"last": (3.7, 2.6, 1.3), "first": (1.6, 2.6, 1.3), "da": (2.4,), "norm": (0.5,)}
PACK_DOWN = 1.0
WHOLE = ((0,), (1, 2), (3, 4), (5, 6), (7, 8))
COLOUR = {1: 0, 3: 1, 4: 2}
PASSES = ("last", "da", "norm", "first")
COUNT = {"last": STEPS, "da": STEPS, "norm": TOKENS // TILE, "first": STEPS}
SIDE, DOWN = 1, 2


def timeline():
    out = []
    for kind in PASSES:
        layer = {"last": 1, "first": 0}.get(kind)
        for t in range(COUNT[kind]):
            half, tt = divmod(t, HALF)
            for i, cost in enumerate(COST[kind]):
                writes, whole = [], []
                if i == SIDE:
                    unit = (layer, half)
                    writes = [(unit, c) for c in range(3)] if tt == 0 else []
                    whole = [(unit, COLOUR[tt])] if tt in COLOUR else []
                if i == DOWN and tt == HALF - 1:
                    cost += PACK_DOWN
                    mine = [((layer, HALVES), c) for c in range(3)]
                    writes, whole = (mine, []) if half == 0 else ([], mine)
                out.append(((kind, t, i), cost, writes, whole))
    return out


def hidden_back(gate, up, d):
    s = jax.nn.sigmoid(gate)
    act = gate * s
    return (act * up).astype(BF16), (d * up * (s + act * (1.0 - s))).astype(BF16), (d * act).astype(BF16)


def backward(torus, gate0, up0, h1, a1, at1, at0, dy, wg, wu, wd, collective_id):
    rs = ReduceScatter(torus, CHUNK, 3)
    actions, copies, balance, flips = {}, {}, Balance(), {}
    for l in range(LAYERS):
        for u in range(3):
            for c in range(3):
                flips[l, u, c] = rs.flips(balance, c)
                got, sent = rs.plan((l, u), c, flips[l, u, c])
                copies |= sent
                actions |= got
                if l:
                    key = ((l, u), c)
                    actions[key, "free"] = ([("action", (key, "end", DIRECT))], [], TURN)
    slots = place(actions, copies, timeline())

    def kernel(gate_ref, up_ref, h1_ref, a1_ref, at1_ref, at0_ref, dy_ref, wg_ref, wu_ref, wd_ref, out, both_ref, dyv, av, at, X, Mb, Db, Wb, Vb, Hb, once, pair, hsem, rsc):
        me = torus.here()
        it = rs.bind(me, rsc)
        copy = pltpu.make_async_copy
        loads = [copy(src, dst, once.at[i]) for i, (src, dst) in enumerate(((dy_ref, dyv), (a1_ref, av), (at1_ref, at)))]
        load_at0 = copy(at0_ref, at, once.at[3])

        def part(i):
            return pl.ds(i * TILE, TILE)

        def sides(layer, t, s):
            return [copy(ref.at[layer, :, part(t)], Wb.at[s, :, part(k)], pair.at[k, s]) for k, ref in enumerate((wg_ref, wu_ref))]

        def fetch(kind, t, s):
            both, rows = pair.at[2, s], pair.at[3, s]
            if kind == "last":
                return sides(1, t, s) + [copy(wd_ref.at[1, part(t)], Vb.at[s], rows)]
            if kind == "da":
                return sides(1, t, s) + [copy(both_ref.at[t], Db.at[s], both)]
            if kind == "norm":
                return [copy(h1_ref.at[part(t)], Vb.at[s], rows)]
            return [copy(wd_ref.at[0, part(t)], Vb.at[s], rows)]

        def save(t, s):
            return copy(Db.at[s], both_ref.at[t], pair.at[4, s])

        def hiddens(t, q):
            return [copy(ref.at[pl.ds(t * LT, LT), pl.ds(q * PART, PART)], Hb.at[q, k], hsem.at[q, k]) for k, ref in enumerate((gate_ref, up_ref))]

        def act(a):
            ((l, u), c), what = a[0], a[1:]
            if what[0] == "free":
                it.wait_sends(u, c, flips[l, u, c])
                it.give_credit(u, c)
                return
            if what[0] == "start" and l == 0:
                it.take_credit(u, c)

            def store(value):
                out[l, u, c] = value

            it.run(u, c, flips[l, u, c], what, store)

        def point(kind, t, i, which):
            for k in range(COUNT[kind]):
                if slots[kind, k, i][which]:

                    @pl.when(t == k)
                    def _(k=k):
                        for a in slots[kind, k, i][which]:
                            act(a)

        def hidden(kind, t, s):
            for q in range(TOKENS // PART):
                rows = pl.ds(q * PART, PART)
                if kind == "last":
                    both = dot(av[rows, :], Wb[s])
                    gate, up = both[:, :TILE], both[:, TILE:]
                else:
                    for f in hiddens(t, q):
                        f.wait()
                    gate, up = (jnp.concatenate([Hb[q, k, j] for j in range(LT)], axis=1) for k in range(2))
                d = dot(dyv[rows, :], Vb[s], NT).astype(BF16).astype(F32)
                mid, Db[s, rows, part(0)], Db[s, rows, part(1)] = hidden_back(gate, up, d)
                Mb[:, rows] = mid.T
                if kind == "first":

                    @pl.when(t + 1 < STEPS)
                    def _(q=q):
                        for f in hiddens(t + 1, q):
                            f.start()

        def side(kind, t, s):
            half, tt = lax.div(t, HALF), lax.rem(t, HALF)
            got = dot(at[...], Db[s])
            for k in range(2 * LT):
                X[pl.ds((lax.rem(tt, 2) * 2 * LT + k) * SIDE_STRIDE + 8, D), :] = got[:, k * LANES : (k + 1) * LANES]
            point(kind, t, SIDE, 0)
            for v, parts in enumerate(WHOLE):

                @pl.when(tt == v)
                def _(parts=parts):
                    pack(torus, 0, X, lambda ct: ct % RING_TILES * SIDE_STRIDE + 8, parts, 0, torus.size, [T.at[half] for T in it.T])

        def down(kind, t, s):
            half, tt = lax.div(t, HALF), lax.rem(t, HALF)
            got = dot(Mb[...], dyv[...])
            for ct in range(D // LANES):
                X[pl.ds(DOWN_BASE + ct * DOWN_STRIDE + 8 + tt * TILE, TILE), :] = got[:, ct * LANES : (ct + 1) * LANES]
            point(kind, t, DOWN, 0)

            @pl.when(tt == HALF - 1)
            def _():
                some = torus.size // HALVES
                pack(torus, HALVES, X, lambda ct: DOWN_BASE + ct * DOWN_STRIDE + 8, range(ROWS // 16), half * some, some, [T.at[HALVES] for T in it.T])

        def d_a(t, s):
            for r in range(0, TOKENS, PART):
                got = dot(Db[s, pl.ds(r, PART), :], Wb[s], NT)
                for ct in range(D // LANES):
                    rows = pl.ds(ct * TOKENS + r, PART)
                    X[rows, :] = jnp.where(t == 0, 0.0, X[rows, :]) + got[:, ct * LANES : (ct + 1) * LANES]

        def norm(t, s):
            da = jnp.concatenate([X[pl.ds(ct * TOKENS + t * TILE, TILE), :] for ct in range(D // LANES)], axis=1).astype(BF16).astype(F32)
            wide = Vb[s].astype(F32)
            scale = scale_of(wide)
            inner = jnp.mean(da * wide, -1, keepdims=True)
            dyv[part(t), :] = dyv[part(t), :] + (scale * da - wide * (scale * scale * scale * inner)).astype(BF16)

        for f in fetch("last", 0, 0) + loads:
            f.start()
        barrier(me, rs.peers())
        for f in loads:
            f.wait()
        for number, kind in enumerate(PASSES):
            count = COUNT[kind]
            following = PASSES[number + 1] if number + 1 < len(PASSES) else None
            if kind == "da":
                load_at0.start()
            if kind == "norm":
                for q in range(TOKENS // PART):
                    for f in hiddens(0, q):
                        f.start()
            if kind == "first":
                load_at0.wait()

            def body(t, carry, kind=kind, count=count, following=following):
                s = lax.rem(t, 2)
                for f in fetch(kind, t, s):
                    f.wait()

                @pl.when(t + 1 < count)
                def _():
                    for f in fetch(kind, t + 1, 1 - s):
                        f.start()

                if kind == "last":

                    @pl.when(t > 1)
                    def _():
                        save(t - 2, s).wait()

                if following:

                    @pl.when(t == count - 1)
                    def _():
                        if kind == "last":
                            save(t - 1, 1 - s).wait()
                        for f in fetch(following, 0, 0):
                            f.start()

                if kind in ("last", "first"):
                    hidden(kind, t, s)
                    if kind == "last":
                        save(t, s).start()
                    point(kind, t, 0, 1)
                    side(kind, t, s)
                    point(kind, t, SIDE, 1)
                    down(kind, t, s)
                    point(kind, t, DOWN, 1)
                else:
                    (d_a if kind == "da" else norm)(t, s)
                    point(kind, t, 0, 1)
                return carry

            lax.fori_loop(0, count, body, 0)
            if kind == "last":
                save(count - 1, (count - 1) % 2).wait()
        for u in range(3):
            for c in range(3):
                it.wait_sends(u, c, flips[0, u, c])

    any_space = pl.BlockSpec(memory_space=pl.ANY)
    return pl.pallas_call(
        kernel,
        out_shape=[jax.ShapeDtypeStruct((LAYERS, 3, 3, CHUNK, LANES), F32), jax.ShapeDtypeStruct((STEPS, TOKENS, 2 * TILE), BF16)],
        in_specs=[any_space] * 10,
        out_specs=[pl.BlockSpec(memory_space=pltpu.VMEM), any_space],
        scratch_shapes=[
            pltpu.VMEM((TOKENS, D), BF16),
            pltpu.VMEM((TOKENS, D), BF16),
            pltpu.VMEM((D, TOKENS), BF16),
            pltpu.VMEM((X_ROWS, LANES), F32),
            pltpu.VMEM((TILE, TOKENS), BF16),
            pltpu.VMEM((2, TOKENS, 2 * TILE), BF16),
            pltpu.VMEM((2, D, 2 * TILE), BF16),
            pltpu.VMEM((2, TILE, D), BF16),
            pltpu.VMEM((TOKENS // PART, 2, LT, PART, LANES), F32),
            pltpu.SemaphoreType.DMA((4,)),
            pltpu.SemaphoreType.DMA((5, 2)),
            pltpu.SemaphoreType.DMA((TOKENS // PART, 2)),
            rs.scratch(),
        ],
        compiler_params=pltpu.CompilerParams(collective_id=collective_id, has_side_effects=True, vmem_limit_bytes=VMEM_ALL),
        cost_estimate=pl.CostEstimate(flops=TOKENS * D * FF * 24, bytes_accessed=TOKENS * FF * 20, transcendentals=0),
        name="backward",
    )(gate0, up0, h1, a1, at1, at0, dy, wg, wu, wd)[0]


def solution(mesh):
    torus = Torus(4, 4, 8)
    count = float(LAYERS * 3 * D * FF)

    def step(x, dy, wg, wu, wd, mg, mu, md, vg, vu, vd):
        x, dy = x[0], dy[0]
        gate0, up0, h1, a1, at1, at0 = forward(x, wg, wu, wd)
        g = backward(torus, gate0, up0, h1, a1, at1, at0, dy, wg, wu, wd, 1)
        G, m, v = step_and_gather(torus, g, (wg, wu, wd), (mg, mu, md), (vg, vu, vd), count, 2)
        return (*unpack(torus, G), *m, *v)

    P = jax.sharding.PartitionSpec
    return jax.shard_map(
        step,
        mesh=mesh,
        in_specs=(P(("rep", "dp")),) * 2 + (P(),) * 3 + (P(None, "dp"),) * 6,
        out_specs=(P("rep"),) * 3 + (P("rep", "dp"),) * 6,
        check_vma=False,
    )
```

time: 492 us -> 466 us (0.947)
  local copies, waits for them, and re-layouts: 30.6 us -> 3.95 us
    pallas_call x1, Pallas kernels: 208 us -> 263 us  [backward(): pl.pallas_call(kernel, out_shape=[jax.ShapeDtypeStruct((LAYERS, 3, 3, CHU...]
    pallas_call x1 -> x0, Pallas kernels: 41.3 us -> none  [last_layer(): pl.pallas_call(kernel, grid=(steps,), out_shape=[jax.ShapeDtypeStruct((FF...]
    squeeze x2 -> x0, local copies, waits for them, and re-layouts: 18.5 us -> none  [step(): mid1, dgate1, dup1 = last_layer(a1, dy, wg[1], wu[1], wd[1])]
    pallas_call x1, Pallas kernels: 144 us -> 133 us  [step_and_gather(): pl.pallas_call(kernel, out_shape=[pltpu.MemorySpace.VMEM(s.shape, s.dtype...]
    unnamed x16 -> x6, local copies, waits for them, and re-layouts: 12.2 us -> 3.95 us
where the time goes in v3:
time: 466 us; the launch traced here: 464 us
  Pallas kernels  460 us (99%)
    pallas_call x1, Pallas kernels, backward(): pl.pallas_call(kernel, out_shape=[jax.ShapeDtypeStruct((LAYERS, 3, 3, CHU...  263 us
    pallas_call x1, Pallas kernels, step_and_gather(): pl.pallas_call(kernel, out_shape=[pltpu.MemorySpace.VMEM(s.shape, s.dtype...  133 us
    pallas_call x1, Pallas kernels, forward(): pl.pallas_call(kernel, grid=(steps,), out_shape=[jax.ShapeDtypeStruct((FF...  49.6 us
    pallas_call x1, Pallas kernels, unpack(): pl.pallas_call(kernel, grid=(LAYERS, groups), out_shape=[jax.ShapeDtypeSt...  13.3 us

profile of v3, /device:TPU:8, one launch (start us, length us, event | category | flops | bytes accessed | tf_op | source)
XLA Modules:
  0.0 464.2 jit_solution(6953160474869921098)
XLA Ops:
  0.6 49.6 %forward.1 = (f32[20,2048,128]{2,1,0:T(8,128)}, f32[20,2048,128]{2,1,0:T(8,128)}, bf16[2048,896]{1,0:T(8,128)(2,1)}, bf16[2048,896]{1,0:T(8,128)(2,1)}, bf16[896...) custom-call(bf16[2048,896]{1,0:T(8,128)(2,1)} %bitcast.26, bf16[2,896,2560]{2,1,0:T(8,128)(2,1)} %refs_0_.1, ...), custom_call_target="tpu_custom_call" | custom-call | flops 28185722880 | bytes 52428800 | tf_op jit(solution)/shard_map/forward/pallas_call | solution.py:767
  50.2 263.3 %backward.1 = (f32[2,3,3,48,128]{4,3,2,1,0:T(8,128)}, bf16[10,2048,512]{2,1,0:T(8,128)(2,1)}) custom-call(f32[20,2048,128]{2,1,0:T(8,128)} %get-tuple-element.28.gate_ref, f32[20,2048,128]{2,1,0:T(8,128)} %get-tuple-element.29.up_ref, bf16[2048,896]{1,0:T(8,128)(2,1)} %get-tuple-element.30.h1_ref, bf16[2048,896]{1,0:T(8,128)(2,1)} %get-tuple-element.31.a1_ref, ...), custom_call_target="tpu_custom_call" | custom-call | flops 112742891520 | bytes 104857600 | tf_op jit(solution)/shard_map/backward/pallas_call | solution.py:1014
  313.6 133.4 %step_and_gather.1 = (bf16[8,16,2,3,48,128]{5,4,3,2,1,0:T(8,128)(2,1)S(1)}, bf16[4,32,2,3,48,128]{5,4,3,2,1,0:T(8,128)(2,1)S(1)}, bf16[4,32,2,3,48,128]{5,4,3,2,...) custom-call(f32[2,3,3,48,128]{4,3,2,1,0:T(8,128)} %get-tuple-element, ...), custom_call_target="tpu_custom_call" | custom-call | tf_op jit(solution)/shard_map/step_and_gather/pallas_call | solution.py:650
  447.0 13.3 %unpack.1 = (bf16[2,896,2560]{2,1,0:T(8,128)(2,1)}, bf16[2,896,2560]{2,1,0:T(8,128)(2,1)}, bf16[2,2560,896]{2,1,0:T(8,128)(2,1)}) custom-call(bf16[8,16,2,3,48,128]{5,4,3,2,1,0:T(8,128)(2,1)S(1)} %get-tuple-element.35.g0, bf16[4,32,2,3,48,128]{5,4,3,2,1,0:T(8,128)(2,1)S(1)} %get-tuple-element.36.g1, bf16[4,32,2,3,48,128]{5,4,3,2,1,0:T(8,128)(2,1)S(1)} %get-tuple-element.37.g2), custom_call_target="tpu_custom_call" | custom-call | tf_op jit(solution)/shard_map/unpack/pallas_call | solution.py:703
  460.3 0.7 copy.26
  460.9 0.7 copy.27
  461.6 0.7 copy.28
  462.3 0.7 copy.29
  462.9 0.7 copy.30
  463.6 0.7 copy.31

commit v4 on v3

--- a/solution.py
+++ b/solution.py
@@ -287,7 +287,10 @@
                 body(i)
                 return carry
 
-            lax.fori_loop(0, count, one, 0, unroll=2 - count % 2)
+            lax.fori_loop(0, count, one, 0)
+
+        def line(q):
+            return pl.ds(q * n3, n3)
 
         def ways(phase):
             for lane, turned in enumerate(flip[phase]):
@@ -315,17 +318,16 @@
             go(*where).wait_recv()
             slot = self.slot(c, phase, s, h)
             q = self.me.up(self.dims[c][phase], s * h)
-            part = n2 * n3 // self.LANES[RING]
-
-            def ring(i):
-                b = lane * part + i
-                T[q, b] = (wide(T[q, b]) + wide(R1[slot, b])).astype(BF16)
-
-            def cross(i):
-                b = q * n3 + i
-                mine[b] = (wide(mine[b]) + wide(R2[slot, i])).astype(BF16)
-
-            loop(part if phase == RING else n3, cross if phase else ring)
+            if phase == RING:
+                lines = n2 // self.LANES[RING]
+
+                def add(i):
+                    b = line(lane * lines + i)
+                    T[q, b] = (wide(T[q, b]) + wide(R1[slot, b])).astype(BF16)
+
+                loop(lines, add)
+            else:
+                mine[line(q)] = (wide(mine[line(q)]) + wide(R2[slot])).astype(BF16)
             go(phase, lane, s, h - 1).start()
         elif where == [RING]:
             got = arrived(RING)
@@ -333,28 +335,21 @@
             def total(b):
                 return sum((wide(R1[g, b]) for g in got), wide(mine[b]))
 
-            def own(i):
-                K2[i] = total(m2 * n3 + i)
-
             def others(i):
-                b = lax.rem((m2 + 1) * n3 + i, n2 * n3)
+                b = line(lax.rem(m2 + 1 + i, n2))
                 mine[b] = total(b).astype(BF16)
 
-            loop((n2 - 1) * n3, others)
+            loop(n2 - 1, others)
             sends(CROSS)
-            loop(n3, own)
+            K2[...] = total(line(m2))
         elif where == [CROSS]:
             got = arrived(CROSS)
-
-            def total(q):
-                return sum((wide(R2[g, q]) for g in got), K2[q])
-
-            for rel in range(1, n3):
-                q = self.me.up(self.dims[c][DIRECT], rel)
-                mine[m2 * n3 + q] = total(q).astype(BF16)
+            total = sum((wide(R2[g]) for g in got), K2[...])
+            K2[...] = total
+            mine[line(m2)] = total.astype(BF16)
             for rel in range(1, n3):
                 go(DIRECT, 0, 0, rel).start()
-            K3[...] = total(m3)
+            K3[...] = K2[m3]
         else:
             for rel in range(1, n3):
                 go(DIRECT, 0, 0, rel).wait_recv()
@@ -521,36 +516,32 @@
     return out
 
 
-def owner_index(torus, c, i):
-    ny, nz = torus.n["y"], torus.n["z"]
-    at = {"z": lax.rem(i, nz), "y": lax.rem(lax.div(i, nz), ny), "x": lax.div(i, ny * nz)}
-    n = torus.n
-    a, b, d = ORDERS[c]
-    return at[a], at[b] * n[d] + at[d]
-
-
 def pack(torus, u, X, base, parts, first, count, outs):
-    high = HIGH[u]
+    high, ny, nz = HIGH[u], torus.n["y"], torus.n["z"]
     sub = lax.broadcasted_iota(jnp.int32, (8, LANES), 0)
-
-    def piece(i, ct, row, whole, more):
-        a = X[pl.ds(base(ct) + high * i + row, 8), :]
-        if whole == 8:
-            return a
-        b = X[pl.ds(base(ct + 1) + high * i - whole, 8), :] if more else jnp.zeros((8, LANES), F32)
-        return jnp.where(sub < whole, a, b)
-
     got = tiles(u)
 
-    def body(i, carry):
-        at = [owner_index(torus, c, first + i) for c in range(3)]
-        for j in parts:
-            both = jnp.concatenate([piece(i, *got[2 * j]), piece(i, *got[2 * j + 1])], axis=0).astype(BF16)
-            c, r = divmod(16 * j, CHUNK)
-            outs[c][at[c][0], at[c][1], pl.ds(r, 16), :] = both
+    def body(line, carry):
+        x, y = lax.div(first + line, ny), lax.rem(first + line, ny)
+        top = pl.multiple_of(line * (high * nz), 8)
+
+        def piece(z, ct, row, whole, more):
+            a = X[pl.ds(top + (base(ct) + high * z + row), 8), :]
+            if whole == 8:
+                return a
+            b = X[pl.ds(top + (base(ct + 1) + high * z - whole), 8), :] if more else jnp.zeros((8, LANES), F32)
+            return jnp.where(sub < whole, a, b)
+
+        for z in range(nz):
+            at = {"x": x, "y": y, "z": z}
+            for j in parts:
+                both = jnp.concatenate([piece(z, *got[2 * j]), piece(z, *got[2 * j + 1])], axis=0).astype(BF16)
+                c, r = divmod(16 * j, CHUNK)
+                d1, d2, d3 = ORDERS[c]
+                outs[c][at[d1], at[d2] * torus.n[d3] + at[d3], pl.ds(r, 16), :] = both
         return carry
 
-    lax.fori_loop(0, count, body, 0, unroll=4)
+    lax.fori_loop(0, count, body, 0)
 
 
 def pieces_shapes(torus, dtype, *mid):
@@ -836,6 +827,7 @@
                     key = ((l, u), c)
                     actions[key, "free"] = ([("action", (key, "end", DIRECT))], [], TURN)
     slots = place(actions, copies, timeline())
+    lines = torus.n["x"] * torus.n["y"]
 
     def kernel(gate_ref, up_ref, h1_ref, a1_ref, at1_ref, at0_ref, dy_ref, wg_ref, wu_ref, wd_ref, out, both_ref, dyv, av, at, X, Mb, Db, Wb, Vb, Hb, once, pair, hsem, rsc):
         me = torus.here()
@@ -919,7 +911,7 @@
 
                 @pl.when(tt == v)
                 def _(parts=parts):
-                    pack(torus, 0, X, lambda ct: ct % RING_TILES * SIDE_STRIDE + 8, parts, 0, torus.size, [T.at[half] for T in it.T])
+                    pack(torus, 0, X, lambda ct: ct % RING_TILES * SIDE_STRIDE + 8, parts, 0, lines, [T.at[half] for T in it.T])
 
         def down(kind, t, s):
             half, tt = lax.div(t, HALF), lax.rem(t, HALF)
@@ -930,7 +922,7 @@
 
             @pl.when(tt == HALF - 1)
             def _():
-                some = torus.size // HALVES
+                some = lines // HALVES
                 pack(torus, HALVES, X, lambda ct: DOWN_BASE + ct * DOWN_STRIDE + 8, range(ROWS // 16), half * some, some, [T.at[HALVES] for T in it.T])
 
         def d_a(t, s):

time: 466 us -> 444 us (0.953)
  Pallas kernels: 460 us -> 438 us
    pallas_call x1, Pallas kernels: 263 us -> 244 us  [backward(): pl.pallas_call(kernel, out_shape=[jax.ShapeDtypeStruct((LAYERS, 3, 3, CHU...]
where the time goes in v4:
time: 444 us; the launch traced here: 442 us
  Pallas kernels  438 us (99%)
    pallas_call x1, Pallas kernels, backward(): pl.pallas_call(kernel, out_shape=[jax.ShapeDtypeStruct((LAYERS, 3, 3, CHU...  244 us
    pallas_call x1, Pallas kernels, step_and_gather(): pl.pallas_call(kernel, out_shape=[pltpu.MemorySpace.VMEM(s.shape, s.dtype...  131 us
    pallas_call x1, Pallas kernels, forward(): pl.pallas_call(kernel, grid=(steps,), out_shape=[jax.ShapeDtypeStruct((FF...  49.6 us
    pallas_call x1, Pallas kernels, unpack(): pl.pallas_call(kernel, grid=(LAYERS, groups), out_shape=[jax.ShapeDtypeSt...  13.3 us

profile of v4, /device:TPU:8, one launch (start us, length us, event | category | flops | bytes accessed | tf_op | source)
XLA Modules:
  0.0 442.2 jit_solution(2094910622071978086)
XLA Ops:
  0.6 49.6 %forward.1 = (f32[20,2048,128]{2,1,0:T(8,128)}, f32[20,2048,128]{2,1,0:T(8,128)}, bf16[2048,896]{1,0:T(8,128)(2,1)}, bf16[2048,896]{1,0:T(8,128)(2,1)}, bf16[896...) custom-call(bf16[2048,896]{1,0:T(8,128)(2,1)} %bitcast.26, bf16[2,896,2560]{2,1,0:T(8,128)(2,1)} %refs_0_.1, ...), custom_call_target="tpu_custom_call" | custom-call | flops 28185722880 | bytes 52428800 | tf_op jit(solution)/shard_map/forward/pallas_call | solution.py:758
  50.2 243.6 %backward.1 = (f32[2,3,3,48,128]{4,3,2,1,0:T(8,128)}, bf16[10,2048,512]{2,1,0:T(8,128)(2,1)}) custom-call(f32[20,2048,128]{2,1,0:T(8,128)} %get-tuple-element.28.gate_ref, f32[20,2048,128]{2,1,0:T(8,128)} %get-tuple-element.29.up_ref, bf16[2048,896]{1,0:T(8,128)(2,1)} %get-tuple-element.30.h1_ref, bf16[2048,896]{1,0:T(8,128)(2,1)} %get-tuple-element.31.a1_ref, ...), custom_call_target="tpu_custom_call" | custom-call | flops 112742891520 | bytes 104857600 | tf_op jit(solution)/shard_map/backward/pallas_call | solution.py:1006
  293.8 131.2 %step_and_gather.1 = (bf16[8,16,2,3,48,128]{5,4,3,2,1,0:T(8,128)(2,1)S(1)}, bf16[4,32,2,3,48,128]{5,4,3,2,1,0:T(8,128)(2,1)S(1)}, bf16[4,32,2,3,48,128]{5,4,3,2,...) custom-call(f32[2,3,3,48,128]{4,3,2,1,0:T(8,128)} %get-tuple-element, ...), custom_call_target="tpu_custom_call" | custom-call | tf_op jit(solution)/shard_map/step_and_gather/pallas_call | solution.py:641
  424.9 13.3 %unpack.1 = (bf16[2,896,2560]{2,1,0:T(8,128)(2,1)}, bf16[2,896,2560]{2,1,0:T(8,128)(2,1)}, bf16[2,2560,896]{2,1,0:T(8,128)(2,1)}) custom-call(bf16[8,16,2,3,48,128]{5,4,3,2,1,0:T(8,128)(2,1)S(1)} %get-tuple-element.35.g0, bf16[4,32,2,3,48,128]{5,4,3,2,1,0:T(8,128)(2,1)S(1)} %get-tuple-element.36.g1, bf16[4,32,2,3,48,128]{5,4,3,2,1,0:T(8,128)(2,1)S(1)} %get-tuple-element.37.g2), custom_call_target="tpu_custom_call" | custom-call | tf_op jit(solution)/shard_map/unpack/pallas_call | solution.py:694
  438.3 0.7 copy.26
  438.9 0.7 copy.27
  439.6 0.7 copy.28
  440.3 0.7 copy.29
  440.9 0.7 copy.30
  441.6 0.7 copy.31

commit v5 on v4

--- a/solution.py
+++ b/solution.py
@@ -10,7 +10,8 @@
 RATE, LATENCY = 46.6e3, 2.3
 TURN, ADD, HOP = 0.1, 2.0e6, 0.7
 WAYS = (1, -1)
-RING, CROSS, DIRECT = range(3)
+TRIO = range(3)
+RING, CROSS, DIRECT = TRIO
 NEVER, MARGIN, SWEEPS = 1e9, 0.5, 2
 
 
@@ -123,7 +124,7 @@
         others = {(l, u, c) for (l, u), c in writes}
         drain(slots[key][0], lambda a: any(a[0][0][1] == u and a[0][1] == c and a[0][0][0] > l for l, u, c in others), True)
         open_keys |= set(whole)
-        drain(slots[key][1], lambda a: a[1] != "start" or a[0] in open_keys, False)
+        drain(slots[key][1], lambda a: a[1] != "start" or (a[0], a[2]) in open_keys, False)
     drain(slots[segments[-1][0]][1], lambda a: True, True)
     assert not left
     place.took = now
@@ -152,7 +153,7 @@
     def __init__(self, torus, rows, units):
         self.t, self.rows, self.units = torus, rows, units
         self.dims = [tuple(order) for order in ORDERS]
-        self.nslots = max(self.base(c, DIRECT, 0) + self.sizes(c)[DIRECT] - 1 for c in range(3))
+        self.nslots = max(self.base(c, DIRECT, 0) + self.sizes(c)[DIRECT] - 1 for c in TRIO)
 
     def sizes(self, c):
         return [self.t.n[d] for d in self.dims[c]]
@@ -232,8 +233,9 @@
             copies[cid] = ((self.dims[c][DIRECT], 1 if rel <= n3 // 2 else -1), size[DIRECT] * far, HOP * (far - 1))
             direct.append(cid)
         sends = first + [direct, []]
-        actions[key, "start"] = ([], sends[RING], TURN)
-        before = (key, "start")
+        for lane in range(self.LANES[RING]):
+            actions[key, "start", lane] = ([], [x for x in sends[RING] if x[3] == lane], TURN)
+        before = (key, "start", 0)
         for phase, needs in enumerate(last + [direct]):
             a = (key, "end", phase)
             actions[a] = (needs + [("action", before)], sends[phase + 1], size[phase] * self.LANES[phase] / ADD + TURN)
@@ -299,9 +301,10 @@
                     if k[s]:
                         yield lane, s, k[s]
 
-        def sends(phase):
+        def sends(phase, only=None):
             for lane, s, k in ways(phase):
-                go(phase, lane, s, k - 1).start()
+                if only in (None, lane):
+                    go(phase, lane, s, k - 1).start()
 
         def arrived(phase):
             got = set()
@@ -312,7 +315,7 @@
 
         kind, *where = what
         if kind == "start":
-            sends(RING)
+            sends(RING, *where)
         elif kind == "step":
             phase, lane, s, h = where
             go(*where).wait_recv()
@@ -383,7 +386,7 @@
 
     def build(self):
         self.copies, self.actions, self.index = {}, {}, {}
-        for c in range(3):
+        for c in TRIO:
             self.plan(c)
         self.order, self.took = simulate({a: (*v, 0) for a, v in self.actions.items()}, self.copies)
 
@@ -494,6 +497,7 @@
 
 
 HALVES, RING_TILES = 2, 8
+COLOURS = {0: (1, 2, 0), 1: (1, 2, 0), 2: (0, 1, 2)}
 TOKENS, TILE, PART = 2048, 256, 512
 LT, STEPS = TILE // LANES, FF // TILE
 HALF = STEPS // HALVES
@@ -516,7 +520,7 @@
     return out
 
 
-def pack(torus, u, X, base, parts, first, count, outs):
+def pack(torus, u, X, base, parts, first, count, outs, colours):
     high, ny, nz = HIGH[u], torus.n["y"], torus.n["z"]
     sub = lax.broadcasted_iota(jnp.int32, (8, LANES), 0)
     got = tiles(u)
@@ -536,7 +540,8 @@
             at = {"x": x, "y": y, "z": z}
             for j in parts:
                 both = jnp.concatenate([piece(z, *got[2 * j]), piece(z, *got[2 * j + 1])], axis=0).astype(BF16)
-                c, r = divmod(16 * j, CHUNK)
+                k, r = divmod(16 * j, CHUNK)
+                c = colours[k]
                 d1, d2, d3 = ORDERS[c]
                 outs[c][at[d1], at[d2] * torus.n[d3] + at[d3], pl.ds(r, 16), :] = both
         return carry
@@ -568,21 +573,21 @@
         me = torus.here()
         p = lax.axis_index("dp")
         loads = []
-        for x in range(3):
+        for x in TRIO:
             first, rows = window(p, x)
             loads.append(pltpu.make_async_copy(w_in[x].at[:, pl.ds(first, rows)], win[x], wsem.at[x]))
             loads[x].start()
         barrier(me, [p for d in "xyz" for p in all_others(torus, d)])
-        for x in range(3):
+        for x in TRIO:
             loads[x].wait()
             for lt in range(WIDE[x] // LANES):
                 wide_win[x][:, lt] = win[x][:, :, pl.ds(lt * LANES, LANES)].astype(F32)
         acc = jnp.zeros((8, LANES), F32)
         for l in range(LAYERS):
-            for u in range(3):
-                for c in range(3):
+            for u in TRIO:
+                for k, c in enumerate(COLOURS[u]):
                     value = g_ref[l, u, c]
-                    flat[l, u, pl.ds(c * CHUNK, CHUNK), :] = value
+                    flat[l, u, pl.ds(k * CHUNK, CHUNK), :] = value
                     for r in range(0, CHUNK, 8):
                         acc = acc + value[r : r + 8] * value[r : r + 8]
         part[0] = acc
@@ -606,7 +611,7 @@
         mean = jnp.sum(part[3], keepdims=True) / count
         factor = jnp.minimum(1.0, 0.5 * lax.rsqrt(mean + 1e-30))
         for l in range(LAYERS):
-            for u in range(3):
+            for u in TRIO:
                 high = HIGH[u]
                 wflat[l, u, pl.ds(ROWS - 8, 8), :] = jnp.zeros((8, LANES), F32)
                 for ct in range(WIDE[u] // LANES):
@@ -621,12 +626,11 @@
                     v_out[x][at] = new_v
                     wflat[l, u, pl.ds(ct * high, high), :] = new_w
         it = ag.bind(me, G, ssem, rsem)
-        for c in range(3):
-            n = [torus.n[d] for d in ORDERS[c]]
-            at = [me.up(d, 0) for d in ORDERS[c]]
-            for l in range(LAYERS):
-                for u in range(3):
-                    G[c][at[0], at[1] * n[2] + at[2], l, u] = wflat[l, u, pl.ds(c * CHUNK, CHUNK), :].astype(BF16)
+        for u in TRIO:
+            for k, c in enumerate(COLOURS[u]):
+                a, b, d = (me.up(x, 0) for x in ORDERS[c])
+                for l in range(LAYERS):
+                    G[c][a, b * torus.n[ORDERS[c][DIRECT]] + d, l, u] = wflat[l, u, pl.ds(k * CHUNK, CHUNK), :].astype(BF16)
         for a in ag.order:
             it.run(a)
         it.wait_sends()
@@ -652,8 +656,8 @@
             pltpu.SemaphoreType.DMA((nsum,)),
             pltpu.SemaphoreType.DMA((k,)),
             pltpu.SemaphoreType.DMA((k,)),
-            [pltpu.VMEM((LAYERS, WINDOW[x], WIDE[x]), BF16) for x in range(3)],
-            [pltpu.VMEM((LAYERS, WIDE[x] // LANES, WINDOW[x], LANES), F32) for x in range(3)],
+            [pltpu.VMEM((LAYERS, WINDOW[x], WIDE[x]), BF16) for x in TRIO],
+            [pltpu.VMEM((LAYERS, WIDE[x] // LANES, WINDOW[x], LANES), F32) for x in TRIO],
             pltpu.SemaphoreType.DMA((3,)),
         ],
         compiler_params=pltpu.CompilerParams(collective_id=collective_id, has_side_effects=True, vmem_limit_bytes=26 * MIB),
@@ -673,14 +677,14 @@
         outs, Z, Y = refs[:3], refs[3], refs[4]
         l, s = pl.program_id(0), pl.program_id(1)
         corner = {"x": lax.div(s, pairs), "y": lax.rem(s, pairs) * pair, "z": 0}
-        for u in range(3):
+        for u in TRIO:
             high, wide = HIGH[u], WIDE[u] // LANES
             for i in range(group):
                 y, z = divmod(i, nz)
                 at = corner | {"y": corner["y"] + y, "z": z}
-                for c, ref in enumerate((g0, g1, g2)):
+                for k, c in enumerate(COLOURS[u]):
                     a, b, d = ORDERS[c]
-                    Z[i, pl.ds(c * CHUNK, CHUNK), :] = ref[at[a], at[b] * torus.n[d] + at[d], l, u].astype(F32)
+                    Z[i, pl.ds(k * CHUNK, CHUNK), :] = (g0, g1, g2)[c][at[a], at[b] * torus.n[d] + at[d], l, u].astype(F32)
             for i in range(group):
                 for ct in range(wide):
                     for r in range(0, high, 8):
@@ -690,20 +694,20 @@
                 x, lt = home(u, ct)
                 outs[x][0, :, pl.ds(lt * LANES, LANES)] = Y[ct, pl.ds(0, rows), :].astype(BF16)
 
-    shapes = [(LAYERS, HIGH[u] * torus.size, WIDE[u]) for u in range(3)]
+    shapes = [(LAYERS, HIGH[u] * torus.size, WIDE[u]) for u in TRIO]
     return pl.pallas_call(
         kernel,
         grid=(LAYERS, groups),
         out_shape=[jax.ShapeDtypeStruct(s, BF16) for s in shapes],
         in_specs=[pl.BlockSpec(memory_space=pltpu.VMEM)] * 3,
-        out_specs=[pl.BlockSpec((1, HIGH[u] * group, WIDE[u]), lambda l, s: (l, s, 0)) for u in range(3)],
+        out_specs=[pl.BlockSpec((1, HIGH[u] * group, WIDE[u]), lambda l, s: (l, s, 0)) for u in TRIO],
         scratch_shapes=[pltpu.VMEM((group, ROWS + 8, LANES), F32), pltpu.VMEM((FF // LANES, HIGH[2] * group + 8, LANES), F32)],
         compiler_params=pltpu.CompilerParams(vmem_limit_bytes=26 * MIB),
         name="unpack",
     )(*G)
 
 
-NN, NT, TN = ((1,), (0,)), ((1,), (1,)), ((0,), (0,))
+NN, NT = ((1,), (0,)), ((1,), (1,))
 
 
 def dot(a, b, dims=NN):
@@ -712,84 +716,25 @@
 
 def scale_of(wide):
     return lax.rsqrt(jnp.mean(wide * wide, -1, keepdims=True) + 1e-6)
-
-
-def normed_into(h_ref, a_ref, t_ref):
-    for r in range(0, TOKENS, TILE):
-        wide = h_ref[pl.ds(r, TILE), :].astype(F32)
-        a = (wide * scale_of(wide)).astype(BF16)
-        a_ref[pl.ds(r, TILE), :] = a
-        t_ref[:, pl.ds(r, TILE)] = a.T
-
-
-def forward(x, wg, wu, wd):
-    steps = STEPS
-
-    def kernel(x_ref, wg_ref, wu_ref, wd_ref, gate_ref, up_ref, h_ref, a_ref, at_ref, xt_ref, xa, acc):
-        t = pl.program_id(0)
-
-        @pl.when(t == 0)
-        def _():
-            normed_into(x_ref, xa, xt_ref)
-            acc[...] = jnp.zeros_like(acc)
-
-        for r in range(0, TOKENS, PART):
-            rows = pl.ds(r, PART)
-            a = xa[rows, :]
-            both = dot(a, jnp.concatenate([wg_ref[0], wu_ref[0]], axis=1))
-            gate, up = both[:, :TILE], both[:, TILE:]
-            for k in range(LT):
-                lanes = slice(k * LANES, (k + 1) * LANES)
-                gate_ref[k, rows, :] = gate[:, lanes]
-                up_ref[k, rows, :] = up[:, lanes]
-            mid = (jax.nn.silu(gate) * up).astype(BF16)
-            acc[rows, :] += dot(mid, wd_ref[0])
-
-        @pl.when(t == steps - 1)
-        def _():
-            for r in range(0, TOKENS, TILE):
-                rows = pl.ds(r, TILE)
-                h_ref[rows, :] = x_ref[rows, :] + acc[rows, :].astype(BF16)
-            normed_into(h_ref, a_ref, at_ref)
-
-    whole = pl.BlockSpec(memory_space=pltpu.VMEM)
-    cols = pl.BlockSpec((1, D, TILE), lambda t: (0, 0, t))
-    saved = pl.BlockSpec((LT, TOKENS, LANES), lambda t: (t, 0, 0))
-    return pl.pallas_call(
-        kernel,
-        grid=(steps,),
-        out_shape=[jax.ShapeDtypeStruct((FF // LANES, TOKENS, LANES), F32)] * 2 + [jax.ShapeDtypeStruct((TOKENS, D), BF16)] * 2 + [jax.ShapeDtypeStruct((D, TOKENS), BF16)] * 2,
-        in_specs=[whole, cols, cols, pl.BlockSpec((1, TILE, D), lambda t: (0, t, 0))],
-        out_specs=[saved] * 2 + [whole] * 4,
-        scratch_shapes=[pltpu.VMEM((TOKENS, D), BF16), pltpu.VMEM((TOKENS, D), F32)],
-        compiler_params=pltpu.CompilerParams(vmem_limit_bytes=60 * MIB),
-        cost_estimate=pl.CostEstimate(flops=6 * TOKENS * D * FF, bytes_accessed=10 * TOKENS * FF, transcendentals=0),
-        name="forward",
-    )(x, wg, wu, wd)
-
-
-def hidden_back(gate, up, d):
-    s = jax.nn.sigmoid(gate)
-    act = gate * s
-    return (act * up).astype(BF16), (d * up * (s + act * (1.0 - s))).astype(BF16), (d * act).astype(BF16)
 
 
 GAP = 24
 SIDE_STRIDE, DOWN_STRIDE = D + GAP, FF // HALVES + GAP
 DOWN_BASE = RING_TILES * SIDE_STRIDE
 X_ROWS = DOWN_BASE + D // LANES * DOWN_STRIDE
-COST = {"last": (3.7, 2.6, 1.3), "first": (1.6, 2.6, 1.3), "da": (2.4,), "norm": (0.5,)}
-PACK_DOWN = 1.0
+COST = {"last": (3.8, 2.3, 1.3), "first": (1.7, 2.3, 1.3), "da": (2.4,), "norm": (0.45,)}
+PACK_DOWN = 0.4
 WHOLE = ((0,), (1, 2), (3, 4), (5, 6), (7, 8))
-COLOUR = {1: 0, 3: 1, 4: 2}
-PASSES = ("last", "da", "norm", "first")
-COUNT = {"last": STEPS, "da": STEPS, "norm": TOKENS // TILE, "first": STEPS}
+CHUNKS = {1: 0, 3: 1, 4: 2}
+PASSES = ("forward", "last", "da", "norm", "first")
+COUNT = {"forward": STEPS, "last": STEPS, "da": STEPS, "norm": TOKENS // TILE, "first": STEPS}
+QUARTERS = TOKENS // PART
 SIDE, DOWN = 1, 2
 
 
 def timeline():
-    out = []
-    for kind in PASSES:
+    out, lanes = [], ReduceScatter.LANES[RING]
+    for kind in PASSES[1:]:
         layer = {"last": 1, "first": 0}.get(kind)
         for t in range(COUNT[kind]):
             half, tt = divmod(t, HALF)
@@ -797,12 +742,13 @@
                 writes, whole = [], []
                 if i == SIDE:
                     unit = (layer, half)
-                    writes = [(unit, c) for c in range(3)] if tt == 0 else []
-                    whole = [(unit, COLOUR[tt])] if tt in COLOUR else []
+                    writes = [(unit, c) for c in TRIO] if tt == 0 else []
+                    whole = [((unit, COLOURS[half][CHUNKS[tt]]), lane) for lane in range(lanes)] if tt in CHUNKS else []
                 if i == DOWN and tt == HALF - 1:
                     cost += PACK_DOWN
-                    mine = [((layer, HALVES), c) for c in range(3)]
-                    writes, whole = (mine, []) if half == 0 else ([], mine)
+                    mine = [((layer, HALVES), c) for c in TRIO]
+                    writes = [] if half else mine
+                    whole = [(key, lane) for key in mine for lane in range(lanes) if half or lane == 0 and ORDERS[key[1]][CROSS] == "x"]
                 out.append(((kind, t, i), cost, writes, whole))
     return out
 
@@ -813,12 +759,12 @@
     return (act * up).astype(BF16), (d * up * (s + act * (1.0 - s))).astype(BF16), (d * act).astype(BF16)
 
 
-def backward(torus, gate0, up0, h1, a1, at1, at0, dy, wg, wu, wd, collective_id):
+def gradients(torus, x, dy, wg, wu, wd, collective_id):
     rs = ReduceScatter(torus, CHUNK, 3)
     actions, copies, balance, flips = {}, {}, Balance(), {}
     for l in range(LAYERS):
-        for u in range(3):
-            for c in range(3):
+        for u in TRIO:
+            for c in TRIO:
                 flips[l, u, c] = rs.flips(balance, c)
                 got, sent = rs.plan((l, u), c, flips[l, u, c])
                 copies |= sent
@@ -829,21 +775,23 @@
     slots = place(actions, copies, timeline())
     lines = torus.n["x"] * torus.n["y"]
 
-    def kernel(gate_ref, up_ref, h1_ref, a1_ref, at1_ref, at0_ref, dy_ref, wg_ref, wu_ref, wd_ref, out, both_ref, dyv, av, at, X, Mb, Db, Wb, Vb, Hb, once, pair, hsem, rsc):
+    def kernel(x_ref, dy_ref, wg_ref, wu_ref, wd_ref, out, both_ref, gate_ref, up_ref, h1_ref, at0_ref, dyv, av, at, X, Mb, Db, Wb, Vb, Hb, once, pair, hsem, rsem, rsc):
         me = torus.here()
         it = rs.bind(me, rsc)
         copy = pltpu.make_async_copy
-        loads = [copy(src, dst, once.at[i]) for i, (src, dst) in enumerate(((dy_ref, dyv), (a1_ref, av), (at1_ref, at)))]
-        load_at0 = copy(at0_ref, at, once.at[3])
+        load_x = copy(x_ref, dyv, once.at[0])
+        save_at0, load_at0 = copy(at, at0_ref, once.at[1]), copy(at0_ref, at, once.at[1])
 
         def part(i):
-            return pl.ds(i * TILE, TILE)
+            return pl.ds(i * TILE if isinstance(i, int) else pl.multiple_of(i * TILE, TILE), TILE)
 
         def sides(layer, t, s):
             return [copy(ref.at[layer, :, part(t)], Wb.at[s, :, part(k)], pair.at[k, s]) for k, ref in enumerate((wg_ref, wu_ref))]
 
         def fetch(kind, t, s):
             both, rows = pair.at[2, s], pair.at[3, s]
+            if kind == "forward":
+                return sides(0, t, s) + [copy(wd_ref.at[0, part(t)], Vb.at[s], rows)]
             if kind == "last":
                 return sides(1, t, s) + [copy(wd_ref.at[1, part(t)], Vb.at[s], rows)]
             if kind == "da":
@@ -855,8 +803,13 @@
         def save(t, s):
             return copy(Db.at[s], both_ref.at[t], pair.at[4, s])
 
-        def hiddens(t, q):
-            return [copy(ref.at[pl.ds(t * LT, LT), pl.ds(q * PART, PART)], Hb.at[q, k], hsem.at[q, k]) for k, ref in enumerate((gate_ref, up_ref))]
+        def hiddens(t, quarters, out=False):
+            got = []
+            for q in quarters:
+                for k, ref in enumerate((gate_ref, up_ref)):
+                    ends = ref.at[pl.ds(t * LT, LT), pl.ds(q * PART, PART)], Hb.at[q, k]
+                    got.append(copy(*(ends[::-1] if out else ends), hsem.at[q, k]))
+            return got
 
         def act(a):
             ((l, u), c), what = a[0], a[1:]
@@ -864,7 +817,7 @@
                 it.wait_sends(u, c, flips[l, u, c])
                 it.give_credit(u, c)
                 return
-            if what[0] == "start" and l == 0:
+            if what == ("start", 0) and l == 0:
                 it.take_credit(u, c)
 
             def store(value):
@@ -881,56 +834,120 @@
                         for a in slots[kind, k, i][which]:
                             act(a)
 
-        def hidden(kind, t, s):
-            for q in range(TOKENS // PART):
-                rows = pl.ds(q * PART, PART)
-                if kind == "last":
+        def normed_into(r):
+            wide = dyv[part(r), :].astype(F32)
+            a = (wide * scale_of(wide)).astype(BF16)
+            av[part(r), :] = a
+            at[:, part(r)] = a.T
+
+        def lanes_of(ct):
+            return slice(ct * LANES, (ct + 1) * LANES)
+
+        def forward(t, s):
+            for first in range(0, QUARTERS, 2):
+                quarters = range(first, first + 2)
+
+                @pl.when(t > 0)
+                def _():
+                    for f in hiddens(t - 1, quarters, True):
+                        f.wait()
+
+                for q in quarters:
+                    rows = pl.ds(q * PART, PART)
                     both = dot(av[rows, :], Wb[s])
                     gate, up = both[:, :TILE], both[:, TILE:]
-                else:
-                    for f in hiddens(t, q):
+                    for j in range(LT):
+                        Hb[q, 0, j], Hb[q, 1, j] = gate[:, lanes_of(j)], up[:, lanes_of(j)]
+                    got = dot((jax.nn.silu(gate) * up).astype(BF16), Vb[s])
+                    for ct in range(D // LANES):
+                        here = pl.ds(ct * TOKENS + q * PART, PART)
+                        X[here, :] = jnp.where(t == 0, 0.0, X[here, :]) + got[:, lanes_of(ct)]
+                for f in hiddens(t, quarters, True):
+                    f.start()
+
+        def turn():
+            for f in hiddens(STEPS - 1, range(QUARTERS), True):
+                f.wait()
+            save_at0.wait()
+            count = TOKENS // TILE
+
+            def saves(r):
+                return copy(dyv.at[part(r)], h1_ref.at[part(r)], rsem.at[0, r])
+
+            def loads(r):
+                return copy(dy_ref.at[part(r)], dyv.at[part(r)], rsem.at[1, r])
+
+            @pl.loop(0, count)
+            def _(r):
+                total = jnp.concatenate([X[pl.ds(ct * TOKENS + r * TILE, TILE), :] for ct in range(D // LANES)], axis=1)
+                dyv[part(r), :] = dyv[part(r), :] + total.astype(BF16)
+                normed_into(r)
+                saves(r).start()
+
+                @pl.when(r > 0)
+                def _():
+                    saves(r - 1).wait()
+                    loads(r - 1).start()
+
+            saves(count - 1).wait()
+            loads(count - 1).start()
+            for r in range(count):
+                loads(r).wait()
+
+        def hidden(kind, t, s):
+            for first in range(0, QUARTERS, 2):
+                quarters = range(first, first + 2)
+                if kind == "first":
+                    for f in hiddens(t, quarters):
                         f.wait()
-                    gate, up = (jnp.concatenate([Hb[q, k, j] for j in range(LT)], axis=1) for k in range(2))
-                d = dot(dyv[rows, :], Vb[s], NT).astype(BF16).astype(F32)
-                mid, Db[s, rows, part(0)], Db[s, rows, part(1)] = hidden_back(gate, up, d)
-                Mb[:, rows] = mid.T
+                for q in quarters:
+                    rows = pl.ds(q * PART, PART)
+                    if kind == "last":
+                        both = dot(av[rows, :], Wb[s])
+                        gate, up = both[:, :TILE], both[:, TILE:]
+                    else:
+                        gate, up = (jnp.concatenate([Hb[q, k, j] for j in range(LT)], axis=1) for k in range(2))
+                    d = dot(dyv[rows, :], Vb[s], NT).astype(BF16).astype(F32)
+                    mid, Db[s, rows, part(0)], Db[s, rows, part(1)] = hidden_back(gate, up, d)
+                    Mb[:, rows] = mid.T
                 if kind == "first":
 
                     @pl.when(t + 1 < STEPS)
-                    def _(q=q):
-                        for f in hiddens(t + 1, q):
+                    def _():
+                        for f in hiddens(t + 1, quarters):
                             f.start()
 
         def side(kind, t, s):
-            half, tt = lax.div(t, HALF), lax.rem(t, HALF)
+            tt = lax.rem(t, HALF)
             got = dot(at[...], Db[s])
             for k in range(2 * LT):
-                X[pl.ds((lax.rem(tt, 2) * 2 * LT + k) * SIDE_STRIDE + 8, D), :] = got[:, k * LANES : (k + 1) * LANES]
+                X[pl.ds((lax.rem(tt, 2) * 2 * LT + k) * SIDE_STRIDE + 8, D), :] = got[:, lanes_of(k)]
             point(kind, t, SIDE, 0)
+            half = lax.div(t, HALF)
             for v, parts in enumerate(WHOLE):
 
                 @pl.when(tt == v)
                 def _(parts=parts):
-                    pack(torus, 0, X, lambda ct: ct % RING_TILES * SIDE_STRIDE + 8, parts, 0, lines, [T.at[half] for T in it.T])
+                    pack(torus, 0, X, lambda ct: ct % RING_TILES * SIDE_STRIDE + 8, parts, 0, lines, [T.at[half] for T in it.T], COLOURS[0])
 
         def down(kind, t, s):
             half, tt = lax.div(t, HALF), lax.rem(t, HALF)
             got = dot(Mb[...], dyv[...])
             for ct in range(D // LANES):
-                X[pl.ds(DOWN_BASE + ct * DOWN_STRIDE + 8 + tt * TILE, TILE), :] = got[:, ct * LANES : (ct + 1) * LANES]
+                X[pl.ds(DOWN_BASE + ct * DOWN_STRIDE + 8 + tt * TILE, TILE), :] = got[:, lanes_of(ct)]
             point(kind, t, DOWN, 0)
 
             @pl.when(tt == HALF - 1)
             def _():
                 some = lines // HALVES
-                pack(torus, HALVES, X, lambda ct: DOWN_BASE + ct * DOWN_STRIDE + 8, range(ROWS // 16), half * some, some, [T.at[HALVES] for T in it.T])
+                pack(torus, HALVES, X, lambda ct: DOWN_BASE + ct * DOWN_STRIDE + 8, range(ROWS // 16), half * some, some, [T.at[HALVES] for T in it.T], COLOURS[HALVES])
 
         def d_a(t, s):
             for r in range(0, TOKENS, PART):
                 got = dot(Db[s, pl.ds(r, PART), :], Wb[s], NT)
                 for ct in range(D // LANES):
                     rows = pl.ds(ct * TOKENS + r, PART)
-                    X[rows, :] = jnp.where(t == 0, 0.0, X[rows, :]) + got[:, ct * LANES : (ct + 1) * LANES]
+                    X[rows, :] = jnp.where(t == 0, 0.0, X[rows, :]) + got[:, lanes_of(ct)]
 
         def norm(t, s):
             da = jnp.concatenate([X[pl.ds(ct * TOKENS + t * TILE, TILE), :] for ct in range(D // LANES)], axis=1).astype(BF16).astype(F32)
@@ -939,20 +956,26 @@
             inner = jnp.mean(da * wide, -1, keepdims=True)
             dyv[part(t), :] = dyv[part(t), :] + (scale * da - wide * (scale * scale * scale * inner)).astype(BF16)
 
-        for f in fetch("last", 0, 0) + loads:
+        for f in fetch("forward", 0, 0) + [load_x]:
             f.start()
         barrier(me, rs.peers())
-        for f in loads:
-            f.wait()
+        load_x.wait()
+
+        @pl.loop(0, TOKENS // TILE)
+        def _(r):
+            normed_into(r)
+
+        save_at0.start()
         for number, kind in enumerate(PASSES):
             count = COUNT[kind]
             following = PASSES[number + 1] if number + 1 < len(PASSES) else None
+            if kind == "last":
+                turn()
             if kind == "da":
                 load_at0.start()
             if kind == "norm":
-                for q in range(TOKENS // PART):
-                    for f in hiddens(0, q):
-                        f.start()
+                for f in hiddens(0, range(QUARTERS)):
+                    f.start()
             if kind == "first":
                 load_at0.wait()
 
@@ -991,23 +1014,26 @@
                     down(kind, t, s)
                     point(kind, t, DOWN, 1)
                 else:
-                    (d_a if kind == "da" else norm)(t, s)
-                    point(kind, t, 0, 1)
+                    {"forward": forward, "da": d_a, "norm": norm}[kind](t, s)
+                    if kind != "forward":
+                        point(kind, t, 0, 1)
                 return carry
 
             lax.fori_loop(0, count, body, 0)
             if kind == "last":
                 save(count - 1, (count - 1) % 2).wait()
-        for u in range(3):
-            for c in range(3):
+        for u in TRIO:
+            for c in TRIO:
                 it.wait_sends(u, c, flips[0, u, c])
 
     any_space = pl.BlockSpec(memory_space=pl.ANY)
     return pl.pallas_call(
         kernel,
-        out_shape=[jax.ShapeDtypeStruct((LAYERS, 3, 3, CHUNK, LANES), F32), jax.ShapeDtypeStruct((STEPS, TOKENS, 2 * TILE), BF16)],
-        in_specs=[any_space] * 10,
-        out_specs=[pl.BlockSpec(memory_space=pltpu.VMEM), any_space],
+        out_shape=[jax.ShapeDtypeStruct((LAYERS, 3, 3, CHUNK, LANES), F32), jax.ShapeDtypeStruct((STEPS, TOKENS, 2 * TILE), BF16)]
+        + [jax.ShapeDtypeStruct((FF // LANES, TOKENS, LANES), F32)] * 2
+        + [jax.ShapeDtypeStruct((TOKENS, D), BF16), jax.ShapeDtypeStruct((D, TOKENS), BF16)],
+        in_specs=[any_space] * 5,
+        out_specs=[pl.BlockSpec(memory_space=pltpu.VMEM)] + [any_space] * 5,
         scratch_shapes=[
             pltpu.VMEM((TOKENS, D), BF16),
             pltpu.VMEM((TOKENS, D), BF16),
@@ -1017,16 +1043,17 @@
             pltpu.VMEM((2, TOKENS, 2 * TILE), BF16),
             pltpu.VMEM((2, D, 2 * TILE), BF16),
             pltpu.VMEM((2, TILE, D), BF16),
-            pltpu.VMEM((TOKENS // PART, 2, LT, PART, LANES), F32),
-            pltpu.SemaphoreType.DMA((4,)),
+            pltpu.VMEM((QUARTERS, 2, LT, PART, LANES), F32),
+            pltpu.SemaphoreType.DMA((2,)),
             pltpu.SemaphoreType.DMA((5, 2)),
-            pltpu.SemaphoreType.DMA((TOKENS // PART, 2)),
+            pltpu.SemaphoreType.DMA((QUARTERS, 2)),
+            pltpu.SemaphoreType.DMA((2, TOKENS // TILE)),
             rs.scratch(),
         ],
         compiler_params=pltpu.CompilerParams(collective_id=collective_id, has_side_effects=True, vmem_limit_bytes=VMEM_ALL),
         cost_estimate=pl.CostEstimate(flops=TOKENS * D * FF * 24, bytes_accessed=TOKENS * FF * 20, transcendentals=0),
-        name="backward",
-    )(gate0, up0, h1, a1, at1, at0, dy, wg, wu, wd)[0]
+        name="gradients",
+    )(x, dy, wg, wu, wd)[0]
 
 
 def solution(mesh):
@@ -1035,8 +1062,7 @@
 
     def step(x, dy, wg, wu, wd, mg, mu, md, vg, vu, vd):
         x, dy = x[0], dy[0]
-        gate0, up0, h1, a1, at1, at0 = forward(x, wg, wu, wd)
-        g = backward(torus, gate0, up0, h1, a1, at1, at0, dy, wg, wu, wd, 1)
+        g = gradients(torus, x, dy, wg, wu, wd, 1)
         G, m, v = step_and_gather(torus, g, (wg, wu, wd), (mg, mu, md), (vg, vu, vd), count, 2)
         return (*unpack(torus, G), *m, *v)
 

time: 444 us -> 422 us (0.950)
  Pallas kernels: 438 us -> 416 us
    pallas_call x2 -> x1, Pallas kernels: 293 us -> 274 us  [gradients(): pl.pallas_call(kernel, out_shape=[jax.ShapeDtypeStruct((LAYERS, 3, 3, CHU...]
where the time goes in v5:
time: 422 us; the launch traced here: 421 us
  Pallas kernels  416 us (99%)
    pallas_call x1, Pallas kernels, gradients(): pl.pallas_call(kernel, out_shape=[jax.ShapeDtypeStruct((LAYERS, 3, 3, CHU...  274 us
    pallas_call x1, Pallas kernels, step_and_gather(): pl.pallas_call(kernel, out_shape=[pltpu.MemorySpace.VMEM(s.shape, s.dtype...  129 us
    pallas_call x1, Pallas kernels, unpack(): pl.pallas_call(kernel, grid=(LAYERS, groups), out_shape=[jax.ShapeDtypeSt...  13.3 us

profile of v5, /device:TPU:8, one launch (start us, length us, event | category | flops | bytes accessed | tf_op | source)
XLA Modules:
  0.0 421.1 jit_solution(18440530916524316428)
XLA Ops:
  0.6 274.0 %gradients.1 = (f32[2,3,3,48,128]{4,3,2,1,0:T(8,128)}, bf16[10,2048,512]{2,1,0:T(8,128)(2,1)}, f32[20,2048,128]{2,1,0:T(8,128)}, f32[20,2048,128]{2,1,0:T(8,128)...) custom-call(bf16[2048,896]{1,0:T(8,128)(2,1)} %bitcast.26, bf16[2048,896]{1,0:T(8,128)(2,1)} %bitcast.27, ...), custom_call_target="tpu_custom_call" | custom-call | flops 112742891520 | bytes 104857600 | tf_op jit(solution)/shard_map/gradients/pallas_call | solution.py:1030
  274.7 129.1 %step_and_gather.1 = (bf16[8,16,2,3,48,128]{5,4,3,2,1,0:T(8,128)(2,1)S(1)}, bf16[4,32,2,3,48,128]{5,4,3,2,1,0:T(8,128)(2,1)S(1)}, bf16[4,32,2,3,48,128]{5,4,3,2,...) custom-call(f32[2,3,3,48,128]{4,3,2,1,0:T(8,128)} %get-tuple-element, ...), custom_call_target="tpu_custom_call" | custom-call | tf_op jit(solution)/shard_map/step_and_gather/pallas_call | solution.py:645
  403.8 13.3 %unpack.1 = (bf16[2,896,2560]{2,1,0:T(8,128)(2,1)}, bf16[2,896,2560]{2,1,0:T(8,128)(2,1)}, bf16[2,2560,896]{2,1,0:T(8,128)(2,1)}) custom-call(bf16[8,16,2,3,48,128]{5,4,3,2,1,0:T(8,128)(2,1)S(1)} %get-tuple-element.23.g0, bf16[4,32,2,3,48,128]{5,4,3,2,1,0:T(8,128)(2,1)S(1)} %get-tuple-element.24.g1, bf16[4,32,2,3,48,128]{5,4,3,2,1,0:T(8,128)(2,1)S(1)} %get-tuple-element.25.g2), custom_call_target="tpu_custom_call" | custom-call | tf_op jit(solution)/shard_map/unpack/pallas_call | solution.py:698
  417.1 0.7 copy.26
  417.8 0.7 copy.27
  418.4 0.7 copy.28
  419.1 0.7 copy.29
  419.8 0.7 copy.30
  420.4 0.7 copy.31

commit v6 on v5

--- a/solution.py
+++ b/solution.py
@@ -12,7 +12,7 @@
 WAYS = (1, -1)
 TRIO = range(3)
 RING, CROSS, DIRECT = TRIO
-NEVER, MARGIN, SWEEPS = 1e9, 0.5, 2
+NEVER, MARGIN, SWEEPS = 1e9, (0.3, 1.2), 3
 
 
 class Torus:
@@ -113,7 +113,7 @@
         while True:
             able = [(max([known.get(c, NEVER) for c in actions[a][0]], default=0.0), i, a) for i, a in enumerate(left) if allowed(a)]
             best, _, a = min(able, default=(NEVER, 0, None))
-            if best >= NEVER or not wait and best + MARGIN > now:
+            if best >= NEVER or not wait and best + MARGIN[a[0][0][0]] > now:
                 return
             now = max(now, best)
             do(a, where)
@@ -371,7 +371,7 @@
 
 
 class AllGather:
-    def __init__(self, torus, block_bytes, split=2):
+    def __init__(self, torus, block_bytes, split=4):
         self.t, self.bytes, self.split = torus, block_bytes, split
         self.dims = [tuple(order) for order in ORDERS]
         self.flip, self.balance = {}, Balance()
@@ -644,7 +644,7 @@
     k = len(ag.copies)
     got = pl.pallas_call(
         kernel,
-        out_shape=[pltpu.MemorySpace.VMEM(s.shape, s.dtype) for s in shapes] + f32 * 2,
+        out_shape=[pltpu.MemorySpace.VMEM(s.shape, s.dtype) for s in shapes + f32 * 2],
         in_specs=[vmem] + [pl.BlockSpec(memory_space=pl.ANY)] * 3 + [vmem] * 6,
         out_specs=[vmem] * 9,
         scratch_shapes=[
@@ -663,10 +663,10 @@
         compiler_params=pltpu.CompilerParams(collective_id=collective_id, has_side_effects=True, vmem_limit_bytes=26 * MIB),
         name="step_and_gather",
     )(g, *w, *m, *v)
-    return got[:3], turn(got[3:6]), turn(got[6:])
-
-
-def unpack(torus, G):
+    return got
+
+
+def unpack(torus, got):
     nx, ny, nz = (torus.n[d] for d in "xyz")
     pair = 2
     group = pair * nz
@@ -674,8 +674,20 @@
     pairs = ny // pair
 
     def kernel(g0, g1, g2, *refs):
-        outs, Z, Y = refs[:3], refs[3], refs[4]
+        moments, outs, kept, (Z, Y, sem) = refs[:6], refs[6:9], refs[9:15], refs[15:]
         l, s = pl.program_id(0), pl.program_id(1)
+        copies = [pltpu.make_async_copy(src, dst, sem.at[i]) for i, (src, dst) in enumerate(zip(moments, kept))]
+
+        @pl.when(l + s == 0)
+        def _():
+            for copy in copies:
+                copy.start()
+
+        @pl.when(l + s == LAYERS - 1 + groups - 1)
+        def _():
+            for copy in copies:
+                copy.wait()
+
         corner = {"x": lax.div(s, pairs), "y": lax.rem(s, pairs) * pair, "z": 0}
         for u in TRIO:
             high, wide = HIGH[u], WIDE[u] // LANES
@@ -698,13 +710,17 @@
     return pl.pallas_call(
         kernel,
         grid=(LAYERS, groups),
-        out_shape=[jax.ShapeDtypeStruct(s, BF16) for s in shapes],
-        in_specs=[pl.BlockSpec(memory_space=pltpu.VMEM)] * 3,
-        out_specs=[pl.BlockSpec((1, HIGH[u] * group, WIDE[u]), lambda l, s: (l, s, 0)) for u in TRIO],
-        scratch_shapes=[pltpu.VMEM((group, ROWS + 8, LANES), F32), pltpu.VMEM((FF // LANES, HIGH[2] * group + 8, LANES), F32)],
+        out_shape=[jax.ShapeDtypeStruct(s, BF16) for s in shapes] + [jax.ShapeDtypeStruct(m.shape, F32) for m in got[3:]],
+        in_specs=[pl.BlockSpec(memory_space=pltpu.VMEM)] * 9,
+        out_specs=[pl.BlockSpec((1, HIGH[u] * group, WIDE[u]), lambda l, s: (l, s, 0)) for u in TRIO] + [pl.BlockSpec(memory_space=pl.ANY)] * 6,
+        scratch_shapes=[
+            pltpu.VMEM((group, ROWS + 8, LANES), F32),
+            pltpu.VMEM((FF // LANES, HIGH[2] * group + 8, LANES), F32),
+            pltpu.SemaphoreType.DMA((6,)),
+        ],
         compiler_params=pltpu.CompilerParams(vmem_limit_bytes=26 * MIB),
         name="unpack",
-    )(*G)
+    )(*got)
 
 
 NN, NT = ((1,), (0,)), ((1,), (1,))
@@ -722,14 +738,14 @@
 SIDE_STRIDE, DOWN_STRIDE = D + GAP, FF // HALVES + GAP
 DOWN_BASE = RING_TILES * SIDE_STRIDE
 X_ROWS = DOWN_BASE + D // LANES * DOWN_STRIDE
-COST = {"last": (3.8, 2.3, 1.3), "first": (1.7, 2.3, 1.3), "da": (2.4,), "norm": (0.45,)}
+COST = {"last": (3.5, 3.5), "first": (1.8, 3.5), "da": (2.5,), "norm": (0.45,)}
 PACK_DOWN = 0.4
 WHOLE = ((0,), (1, 2), (3, 4), (5, 6), (7, 8))
 CHUNKS = {1: 0, 3: 1, 4: 2}
 PASSES = ("forward", "last", "da", "norm", "first")
 COUNT = {"forward": STEPS, "last": STEPS, "da": STEPS, "norm": TOKENS // TILE, "first": STEPS}
 QUARTERS = TOKENS // PART
-SIDE, DOWN = 1, 2
+MAKE = 1
 
 
 def timeline():
@@ -740,15 +756,17 @@
             half, tt = divmod(t, HALF)
             for i, cost in enumerate(COST[kind]):
                 writes, whole = [], []
-                if i == SIDE:
+                if i == MAKE:
                     unit = (layer, half)
-                    writes = [(unit, c) for c in TRIO] if tt == 0 else []
-                    whole = [((unit, COLOURS[half][CHUNKS[tt]]), lane) for lane in range(lanes)] if tt in CHUNKS else []
-                if i == DOWN and tt == HALF - 1:
-                    cost += PACK_DOWN
-                    mine = [((layer, HALVES), c) for c in TRIO]
-                    writes = [] if half else mine
-                    whole = [(key, lane) for key in mine for lane in range(lanes) if half or lane == 0 and ORDERS[key[1]][CROSS] == "x"]
+                    if tt == 0:
+                        writes += [(unit, c) for c in TRIO]
+                    if tt in CHUNKS:
+                        whole += [((unit, COLOURS[half][CHUNKS[tt]]), lane) for lane in range(lanes)]
+                    if tt == HALF - 1:
+                        cost += PACK_DOWN
+                        mine = [((layer, HALVES), c) for c in TRIO]
+                        writes += [] if half else mine
+                        whole += [(key, lane) for key in mine for lane in range(lanes) if half or lane == 0 and ORDERS[key[1]][CROSS] == "x"]
                 out.append(((kind, t, i), cost, writes, whole))
     return out
 
@@ -917,25 +935,20 @@
                         for f in hiddens(t + 1, quarters):
                             f.start()
 
-        def side(kind, t, s):
-            tt = lax.rem(t, HALF)
+        def make(kind, t, s):
+            half, tt = lax.div(t, HALF), lax.rem(t, HALF)
             got = dot(at[...], Db[s])
             for k in range(2 * LT):
                 X[pl.ds((lax.rem(tt, 2) * 2 * LT + k) * SIDE_STRIDE + 8, D), :] = got[:, lanes_of(k)]
-            point(kind, t, SIDE, 0)
-            half = lax.div(t, HALF)
+            got = dot(Mb[...], dyv[...])
+            for ct in range(D // LANES):
+                X[pl.ds(DOWN_BASE + ct * DOWN_STRIDE + 8 + tt * TILE, TILE), :] = got[:, lanes_of(ct)]
+            point(kind, t, MAKE, 0)
             for v, parts in enumerate(WHOLE):
 
                 @pl.when(tt == v)
                 def _(parts=parts):
                     pack(torus, 0, X, lambda ct: ct % RING_TILES * SIDE_STRIDE + 8, parts, 0, lines, [T.at[half] for T in it.T], COLOURS[0])
-
-        def down(kind, t, s):
-            half, tt = lax.div(t, HALF), lax.rem(t, HALF)
-            got = dot(Mb[...], dyv[...])
-            for ct in range(D // LANES):
-                X[pl.ds(DOWN_BASE + ct * DOWN_STRIDE + 8 + tt * TILE, TILE), :] = got[:, lanes_of(ct)]
-            point(kind, t, DOWN, 0)
 
             @pl.when(tt == HALF - 1)
             def _():
@@ -1009,10 +1022,8 @@
                     if kind == "last":
                         save(t, s).start()
                     point(kind, t, 0, 1)
-                    side(kind, t, s)
-                    point(kind, t, SIDE, 1)
-                    down(kind, t, s)
-                    point(kind, t, DOWN, 1)
+                    make(kind, t, s)
+                    point(kind, t, MAKE, 1)
                 else:
                     {"forward": forward, "da": d_a, "norm": norm}[kind](t, s)
                     if kind != "forward":
@@ -1063,8 +1074,9 @@
     def step(x, dy, wg, wu, wd, mg, mu, md, vg, vu, vd):
         x, dy = x[0], dy[0]
         g = gradients(torus, x, dy, wg, wu, wd, 1)
-        G, m, v = step_and_gather(torus, g, (wg, wu, wd), (mg, mu, md), (vg, vu, vd), count, 2)
-        return (*unpack(torus, G), *m, *v)
+        got = step_and_gather(torus, g, (wg, wu, wd), (mg, mu, md), (vg, vu, vd), count, 2)
+        new = unpack(torus, got)
+        return (*new[:3], *(jnp.transpose(t, (1, 0, 2)) for t in new[3:]))
 
     P = jax.sharding.PartitionSpec
     return jax.shard_map(

time: 422 us -> 415 us (0.983)
  no operation moved by 1% of the time
where the time goes in v6:
time: 415 us; the launch traced here: 414 us
  Pallas kernels  414 us (100%)
    pallas_call x1, Pallas kernels, gradients(): pl.pallas_call(kernel, out_shape=[jax.ShapeDtypeStruct((LAYERS, 3, 3, CHU...  271 us
    pallas_call x1, Pallas kernels, step_and_gather(): pl.pallas_call(kernel, out_shape=[pltpu.MemorySpace.VMEM(s.shape, s.dtype...  129 us
    pallas_call x1, Pallas kernels, unpack(): pl.pallas_call(kernel, grid=(LAYERS, groups), out_shape=[jax.ShapeDtypeSt...  13.5 us

profile of v6, /device:TPU:8, one launch (start us, length us, event | category | flops | bytes accessed | tf_op | source)
XLA Modules:
  0.0 414.4 jit_solution(8706564518294898479)
XLA Ops:
  0.6 270.9 %gradients.1 = (f32[2,3,3,48,128]{4,3,2,1,0:T(8,128)}, bf16[10,2048,512]{2,1,0:T(8,128)(2,1)}, f32[20,2048,128]{2,1,0:T(8,128)}, f32[20,2048,128]{2,1,0:T(8,128)...) custom-call(bf16[2048,896]{1,0:T(8,128)(2,1)} %bitcast.20, bf16[2048,896]{1,0:T(8,128)(2,1)} %bitcast.21, ...), custom_call_target="tpu_custom_call" | custom-call | flops 112742891520 | bytes 104857600 | tf_op jit(solution)/shard_map/gradients/pallas_call | solution.py:1041
  271.5 129.1 %step_and_gather.1 = (bf16[8,16,2,3,48,128]{5,4,3,2,1,0:T(8,128)(2,1)S(1)}, bf16[4,32,2,3,48,128]{5,4,3,2,1,0:T(8,128)(2,1)S(1)}, bf16[4,32,2,3,48,128]{5,4,3,2,...) custom-call(f32[2,3,3,48,128]{4,3,2,1,0:T(8,128)} %get-tuple-element, ...), custom_call_target="tpu_custom_call" | custom-call | tf_op jit(solution)/shard_map/step_and_gather/pallas_call | solution.py:645
  400.6 13.5 %unpack.1 = (bf16[2,896,2560]{2,1,0:T(8,128)(2,1)}, bf16[2,896,2560]{2,1,0:T(8,128)(2,1)}, bf16[2,2560,896]{2,1,0:T(8,128)(2,1)}, f32[7,2,2560]{2,1,0:T(2,128)},...) custom-call(bf16[8,16,2,3,48,128]{5,4,3,2,1,0:T(8,128)(2,1)S(1)} %ge, ...), custom_call_target="tpu_custom_call" | custom-call | tf_op jit(solution)/shard_map/unpack/pallas_call | solution.py:710

commit v7 on v6

--- a/solution.py
+++ b/solution.py
@@ -131,11 +131,14 @@
     return slots
 
 
-def barrier(me, peers):
+def arrive(me, peers):
     sem = pltpu.get_barrier_semaphore()
     for dim, delta in peers:
         pl.semaphore_signal(sem, inc=1, device_id=me.peer(dim, delta), device_id_type=MESH)
-    pl.semaphore_wait(sem, len(peers))
+
+
+def meet(peers):
+    pl.semaphore_wait(pltpu.get_barrier_semaphore(), len(peers))
 
 
 def both_ways(torus, dim):
@@ -491,6 +494,7 @@
 VMEM_ALL = 67043328
 LAYERS, D, FF = 2, 896, 2560
 LANES, ROWS, CHUNK = 128, 144, 48
+USED = 140
 HIGH = {0: 7, 1: 7, 2: 20}
 WIDE = {0: FF, 1: FF, 2: D}
 WINDOW = (16, 16, 24)
@@ -549,16 +553,8 @@
     lax.fori_loop(0, count, body, 0)
 
 
-def pieces_shapes(torus, dtype, *mid):
-    out = []
-    for order in ORDERS:
-        a, b, d = (torus.n[x] for x in order)
-        out.append(jax.ShapeDtypeStruct((a, b * d) + mid + (CHUNK, LANES), dtype))
-    return out
-
-
 def step_and_gather(torus, g, w, m, v, count, collective_id):
-    ag = AllGather(torus, LAYERS * 3 * CHUNK * 256)
+    ag = AllGather(torus, LAYERS * USED * 256)
     dims = "zxy"
     slots = {d: torus.n[d] - 1 for d in dims}
 
@@ -577,11 +573,8 @@
             first, rows = window(p, x)
             loads.append(pltpu.make_async_copy(w_in[x].at[:, pl.ds(first, rows)], win[x], wsem.at[x]))
             loads[x].start()
-        barrier(me, [p for d in "xyz" for p in all_others(torus, d)])
-        for x in TRIO:
-            loads[x].wait()
-            for lt in range(WIDE[x] // LANES):
-                wide_win[x][:, lt] = win[x][:, :, pl.ds(lt * LANES, LANES)].astype(F32)
+        peers = [p for d in "xyz" for p in all_others(torus, d)]
+        arrive(me, peers)
         acc = jnp.zeros((8, LANES), F32)
         for l in range(LAYERS):
             for u in TRIO:
@@ -591,6 +584,7 @@
                     for r in range(0, CHUNK, 8):
                         acc = acc + value[r : r + 8] * value[r : r + 8]
         part[0] = acc
+        meet(peers)
         base = 0
         for i, d in enumerate(dims):
             n = torus.n[d]
@@ -600,6 +594,11 @@
                 copies.append(pltpu.make_async_remote_copy(src_ref=part.at[i], dst_ref=E.at[s], send_sem=esend.at[s], recv_sem=erecv.at[s], device_id=me.peer(d, rel), device_id_type=MESH))
             for copy in copies:
                 copy.start()
+            if i == 0:
+                for x in TRIO:
+                    loads[x].wait()
+                    for lt in range(WIDE[x] // LANES):
+                        wide_win[x][:, lt] = win[x][:, :, pl.ds(lt * LANES, LANES)].astype(F32)
             total = part[i]
             for rel in range(1, n):
                 copies[rel - 1].wait_recv()
@@ -613,7 +612,6 @@
         for l in range(LAYERS):
             for u in TRIO:
                 high = HIGH[u]
-                wflat[l, u, pl.ds(ROWS - 8, 8), :] = jnp.zeros((8, LANES), F32)
                 for ct in range(WIDE[u] // LANES):
                     x, lt = home(u, ct)
                     at = (slice(None), l, pl.ds(lt * LANES, LANES))
@@ -624,20 +622,18 @@
                     new_w = wide - 0.02 * (new_m * lax.rsqrt(new_v + 1e-8) + 0.1 * wide)
                     m_out[x][at] = new_m
                     v_out[x][at] = new_v
-                    wflat[l, u, pl.ds(ct * high, high), :] = new_w
+                    wflat[u, pl.ds(l * USED + ct * high, high), :] = new_w
         it = ag.bind(me, G, ssem, rsem)
         for u in TRIO:
-            for k, c in enumerate(COLOURS[u]):
-                a, b, d = (me.up(x, 0) for x in ORDERS[c])
-                for l in range(LAYERS):
-                    G[c][a, b * torus.n[ORDERS[c][DIRECT]] + d, l, u] = wflat[l, u, pl.ds(k * CHUNK, CHUNK), :].astype(BF16)
+            a, b, d = (me.up(x, 0) for x in ORDERS[u])
+            G[u][a, b * torus.n[ORDERS[u][DIRECT]] + d] = wflat[u].astype(BF16)
         for a in ag.order:
             it.run(a)
         it.wait_sends()
 
     vmem = pl.BlockSpec(memory_space=pltpu.VMEM)
     nsum = sum(slots.values())
-    shapes = pieces_shapes(torus, BF16, LAYERS, 3)
+    shapes = [jax.ShapeDtypeStruct((torus.n[a], torus.n[b] * torus.n[d], LAYERS * USED, LANES), BF16) for a, b, d in ORDERS]
     turn = lambda ts: [jnp.transpose(t, (1, 0, 2)) for t in ts]
     m, v = turn(m), turn(v)
     f32 = [jax.ShapeDtypeStruct(t.shape, F32) for t in m]
@@ -649,7 +645,7 @@
         out_specs=[vmem] * 9,
         scratch_shapes=[
             pltpu.VMEM((LAYERS, 3, ROWS, LANES), F32),
-            pltpu.VMEM((LAYERS, 3, ROWS, LANES), F32),
+            pltpu.VMEM((3, LAYERS * USED, LANES), F32),
             pltpu.VMEM((4, 8, LANES), F32),
             pltpu.VMEM((nsum, 8, LANES), F32),
             pltpu.SemaphoreType.DMA((nsum,)),
@@ -672,6 +668,7 @@
     group = pair * nz
     groups = torus.size // group
     pairs = ny // pair
+    skip = LAYERS * USED - ROWS
 
     def kernel(g0, g1, g2, *refs):
         moments, outs, kept, (Z, Y, sem) = refs[:6], refs[6:9], refs[9:15], refs[15:]
@@ -694,13 +691,12 @@
             for i in range(group):
                 y, z = divmod(i, nz)
                 at = corner | {"y": corner["y"] + y, "z": z}
-                for k, c in enumerate(COLOURS[u]):
-                    a, b, d = ORDERS[c]
-                    Z[i, pl.ds(k * CHUNK, CHUNK), :] = (g0, g1, g2)[c][at[a], at[b] * torus.n[d] + at[d], l, u].astype(F32)
+                a, b, d = ORDERS[u]
+                Z[i, pl.ds(0, ROWS), :] = (g0, g1, g2)[u][at[a], at[b] * torus.n[d] + at[d], pl.ds(l * skip, ROWS), :].astype(F32)
             for i in range(group):
                 for ct in range(wide):
                     for r in range(0, high, 8):
-                        Y[ct, pl.ds(high * i + r, 8), :] = Z[i, pl.ds(high * ct + r, 8), :]
+                        Y[ct, pl.ds(high * i + r, 8), :] = Z[i, pl.ds(l * (USED - skip) + high * ct + r, 8), :]
             rows = high * group
             for ct in range(wide):
                 x, lt = home(u, ct)
@@ -971,7 +967,7 @@
 
         for f in fetch("forward", 0, 0) + [load_x]:
             f.start()
-        barrier(me, rs.peers())
+        arrive(me, rs.peers())
         load_x.wait()
 
         @pl.loop(0, TOKENS // TILE)
@@ -984,6 +980,7 @@
             following = PASSES[number + 1] if number + 1 < len(PASSES) else None
             if kind == "last":
                 turn()
+                meet(rs.peers())
             if kind == "da":
                 load_at0.start()
             if kind == "norm":

time: 415 us -> 418 us (level)
  local copies, waits for them, and re-layouts: 0 us -> 5.44 us
    unnamed x0 -> x12, local copies, waits for them, and re-layouts: none -> 5.44 us
where the time goes in v7:
time: 418 us
  Pallas kernels  412 us (99%)
  local copies, waits for them, and re-layouts  5.44 us (1%)
    pallas_call x1, Pallas kernels, gradients(): pl.pallas_call(kernel, out_shape=[jax.ShapeDtypeStruct((LAYERS, 3, 3, CHU...  269 us
    pallas_call x1, Pallas kernels, step_and_gather(): pl.pallas_call(kernel, out_shape=[pltpu.MemorySpace.VMEM(s.shape, s.dtype...  129 us
    pallas_call x1, Pallas kernels, unpack(): pl.pallas_call(kernel, grid=(LAYERS, groups), out_shape=[jax.ShapeDtypeSt...  13.4 us

profile of v7, /device:TPU:8, one launch (start us, length us, event | category | flops | bytes accessed | tf_op | source)
XLA Modules:
  0.0 417.8 jit_solution(296107985239955207)
XLA Ops:
  0.6 269.3 %gradients.1 = (f32[2,3,3,48,128]{4,3,2,1,0:T(8,128)}, bf16[10,2048,512]{2,1,0:T(8,128)(2,1)}, f32[20,2048,128]{2,1,0:T(8,128)}, f32[20,2048,128]{2,1,0:T(8,128)...) custom-call(bf16[2048,896]{1,0:T(8,128)(2,1)} %bitcast.20, bf16[2048,896]{1,0:T(8,128)(2,1)} %bitcast.21, ...), custom_call_target="tpu_custom_call" | custom-call | flops 112742891520 | bytes 104857600 | tf_op jit(solution)/shard_map/gradients/pallas_call | solution.py:1038
  270.0 0.0 copy-start
  270.0 0.9 copy-done
  270.9 0.0 copy-start.1
  270.9 0.9 copy-done.1
  271.8 0.0 copy-start.2
  271.8 0.9 copy-done.2
  272.7 0.0 copy-start.3
  272.7 0.9 copy-done.3
  273.6 0.0 copy-start.4
  273.6 0.9 copy-done.4
  274.5 0.0 copy-start.5
  274.5 0.9 copy-done.5
  275.4 128.8 %step_and_gather.1 = (bf16[8,16,280,128]{3,2,1,0:T(8,128)(2,1)S(1)}, bf16[4,32,280,128]{3,2,1,0:T(8,128)(2,1)S(1)}, bf16[4,32,280,128]{3,2,1,0:T(8,128)(2,1)S(1)...) custom-call(f32[2,3,3,48,128]{4,3,2,1,0:T(8,128)} %get-tuple-element, ...), custom_call_target="tpu_custom_call" | custom-call | tf_op jit(solution)/shard_map/step_and_gather/pallas_call | solution.py:641
  404.3 13.4 %unpack.1 = (bf16[2,896,2560]{2,1,0:T(8,128)(2,1)}, bf16[2,896,2560]{2,1,0:T(8,128)(2,1)}, bf16[2,2560,896]{2,1,0:T(8,128)(2,1)}, f32[7,2,2560]{2,1,0:T(2,128)},...) custom-call(bf16[8,16,280,128]{3,2,1,0:T(8,128)(2,1)S(1)} %get-tuple, ...), custom_call_target="tpu_custom_call" | custom-call | tf_op jit(solution)/shard_map/unpack/pallas_call | solution.py:706
Async XLA Ops:
  270.0 0.9 copy-start
  270.9 0.9 copy-start.1
  271.8 0.9 copy-start.2
  272.7 0.9 copy-start.3
  273.6 0.9 copy-start.4
  274.5 0.9 copy-start.5

commit v8 on v7

--- a/solution.py
+++ b/solution.py
@@ -34,6 +34,9 @@
         self.to = {d: [p + (self.at[d][i] - mine[d]) * step[d] for i in range(n[d])] for d in n}
 
     def peer(self, dim, delta):
+        if dim == "xy":
+            dx, dy = delta
+            return {"dp": self.to["x"][dx] + self.to["y"][dy] - self.to["x"][0]}
         return {"dp": self.to[dim][delta % len(self.to[dim])]}
 
     def up(self, dim, delta):
@@ -493,8 +496,7 @@
 MIB = 2**20
 VMEM_ALL = 67043328
 LAYERS, D, FF = 2, 896, 2560
-LANES, ROWS, CHUNK = 128, 144, 48
-USED = 140
+LANES, SUB, ROWS, CHUNK = 128, 8, 144, 48
 HIGH = {0: 7, 1: 7, 2: 20}
 WIDE = {0: FF, 1: FF, 2: D}
 WINDOW = (16, 16, 24)
@@ -518,26 +520,26 @@
 def tiles(u):
     high, wide = HIGH[u], WIDE[u] // LANES
     out = []
-    for k in range(ROWS // 8):
-        ct, row = divmod(8 * k, high)
-        out.append((ct, row, min(8, high - row), ct + 1 < wide))
+    for k in range(ROWS // SUB):
+        ct, row = divmod(SUB * k, high)
+        out.append((ct, row, min(SUB, high - row), ct + 1 < wide))
     return out
 
 
 def pack(torus, u, X, base, parts, first, count, outs, colours):
     high, ny, nz = HIGH[u], torus.n["y"], torus.n["z"]
-    sub = lax.broadcasted_iota(jnp.int32, (8, LANES), 0)
+    sub = lax.broadcasted_iota(jnp.int32, (SUB, LANES), 0)
     got = tiles(u)
 
     def body(line, carry):
         x, y = lax.div(first + line, ny), lax.rem(first + line, ny)
-        top = pl.multiple_of(line * (high * nz), 8)
+        top = pl.multiple_of(line * (high * nz), SUB)
 
         def piece(z, ct, row, whole, more):
-            a = X[pl.ds(top + (base(ct) + high * z + row), 8), :]
-            if whole == 8:
+            a = X[pl.ds(top + (base(ct) + high * z + row), SUB), :]
+            if whole == SUB:
                 return a
-            b = X[pl.ds(top + (base(ct + 1) + high * z - whole), 8), :] if more else jnp.zeros((8, LANES), F32)
+            b = X[pl.ds(top + (base(ct + 1) + high * z - whole), SUB), :] if more else jnp.zeros((SUB, LANES), F32)
             return jnp.where(sub < whole, a, b)
 
         for z in range(nz):
@@ -554,14 +556,14 @@
 
 
 def step_and_gather(torus, g, w, m, v, count, collective_id):
-    ag = AllGather(torus, LAYERS * USED * 256)
-    dims = "zxy"
-    slots = {d: torus.n[d] - 1 for d in dims}
+    ag = AllGather(torus, LAYERS * 3 * CHUNK * 256)
+    plane = [("xy", (i, j)) for i in range(torus.n["x"]) for j in range(torus.n["y"]) if i + j]
+    rounds = all_others(torus, "z"), plane
 
     def window(p, x):
         rows = WINDOW[x]
-        first = lax.div(p * HIGH[x], 8) * 8
-        return pl.multiple_of(jnp.minimum(first, HIGH[x] * torus.size - rows), 8), rows
+        first = lax.div(p * HIGH[x], SUB) * SUB
+        return pl.multiple_of(jnp.minimum(first, HIGH[x] * torus.size - rows), SUB), rows
 
     def kernel(g_ref, *refs):
         w_in, m_in, v_in, G, m_out, v_out = (refs[i : i + 3] for i in range(0, 18, 3))
@@ -573,24 +575,22 @@
             first, rows = window(p, x)
             loads.append(pltpu.make_async_copy(w_in[x].at[:, pl.ds(first, rows)], win[x], wsem.at[x]))
             loads[x].start()
-        peers = [p for d in "xyz" for p in all_others(torus, d)]
+        peers = rounds[0] + rounds[1]
         arrive(me, peers)
-        acc = jnp.zeros((8, LANES), F32)
+        acc = jnp.zeros((SUB, LANES), F32)
         for l in range(LAYERS):
             for u in TRIO:
                 for k, c in enumerate(COLOURS[u]):
                     value = g_ref[l, u, c]
                     flat[l, u, pl.ds(k * CHUNK, CHUNK), :] = value
-                    for r in range(0, CHUNK, 8):
-                        acc = acc + value[r : r + 8] * value[r : r + 8]
+                    for r in range(0, CHUNK, SUB):
+                        acc = acc + value[r : r + SUB] * value[r : r + SUB]
         part[0] = acc
         meet(peers)
         base = 0
-        for i, d in enumerate(dims):
-            n = torus.n[d]
+        for i, others in enumerate(rounds):
             copies = []
-            for rel in range(1, n):
-                s = base + rel - 1
+            for s, (d, rel) in enumerate(others, base):
                 copies.append(pltpu.make_async_remote_copy(src_ref=part.at[i], dst_ref=E.at[s], send_sem=esend.at[s], recv_sem=erecv.at[s], device_id=me.peer(d, rel), device_id_type=MESH))
             for copy in copies:
                 copy.start()
@@ -600,18 +600,19 @@
                     for lt in range(WIDE[x] // LANES):
                         wide_win[x][:, lt] = win[x][:, :, pl.ds(lt * LANES, LANES)].astype(F32)
             total = part[i]
-            for rel in range(1, n):
-                copies[rel - 1].wait_recv()
-                total = total + E[base + rel - 1]
+            for s, copy in enumerate(copies, base):
+                copy.wait_recv()
+                total = total + E[s]
             part[i + 1] = total
             for copy in copies:
                 copy.wait_send()
-            base += n - 1
-        mean = jnp.sum(part[3], keepdims=True) / count
+            base += len(others)
+        mean = jnp.sum(part[2], keepdims=True) / count
         factor = jnp.minimum(1.0, 0.5 * lax.rsqrt(mean + 1e-30))
         for l in range(LAYERS):
             for u in TRIO:
                 high = HIGH[u]
+                wflat[l, u, pl.ds(ROWS - SUB, SUB), :] = jnp.zeros((SUB, LANES), F32)
                 for ct in range(WIDE[u] // LANES):
                     x, lt = home(u, ct)
                     at = (slice(None), l, pl.ds(lt * LANES, LANES))
@@ -622,18 +623,20 @@
                     new_w = wide - 0.02 * (new_m * lax.rsqrt(new_v + 1e-8) + 0.1 * wide)
                     m_out[x][at] = new_m
                     v_out[x][at] = new_v
-                    wflat[u, pl.ds(l * USED + ct * high, high), :] = new_w
+                    wflat[l, u, pl.ds(ct * high, high), :] = new_w
         it = ag.bind(me, G, ssem, rsem)
         for u in TRIO:
-            a, b, d = (me.up(x, 0) for x in ORDERS[u])
-            G[u][a, b * torus.n[ORDERS[u][DIRECT]] + d] = wflat[u].astype(BF16)
+            for c in TRIO:
+                a, b, d = (me.up(x, 0) for x in ORDERS[c])
+                for l in range(LAYERS):
+                    G[c][a, b * torus.n[ORDERS[c][DIRECT]] + d, l, u] = wflat[l, u, pl.ds(c * CHUNK, CHUNK), :].astype(BF16)
         for a in ag.order:
             it.run(a)
         it.wait_sends()
 
     vmem = pl.BlockSpec(memory_space=pltpu.VMEM)
-    nsum = sum(slots.values())
-    shapes = [jax.ShapeDtypeStruct((torus.n[a], torus.n[b] * torus.n[d], LAYERS * USED, LANES), BF16) for a, b, d in ORDERS]
+    nsum = len(rounds[0]) + len(rounds[1])
+    shapes = [jax.ShapeDtypeStruct((torus.n[a], torus.n[b] * torus.n[d], LAYERS, 3, CHUNK, LANES), BF16) for a, b, d in ORDERS]
     turn = lambda ts: [jnp.transpose(t, (1, 0, 2)) for t in ts]
     m, v = turn(m), turn(v)
     f32 = [jax.ShapeDtypeStruct(t.shape, F32) for t in m]
@@ -645,9 +648,9 @@
         out_specs=[vmem] * 9,
         scratch_shapes=[
             pltpu.VMEM((LAYERS, 3, ROWS, LANES), F32),
-            pltpu.VMEM((3, LAYERS * USED, LANES), F32),
-            pltpu.VMEM((4, 8, LANES), F32),
-            pltpu.VMEM((nsum, 8, LANES), F32),
+            pltpu.VMEM((LAYERS, 3, ROWS, LANES), F32),
+            pltpu.VMEM((3, SUB, LANES), F32),
+            pltpu.VMEM((nsum, SUB, LANES), F32),
             pltpu.SemaphoreType.DMA((nsum,)),
             pltpu.SemaphoreType.DMA((nsum,)),
             pltpu.SemaphoreType.DMA((k,)),
@@ -668,7 +671,6 @@
     group = pair * nz
     groups = torus.size // group
     pairs = ny // pair
-    skip = LAYERS * USED - ROWS
 
     def kernel(g0, g1, g2, *refs):
         moments, outs, kept, (Z, Y, sem) = refs[:6], refs[6:9], refs[9:15], refs[15:]
@@ -691,12 +693,19 @@
             for i in range(group):
                 y, z = divmod(i, nz)
                 at = corner | {"y": corner["y"] + y, "z": z}
-                a, b, d = ORDERS[u]
-                Z[i, pl.ds(0, ROWS), :] = (g0, g1, g2)[u][at[a], at[b] * torus.n[d] + at[d], pl.ds(l * skip, ROWS), :].astype(F32)
+                for c, ref in enumerate((g0, g1, g2)):
+                    a, b, d = ORDERS[c]
+                    chunk = ref[at[a], at[b] * torus.n[d] + at[d], l, u].astype(F32)
+                    if high > SUB:
+                        for k, (ct, row, whole, more) in enumerate(tiles(u)[c * CHUNK // SUB : (c + 1) * CHUNK // SUB]):
+                            Y[ct, pl.ds(high * i + row, whole), :] = chunk[SUB * k : SUB * k + whole]
+                            if more and whole < SUB:
+                                Y[ct + 1, pl.ds(high * i, SUB - whole), :] = chunk[SUB * k + whole : SUB * k + SUB]
+                    else:
+                        Z[i, pl.ds(c * CHUNK, CHUNK), :] = chunk
             for i in range(group):
-                for ct in range(wide):
-                    for r in range(0, high, 8):
-                        Y[ct, pl.ds(high * i + r, 8), :] = Z[i, pl.ds(l * (USED - skip) + high * ct + r, 8), :]
+                for ct in range(wide if high <= SUB else 0):
+                    Y[ct, pl.ds(high * i, SUB), :] = Z[i, pl.ds(high * ct, SUB), :]
             rows = high * group
             for ct in range(wide):
                 x, lt = home(u, ct)
@@ -710,8 +719,8 @@
         in_specs=[pl.BlockSpec(memory_space=pltpu.VMEM)] * 9,
         out_specs=[pl.BlockSpec((1, HIGH[u] * group, WIDE[u]), lambda l, s: (l, s, 0)) for u in TRIO] + [pl.BlockSpec(memory_space=pl.ANY)] * 6,
         scratch_shapes=[
-            pltpu.VMEM((group, ROWS + 8, LANES), F32),
-            pltpu.VMEM((FF // LANES, HIGH[2] * group + 8, LANES), F32),
+            pltpu.VMEM((group, ROWS + SUB, LANES), F32),
+            pltpu.VMEM((FF // LANES, HIGH[2] * group + SUB, LANES), F32),
             pltpu.SemaphoreType.DMA((6,)),
         ],
         compiler_params=pltpu.CompilerParams(vmem_limit_bytes=26 * MIB),
@@ -793,7 +802,6 @@
         me = torus.here()
         it = rs.bind(me, rsc)
         copy = pltpu.make_async_copy
-        load_x = copy(x_ref, dyv, once.at[0])
         save_at0, load_at0 = copy(at, at0_ref, once.at[1]), copy(at0_ref, at, once.at[1])
 
         def part(i):
@@ -965,13 +973,16 @@
             inner = jnp.mean(da * wide, -1, keepdims=True)
             dyv[part(t), :] = dyv[part(t), :] + (scale * da - wide * (scale * scale * scale * inner)).astype(BF16)
 
-        for f in fetch("forward", 0, 0) + [load_x]:
+        def load_x(r):
+            return copy(x_ref.at[part(r)], dyv.at[part(r)], rsem.at[0, r])
+
+        for f in [load_x(r) for r in range(TOKENS // TILE)] + fetch("forward", 0, 0):
             f.start()
         arrive(me, rs.peers())
-        load_x.wait()
 
         @pl.loop(0, TOKENS // TILE)
         def _(r):
+            load_x(r).wait()
             normed_into(r)
 
         save_at0.start()

time: 418 us -> 414 us (level)
  local copies, waits for them, and re-layouts: 5.44 us -> 0 us
    unnamed x12 -> x0, local copies, waits for them, and re-layouts: 5.44 us -> none
where the time goes in v8:
time: 414 us; the launch traced here: 413 us
  Pallas kernels  412 us (100%)
    pallas_call x1, Pallas kernels, gradients(): pl.pallas_call(kernel, out_shape=[jax.ShapeDtypeStruct((LAYERS, 3, 3, CHU...  268 us
    pallas_call x1, Pallas kernels, step_and_gather(): pl.pallas_call(kernel, out_shape=[pltpu.MemorySpace.VMEM(s.shape, s.dtype...  131 us
    pallas_call x1, Pallas kernels, unpack(): pl.pallas_call(kernel, grid=(LAYERS, groups), out_shape=[jax.ShapeDtypeSt...  13.1 us

profile of v8, /device:TPU:8, one launch (start us, length us, event | category | flops | bytes accessed | tf_op | source)
XLA Modules:
  0.0 412.7 jit_solution(11619238982001161381)
XLA Ops:
  0.6 268.2 %gradients.1 = (f32[2,3,3,48,128]{4,3,2,1,0:T(8,128)}, bf16[10,2048,512]{2,1,0:T(8,128)(2,1)}, f32[20,2048,128]{2,1,0:T(8,128)}, f32[20,2048,128]{2,1,0:T(8,128)...) custom-call(bf16[2048,896]{1,0:T(8,128)(2,1)} %bitcast.20, bf16[2048,896]{1,0:T(8,128)(2,1)} %bitcast.21, ...), custom_call_target="tpu_custom_call" | custom-call | flops 112742891520 | bytes 104857600 | tf_op jit(solution)/shard_map/gradients/pallas_call | solution.py:1049
  268.9 130.6 %step_and_gather.1 = (bf16[8,16,2,3,48,128]{5,4,3,2,1,0:T(8,128)(2,1)S(1)}, bf16[4,32,2,3,48,128]{5,4,3,2,1,0:T(8,128)(2,1)S(1)}, bf16[4,32,2,3,48,128]{5,4,3,2,...) custom-call(f32[2,3,3,48,128]{4,3,2,1,0:T(8,128)} %get-tuple-element, ...), custom_call_target="tpu_custom_call" | custom-call | tf_op jit(solution)/shard_map/step_and_gather/pallas_call | solution.py:644
  399.4 13.1 %unpack.1 = (bf16[2,896,2560]{2,1,0:T(8,128)(2,1)}, bf16[2,896,2560]{2,1,0:T(8,128)(2,1)}, bf16[2,2560,896]{2,1,0:T(8,128)(2,1)}, f32[7,2,2560]{2,1,0:T(2,128)},...) custom-call(bf16[8,16,2,3,48,128]{5,4,3,2,1,0:T(8,128)(2,1)S(1)} %ge, ...), custom_call_target="tpu_custom_call" | custom-call | tf_op jit(solution)/shard_map/unpack/pallas_call | solution.py:715

commit v9 on v8

--- a/solution.py
+++ b/solution.py
@@ -7,7 +7,7 @@
 
 F32, BF16 = jnp.float32, jnp.bfloat16
 MESH = pl.DeviceIdType.MESH
-RATE, LATENCY = 46.6e3, 2.3
+RATE, LATENCY, SLACK = 46.6e3, 2.9, 0.6
 TURN, ADD, HOP = 0.1, 2.0e6, 0.7
 WAYS = (1, -1)
 TRIO = range(3)
@@ -86,7 +86,7 @@
                 link, size, extra = copies[c]
                 start = max(now, links.get(link, 0.0))
                 links[link] = start + size / RATE
-                end = links[link] + LATENCY + extra
+                end = links[link] + LATENCY + SLACK + extra
             for b in by_need.get(c, ()):
                 waiting[b].discard(c)
                 arrived[b] = max(arrived.get(b, 0.0), end)
@@ -743,7 +743,7 @@
 SIDE_STRIDE, DOWN_STRIDE = D + GAP, FF // HALVES + GAP
 DOWN_BASE = RING_TILES * SIDE_STRIDE
 X_ROWS = DOWN_BASE + D // LANES * DOWN_STRIDE
-COST = {"last": (3.5, 3.5), "first": (1.8, 3.5), "da": (2.5,), "norm": (0.45,)}
+COST = {"last": (3.6, 3.5), "first": (2.1, 3.5), "da": (2.5,), "norm": (0.45,)}
 PACK_DOWN = 0.4
 WHOLE = ((0,), (1, 2), (3, 4), (5, 6), (7, 8))
 CHUNKS = {1: 0, 3: 1, 4: 2}

time: 414 us -> 414 us (level)
  no operation moved by 1% of the time
where the time goes in v9:
time: 414 us; the launch traced here: 413 us
  Pallas kernels  412 us (100%)
    pallas_call x1, Pallas kernels, gradients(): pl.pallas_call(kernel, out_shape=[jax.ShapeDtypeStruct((LAYERS, 3, 3, CHU...  268 us
    pallas_call x1, Pallas kernels, step_and_gather(): pl.pallas_call(kernel, out_shape=[pltpu.MemorySpace.VMEM(s.shape, s.dtype...  131 us
    pallas_call x1, Pallas kernels, unpack(): pl.pallas_call(kernel, grid=(LAYERS, groups), out_shape=[jax.ShapeDtypeSt...  13.1 us

profile of v9, /device:TPU:8, one launch (start us, length us, event | category | flops | bytes accessed | tf_op | source)
XLA Modules:
  0.0 413.2 jit_solution(7170406259593204724)
XLA Ops:
  0.6 268.4 %gradients.1 = (f32[2,3,3,48,128]{4,3,2,1,0:T(8,128)}, bf16[10,2048,512]{2,1,0:T(8,128)(2,1)}, f32[20,2048,128]{2,1,0:T(8,128)}, f32[20,2048,128]{2,1,0:T(8,128)...) custom-call(bf16[2048,896]{1,0:T(8,128)(2,1)} %bitcast.20, bf16[2048,896]{1,0:T(8,128)(2,1)} %bitcast.21, ...), custom_call_target="tpu_custom_call" | custom-call | flops 112742891520 | bytes 104857600 | tf_op jit(solution)/shard_map/gradients/pallas_call | solution.py:1049
  269.0 130.9 %step_and_gather.1 = (bf16[8,16,2,3,48,128]{5,4,3,2,1,0:T(8,128)(2,1)S(1)}, bf16[4,32,2,3,48,128]{5,4,3,2,1,0:T(8,128)(2,1)S(1)}, bf16[4,32,2,3,48,128]{5,4,3,2,...) custom-call(f32[2,3,3,48,128]{4,3,2,1,0:T(8,128)} %get-tuple-element, ...), custom_call_target="tpu_custom_call" | custom-call | tf_op jit(solution)/shard_map/step_and_gather/pallas_call | solution.py:644
  400.0 13.1 %unpack.1 = (bf16[2,896,2560]{2,1,0:T(8,128)(2,1)}, bf16[2,896,2560]{2,1,0:T(8,128)(2,1)}, bf16[2,2560,896]{2,1,0:T(8,128)(2,1)}, f32[7,2,2560]{2,1,0:T(2,128)},...) custom-call(bf16[8,16,2,3,48,128]{5,4,3,2,1,0:T(8,128)(2,1)S(1)} %ge, ...), custom_call_target="tpu_custom_call" | custom-call | tf_op jit(solution)/shard_map/unpack/pallas_call | solution.py:715
